TPU v7x, 512 devices: a whole 4x8x8 slice. The times are simulated.
512 devices in a mesh: heads: 8 (over y_lo, x), blk: 64 (over y_hi, z, core).
Axes of the slice: x: 4, y: 8 (y_hi: 4, y_lo: 2; y = y_hi * 2 + y_lo), z: 8, core: 2. Of those that a mesh axis runs over, the one named last changes fastest.
Arguments:
- queries: bfloat16 [4096, 64, 128], P('blk', 'heads'), may hold values from -8 to 8
- prefix_keys: bfloat16 [8, 131072, 128], P('heads', 'blk'), may hold values from -8 to 8
- cached_prefix_values: bfloat16 [8, 131072, 128], P('heads', 'blk'), may hold values from -6 to 6
- shard_len: int32 [64], replicated, may hold values from 512 to 2048
- reach: int32 [64], replicated, may hold values from 4096 to 8192
- w_out: bfloat16 [8192, 16384], P('heads', 'blk'), may hold values from -0.0625 to 0.0625
Outputs:
- projected: bfloat16 [4096, 16384], P('heads', 'blk')
All inputs are finite; a program needn't handle non-finite values.
Results may differ from a plain program's by a relative error of at most 0.0056.
Values may be sent and summed in bfloat16 or wider, within the bound.
No kernel may reach another device: no remote copies, remote signals or barrier semaphores. Data moves between devices by JAX's collectives and lax.ppermute only.
A program may use at most 64 MiB of HBM per device.

v0:
```python
import jax
import jax.numpy as jnp
from jax import lax
from jax.sharding import Mesh
from jax.sharding import PartitionSpec as P

SPAN = 4
HEADS = ("heads_0", "heads_1")


masked_score = -1e30


def passed_along(value, axis, steps):
    count = lax.axis_size(axis)
    pairs = [(source, (source + steps) % count) for source in range(count)]
    return lax.ppermute(value, axis, pairs)


def split_up(value, dim, length):
    lengths = value.shape
    blocks = value.reshape(*lengths[:dim], length, lengths[dim] // length, *lengths[dim + 1 :])
    return jnp.moveaxis(blocks, dim, 0)


def joined_along(blocks, dim):
    lengths = list(blocks.shape[1:])
    lengths[dim] *= blocks.shape[0]
    return jnp.moveaxis(blocks, 0, dim).reshape(lengths)


def exchange_in_order(blocks, axes, turns):
    lengths = [lax.axis_size(a) for a in axes]
    blocks = blocks.reshape(*lengths, *blocks.shape[1:])
    for k in turns:
        blocks = lax.all_to_all(blocks, axes[k], split_axis=k, concat_axis=k, tiled=True)
    return blocks.reshape(-1, *blocks.shape[len(axes) :])


def stepwise_exchange(value, axes, turns, split_dim, concat_dim):
    blocks = split_up(value, split_dim, lax.axis_size(axes))
    return joined_along(exchange_in_order(blocks, axes, turns), concat_dim)


def part_stats(query_tile_rows, key_block, value_block, visible):
    head_size = query_tile_rows.shape[-1]
    scores = jnp.einsum(
        "thgd,hnd->thgn", query_tile_rows, key_block, preferred_element_type=jnp.float32
    ) * head_size ** (-0.5)
    visible_grid = visible[:, None, None, :]
    maxima = jnp.max(jnp.where(visible_grid, scores, masked_score), axis=-1)
    weights = jnp.where(visible_grid, jnp.exp(scores - maxima[..., None]), 0.0)
    totals = jnp.sum(weights, axis=-1)
    weighted = jnp.einsum(
        "thgn,hnd->thgd",
        weights.astype(jnp.bfloat16),
        value_block,
        preferred_element_type=jnp.float32,
    )
    return (maxima, totals, weighted)


def combine_parts(first, second):
    joined = jnp.maximum(first[0], second[0])
    first_factor = jnp.exp(first[0] - joined)
    second_factor = jnp.exp(second[0] - joined)
    totals = first[1] * first_factor + second[1] * second_factor
    weighted = first[2] * first_factor[..., None] + second[2] * second_factor[..., None]
    return (joined, totals, weighted)


def on_device(queries, prefix_keys, cached_prefix_values, shard_len, reach, w_out):
    shard_count = lax.axis_size("blk")
    group_count = lax.axis_size(HEADS)
    own_index = lax.axis_index("blk")
    query_len = queries.shape[0]
    heads_local = queries.shape[1]
    head_size = queries.shape[2]
    kv_local = prefix_keys.shape[0]
    keys_len = prefix_keys.shape[1]
    columns = w_out.shape[1]
    full_weight = lax.all_gather(w_out, HEADS, axis=0, tiled=True)
    local_queries = queries.reshape(query_len, kv_local, heads_local // kv_local, head_size)
    row_ids = jnp.arange(query_len, dtype=jnp.int32)[:, None]
    slot_ids = jnp.arange(keys_len, dtype=jnp.int32)[None, :]

    def mask_for(block_id, shard_id, offset):
        return (slot_ids < shard_len[shard_id]) & (
            offset * keys_len + slot_ids < reach[block_id] + row_ids
        )

    running = part_stats(
        local_queries, prefix_keys, cached_prefix_values, mask_for(own_index, own_index, 0)
    )
    for offset in range(1, SPAN):
        visitor = passed_along(local_queries, "blk", offset)
        owner_id = (own_index - offset + shard_count) % shard_count
        maxima, totals, weighted = part_stats(
            visitor, prefix_keys, cached_prefix_values, mask_for(owner_id, own_index, offset)
        )
        returned = passed_along((maxima, totals, weighted), "blk", -offset)
        running = combine_parts(running, returned)
    attended = (
        (running[2] / running[1][..., None])
        .astype(jnp.bfloat16)
        .reshape(query_len, heads_local * head_size)
    )
    share_rows = stepwise_exchange(attended, HEADS, (0, 1), 0, 1)
    strided = jnp.dot(
        lax.all_gather(share_rows, "blk", axis=0, tiled=True),
        full_weight,
        preferred_element_type=jnp.float32,
    ).astype(jnp.bfloat16)
    share_len = share_rows.shape[0]
    grouped = strided.reshape(group_count, shard_count // group_count, 1, share_len, columns)
    ordered = lax.all_to_all(grouped, HEADS, split_axis=0, concat_axis=2, tiled=True)
    return ordered.reshape(shard_count // group_count * group_count * share_len, columns)


def solution(mesh):
    finer = Mesh(mesh.devices.reshape(2, 4, mesh.shape["blk"]), ("heads_0", "heads_1", "blk"))
    placed = (
        P("blk", HEADS, None),
        P(HEADS, "blk", None),
        P(HEADS, "blk", None),
        P(),
        P(),
        P(HEADS, "blk"),
    )
    return jax.shard_map(
        on_device, mesh=finer, in_specs=placed, out_specs=P(HEADS, "blk"), check_vma=False
    )
```

profile of v0, /device:TPU:16, one launch (start us, length us, event | category | flops | bytes accessed | tf_op | source)
XLA Modules:
  0.0 239.9 jit_solution(17325042349350337519)
XLA Ops:
  6.5 0.7 all-gather.5.cloned.1.call-update
  7.3 0.0 all-gather.3.cloned.1.call-start
  7.3 0.9 copy.53
  8.2 3.7 %collective-permute-start.6 = (bf16[64,1,8,128]{3,0,2,1:T(8,128)(2,1)S(1)}, bf16[64,1,8,128]{3,0,2,1:T(8,128)(2,1)S(1)}, u32[]{:S(2)}, u32[]{:S(2)}) collective-permute-start(bf16[64,1,8,128]{3,0,2,1:T(8,128)(2,1)S(1)} %bitcast.279), channel_id=1, source_target_pairs={{0,3},{1,4},{2,5},{3,6},{4,7},{5,8},{6,9},{7,10},{8,11},{9,12},{10... | collective-permute-start | bytes 393224 | tf_op jit(solution)/shard_map/ppermute | solution.py:17
  12.0 4.3 %collective-permute-start.3 = (bf16[64,1,8,128]{3,0,2,1:T(8,128)(2,1)S(1)}, bf16[64,1,8,128]{3,0,2,1:T(8,128)(2,1)S(1)}, u32[]{:S(2)}, u32[]{:S(2)}) collective-permute-start(bf16[64,1,8,128]{3,0,2,1:T(8,128)(2,1)S(1)} %bitcast.280), channel_id=1, source_target_pairs={{0,2},{1,3},{2,4},{3,5},{4,6},{5,7},{6,8},{7,9},{8,10},{9,11},{10,... | collective-permute-start | bytes 393224 | tf_op jit(solution)/shard_map/ppermute | solution.py:17
  16.2 4.1 %collective-permute-start = (bf16[64,1,8,128]{3,0,2,1:T(8,128)(2,1)S(1)}, bf16[64,1,8,128]{3,0,2,1:T(8,128)(2,1)S(1)}, u32[]{:S(2)}, u32[]{:S(2)}) collective-permute-start(bf16[64,1,8,128]{3,0,2,1:T(8,128)(2,1)S(1)} %bitcast.281), channel_id=1, source_target_pairs={{0,1},{1,2},{2,3},{3,4},{4,5},{5,6},{6,7},{7,8},{8,9},{9,10},{10,1... | collective-permute-start | bytes 393224 | tf_op jit(solution)/shard_map/ppermute | solution.py:17
  20.4 1.3 dynamic_slice.18
  21.7 1.5 fusion.99
  23.2 1.2 iota_add_fusion.5
  24.4 1.3 iota_add_fusion.3
  25.7 0.7 iota_compare_fusion.1
  26.5 0.4 fusion.60
  26.9 1.8 fusion.9
  28.7 2.2 collective-permute-done
  31.0 0.9 fusion.6
  31.9 1.1 fusion.14
  33.0 2.2 collective-permute-start.9
  35.2 2.1 collective-permute-start.1
  37.4 0.0 collective-permute-done.3
  37.4 0.9 fusion.3
  38.3 1.1 fusion.16
  39.4 3.9 %collective-permute-start.10 = (f32[64,1,8]{0,2,1:T(8,128)S(1)}, f32[64,1,8]{0,2,1:T(8,128)S(1)}, u32[]{:S(2)}, u32[]{:S(2)}) collective-permute-start(f32[64,1,8]{0,2,1:T(8,128)S(1)} %bitcast.286), channel_id=1, source_target_pairs={{0,62},{1,63},{2,0},{3,1},{4,2},{5,3},{6,4},{7,5},{8,6},{9,7},{10,... | collective-permute-start | bytes 6152 | tf_op jit(solution)/shard_map/ppermute | solution.py:17
  43.3 3.5 %collective-permute-start.4 = (f32[64,1,8]{0,2,1:T(8,128)S(1)}, f32[64,1,8]{0,2,1:T(8,128)S(1)}, u32[]{:S(2)}, u32[]{:S(2)}) collective-permute-start(f32[64,1,8]{0,2,1:T(8,128)S(1)} %bitcast.283), channel_id=1, source_target_pairs={{0,62},{1,63},{2,0},{3,1},{4,2},{5,3},{6,4},{7,5},{8,6},{9,7},{10,... | collective-permute-start | bytes 6152 | tf_op jit(solution)/shard_map/ppermute | solution.py:17
  46.8 0.0 collective-permute-done.6
  46.8 0.9 fusion
  47.8 0.9 fusion.42
  48.7 0.9 fusion.39
  49.6 0.9 fusion.36
  50.4 1.1 fusion.18
  51.6 2.9 %collective-permute-start.2 = (f32[64,1,8,128]{3,0,2,1:T(8,128)S(1)}, f32[64,1,8,128]{3,0,2,1:T(8,128)S(1)}, u32[]{:S(2)}, u32[]{:S(2)}) collective-permute-start(f32[64,1,8,128]{3,0,2,1:T(8,128)S(1)} %fusion.42), channel_id=1, source_target_pairs={{0,63},{1,0},{2,1},{3,2},{4,3},{5,4},{6,5},{7,6},{8,7},{9,8},{10,9... | collective-permute-start | bytes 786440 | tf_op jit(solution)/shard_map/ppermute | solution.py:17
  54.5 3.7 %collective-permute-start.5 = (f32[64,1,8,128]{3,0,2,1:T(8,128)S(1)}, f32[64,1,8,128]{3,0,2,1:T(8,128)S(1)}, u32[]{:S(2)}, u32[]{:S(2)}) collective-permute-start(f32[64,1,8,128]{3,0,2,1:T(8,128)S(1)} %fusion.39), channel_id=1, source_target_pairs={{0,62},{1,63},{2,0},{3,1},{4,2},{5,3},{6,4},{7,5},{8,6},{9,7},{10,... | collective-permute-start | bytes 786440 | tf_op jit(solution)/shard_map/ppermute | solution.py:17
  58.2 2.4 %collective-permute-start.11 = (f32[64,1,8]{0,2,1:T(8,128)S(1)}, f32[64,1,8]{0,2,1:T(8,128)S(1)}, u32[]{:S(2)}, u32[]{:S(2)}) collective-permute-start(f32[64,1,8]{0,2,1:T(8,128)S(1)} %bitcast.287), channel_id=1, source_target_pairs={{0,61},{1,62},{2,63},{3,0},{4,1},{5,2},{6,3},{7,4},{8,5},{9,6},{10... | collective-permute-start | bytes 6152 | tf_op jit(solution)/shard_map/ppermute | solution.py:17
  60.6 2.4 collective-permute-start.7
  63.0 7.1 %collective-permute-start.8 = (f32[64,1,8,128]{3,0,2,1:T(8,128)S(1)}, f32[64,1,8,128]{3,0,2,1:T(8,128)S(1)}, u32[]{:S(2)}, u32[]{:S(2)}) collective-permute-start(f32[64,1,8,128]{3,0,2,1:T(8,128)S(1)} %fusion.36), channel_id=1, source_target_pairs={{0,61},{1,62},{2,63},{3,0},{4,1},{5,2},{6,3},{7,4},{8,5},{9,6},{10... | collective-permute-start | bytes 786440 | tf_op jit(solution)/shard_map/ppermute | solution.py:17
  70.1 1.1 fusion.12
  71.3 8.1 %collective-permute-done.8 = f32[64,1,8,128]{3,0,2,1:T(8,128)S(1)} collective-permute-done((f32[64,1,8,128]{3,0,2,1:T(8,128)S(1)}, f32[64,1,8,128]{3,0,2,1:T(8,128)S(1)}, u32[]{:S(2)}, u32[]{:S(2)}) %collective-permute-start.8) | collective-permute-done | bytes 262176 | tf_op jit(solution)/shard_map/ppermute | solution.py:17
  79.3 1.4 fusion.66
  80.7 0.1 copy.43
  80.8 0.1 reshape_reshape_reshape.3
  80.9 23.8 %all_to_all.25 = bf16[2,4,8,1024]{3,2,1,0:T(8,128)(2,1)S(1)} all-to-all(bf16[2,4,8,1024]{3,2,1,0:T(8,128)(2,1)S(1)} %reshape_reshape_reshape.3), channel_id=1, replica_groups=mesh['heads_0'=2,'heads_1'=4,'blk'=64] {'heads_0'}, dimensions={0} | all-to-all | bytes 262144 | tf_op jit(solution)/shard_map/all_to_all | solution.py:36
  104.7 9.7 %all_to_all.26 = bf16[2,4,8,1024]{3,2,0,1:T(8,128)(2,1)S(1)} all-to-all(bf16[2,4,8,1024]{3,2,0,1:T(8,128)(2,1)S(1)} %copy.44), channel_id=1, replica_groups=mesh['heads_0'=2,'heads_1'=4,'blk'=64] {'heads_1'}, dimensions={1} | all-to-all | bytes 262144 | tf_op jit(solution)/shard_map/all_to_all | solution.py:36
  114.4 0.7 copy.45
  115.0 0.0 all-gather.3.cloned.1.call-update
  115.1 0.0 all-gather.5.cloned.1.call-done
  115.1 95.9 %all-gather.3.cloned.1.call-done = bf16[512,8192]{1,0:T(8,128)(2,1)} async-done(((bf16[8,8192]{1,0:T(8,128)(2,1)}), bf16[512,8192]{1,0:T(8,128)(2,1)}) %all-gather.3.cloned.1.call-update) | async-done | bytes 8388624 | tf_op jit(solution)/shard_map/all_gather | solution.py:110
  211.0 6.9 %convolution_convert_fusion = bf16[512,256]{1,0:T(8,128)(2,1)S(1)} fusion(bf16[512,8192]{1,0:T(8,128)(2,1)} %all-gather.3.cloned.1.call-done, bf16[8192,256]{1,0:T(8,128)(2,1)} %all-gather.5.cloned.1.call-done), kind=kOutput, calls=%fused_computation.40 | convolution fusion | flops 2147614720 | bytes 12845056 | tf_op jit(solution)/shard_map/dot_general | solution.py:109
  217.9 14.4 %all_to_all.27 = bf16[8,8,1,8,256]{4,3,1,2,0:T(8,128)(2,1)S(1)} all-to-all(bf16[8,8,1,8,256]{4,3,1,2,0:T(8,128)(2,1)S(1)} %bitcast.278), channel_id=1, replica_groups=mesh['heads_0'=2,'heads_1'=4,'blk'=64] {'heads_0','heads_1'}, dimensions={0} | all-to-all | bytes 524288 | tf_op jit(solution)/shard_map/all_to_all | solution.py:116
  232.3 0.7 copy.47
  (17 shorter events, 0.1 us)
Async XLA Ops:
  6.5 20.4 %copy-start = (bf16[1,2048,128]{2,1,0:T(8,128)(2,1)S(1)}, bf16[1,2048,128]{2,1,0:T(8,128)(2,1)}, u32[]{:S(2)}) copy-start(bf16[1,2048,128]{2,1,0:T(8,128)(2,1)} %param.7) | copy-start | bytes 1572868
  6.5 108.6 %all-gather.5.cloned.1.call-start = ((), (), s32[]{:S(2)}) async-start(), calls=%async_computation.4 | async-start | bytes 4718592 | tf_op jit(solution)/shard_map/all_gather | solution.py:82
  7.3 203.8 %all-gather.3.cloned.1.call-start = ((), (), s32[]{:S(2)}) async-start(), calls=%async_computation.3 | async-start | bytes 8519680 | tf_op jit(solution)/shard_map/all_gather | solution.py:110
  8.2 38.6 %collective-permute-start.6 = (bf16[64,1,8,128]{3,0,2,1:T(8,128)(2,1)S(1)}, bf16[64,1,8,128]{3,0,2,1:T(8,128)(2,1)S(1)}, u32[]{:S(2)}, u32[]{:S(2)}) collective-permute-start(bf16[64,1,8,128]{3,0,2,1:T(8,128)(2,1)S(1)} %bitcast.279), channel_id=1, source_target_pairs={{0,3},{1,4},{2,5},{3,6},{4,7},{5,8},{6,9},{7,10},{8,11},{9,12},{10... | collective-permute-start | bytes 393224 | tf_op jit(solution)/shard_map/ppermute | solution.py:17
  12.0 25.4 %collective-permute-start.3 = (bf16[64,1,8,128]{3,0,2,1:T(8,128)(2,1)S(1)}, bf16[64,1,8,128]{3,0,2,1:T(8,128)(2,1)S(1)}, u32[]{:S(2)}, u32[]{:S(2)}) collective-permute-start(bf16[64,1,8,128]{3,0,2,1:T(8,128)(2,1)S(1)} %bitcast.280), channel_id=1, source_target_pairs={{0,2},{1,3},{2,4},{3,5},{4,6},{5,7},{6,8},{7,9},{8,10},{9,11},{10,... | collective-permute-start | bytes 393224 | tf_op jit(solution)/shard_map/ppermute | solution.py:17
  16.2 14.7 %collective-permute-start = (bf16[64,1,8,128]{3,0,2,1:T(8,128)(2,1)S(1)}, bf16[64,1,8,128]{3,0,2,1:T(8,128)(2,1)S(1)}, u32[]{:S(2)}, u32[]{:S(2)}) collective-permute-start(bf16[64,1,8,128]{3,0,2,1:T(8,128)(2,1)S(1)} %bitcast.281), channel_id=1, source_target_pairs={{0,1},{1,2},{2,3},{3,4},{4,5},{5,6},{6,7},{7,8},{8,9},{9,10},{10,1... | collective-permute-start | bytes 393224 | tf_op jit(solution)/shard_map/ppermute | solution.py:17
  33.0 21.5 %collective-permute-start.9 = (f32[64,1,8]{0,2,1:T(8,128)S(1)}, f32[64,1,8]{0,2,1:T(8,128)S(1)}, u32[]{:S(2)}, u32[]{:S(2)}) collective-permute-start(f32[64,1,8]{0,2,1:T(8,128)S(1)} %bitcast.285), channel_id=1, source_target_pairs={{0,63},{1,0},{2,1},{3,2},{4,3},{5,4},{6,5},{7,6},{8,7},{9,8},{10,9... | collective-permute-start | bytes 6152 | tf_op jit(solution)/shard_map/ppermute | solution.py:17
  35.2 22.9 %collective-permute-start.1 = (f32[64,1,8]{0,2,1:T(8,128)S(1)}, f32[64,1,8]{0,2,1:T(8,128)S(1)}, u32[]{:S(2)}, u32[]{:S(2)}) collective-permute-start(f32[64,1,8]{0,2,1:T(8,128)S(1)} %bitcast.282), channel_id=1, source_target_pairs={{0,63},{1,0},{2,1},{3,2},{4,3},{5,4},{6,5},{7,6},{8,7},{9,8},{10,9... | collective-permute-start | bytes 6152 | tf_op jit(solution)/shard_map/ppermute | solution.py:17
  39.4 8.3 %copy-start.1 = (bf16[1,2048,128]{2,1,0:T(8,128)(2,1)S(1)}, bf16[1,2048,128]{2,1,0:T(8,128)(2,1)}, u32[]{:S(2)}) copy-start(bf16[1,2048,128]{2,1,0:T(8,128)(2,1)} %param.8) | copy-start | bytes 1572868
  39.4 21.2 %collective-permute-start.10 = (f32[64,1,8]{0,2,1:T(8,128)S(1)}, f32[64,1,8]{0,2,1:T(8,128)S(1)}, u32[]{:S(2)}, u32[]{:S(2)}) collective-permute-start(f32[64,1,8]{0,2,1:T(8,128)S(1)} %bitcast.286), channel_id=1, source_target_pairs={{0,62},{1,63},{2,0},{3,1},{4,2},{5,3},{6,4},{7,5},{8,6},{9,7},{10,... | collective-permute-start | bytes 6152 | tf_op jit(solution)/shard_map/ppermute | solution.py:17
  43.3 19.7 %collective-permute-start.4 = (f32[64,1,8]{0,2,1:T(8,128)S(1)}, f32[64,1,8]{0,2,1:T(8,128)S(1)}, u32[]{:S(2)}, u32[]{:S(2)}) collective-permute-start(f32[64,1,8]{0,2,1:T(8,128)S(1)} %bitcast.283), channel_id=1, source_target_pairs={{0,62},{1,63},{2,0},{3,1},{4,2},{5,3},{6,4},{7,5},{8,6},{9,7},{10,... | collective-permute-start | bytes 6152 | tf_op jit(solution)/shard_map/ppermute | solution.py:17
  51.6 19.7 %collective-permute-start.2 = (f32[64,1,8,128]{3,0,2,1:T(8,128)S(1)}, f32[64,1,8,128]{3,0,2,1:T(8,128)S(1)}, u32[]{:S(2)}, u32[]{:S(2)}) collective-permute-start(f32[64,1,8,128]{3,0,2,1:T(8,128)S(1)} %fusion.42), channel_id=1, source_target_pairs={{0,63},{1,0},{2,1},{3,2},{4,3},{5,4},{6,5},{7,6},{8,7},{9,8},{10,9... | collective-permute-start | bytes 786440 | tf_op jit(solution)/shard_map/ppermute | solution.py:17
  54.5 16.8 %collective-permute-start.5 = (f32[64,1,8,128]{3,0,2,1:T(8,128)S(1)}, f32[64,1,8,128]{3,0,2,1:T(8,128)S(1)}, u32[]{:S(2)}, u32[]{:S(2)}) collective-permute-start(f32[64,1,8,128]{3,0,2,1:T(8,128)S(1)} %fusion.39), channel_id=1, source_target_pairs={{0,62},{1,63},{2,0},{3,1},{4,2},{5,3},{6,4},{7,5},{8,6},{9,7},{10,... | collective-permute-start | bytes 786440 | tf_op jit(solution)/shard_map/ppermute | solution.py:17
  58.2 13.0 %collective-permute-start.11 = (f32[64,1,8]{0,2,1:T(8,128)S(1)}, f32[64,1,8]{0,2,1:T(8,128)S(1)}, u32[]{:S(2)}, u32[]{:S(2)}) collective-permute-start(f32[64,1,8]{0,2,1:T(8,128)S(1)} %bitcast.287), channel_id=1, source_target_pairs={{0,61},{1,62},{2,63},{3,0},{4,1},{5,2},{6,3},{7,4},{8,5},{9,6},{10... | collective-permute-start | bytes 6152 | tf_op jit(solution)/shard_map/ppermute | solution.py:17
  60.6 10.6 %collective-permute-start.7 = (f32[64,1,8]{0,2,1:T(8,128)S(1)}, f32[64,1,8]{0,2,1:T(8,128)S(1)}, u32[]{:S(2)}, u32[]{:S(2)}) collective-permute-start(f32[64,1,8]{0,2,1:T(8,128)S(1)} %bitcast.284), channel_id=1, source_target_pairs={{0,61},{1,62},{2,63},{3,0},{4,1},{5,2},{6,3},{7,4},{8,5},{9,6},{10... | collective-permute-start | bytes 6152 | tf_op jit(solution)/shard_map/ppermute | solution.py:17
  63.0 16.4 %collective-permute-start.8 = (f32[64,1,8,128]{3,0,2,1:T(8,128)S(1)}, f32[64,1,8,128]{3,0,2,1:T(8,128)S(1)}, u32[]{:S(2)}, u32[]{:S(2)}) collective-permute-start(f32[64,1,8,128]{3,0,2,1:T(8,128)S(1)} %fusion.36), channel_id=1, source_target_pairs={{0,61},{1,62},{2,63},{3,0},{4,1},{5,2},{6,3},{7,4},{8,5},{9,6},{10... | collective-permute-start | bytes 786440 | tf_op jit(solution)/shard_map/ppermute | solution.py:17
Sparse Core Ops, SparseCore 0:
  9.4 88.5 all-gather.4
  115.2 95.7 all-gather.2
where the time goes:
time: 241 us; the launch traced here: 240 us
  waiting for transfers between devices  107 us (44%)
  blocking collectives  47.9 us (20%)
  starting transfers between devices  42.3 us (18%)
  matrix products  15.5 us (6%)
  between operations  13.7 us (6%)
  other arithmetic  8.18 us (3%)
  local copies, waits for them, and re-layouts  5.26 us (2%)
    all_gather x1, waiting for transfers between devices, on_device(): lax.all_gather(share_rows, 'blk', axis=0, tiled=True)  95.9 us
    ppermute x12, starting transfers between devices, passed_along(): return lax.ppermute(value, axis, pairs)  42.3 us
    all_to_all x2, blocking collectives, exchange_in_order(): lax.all_to_all(blocks, axes[k], split_axis=k, concat_axis=k, tiled=True)  33.5 us
    all_to_all x1, blocking collectives, on_device(): lax.all_to_all(grouped, HEADS, split_axis=0, concat_axis=2, tiled=True)  14.4 us
    ppermute x12, waiting for transfers between devices, passed_along(): return lax.ppermute(value, axis, pairs)  10.3 us
    dot_general x1, matrix products, on_device(): jnp.dot(lax.all_gather(share_rows, 'blk', axis=0, tiled=True), full_weigh...  6.9 us
  transfers between devices with their start and end apart: 14, of which 3 were waited for; matrix products, arithmetic and copies ran while one was open for 9% of the time, Pallas kernels for 0%

commit v1 on v0

v1 whole, which is shorter than its diff:
```python
import functools
import math

import jax
import jax.numpy as jnp
from jax import lax
from jax.experimental import pallas as pl
from jax.experimental.pallas import tpu as pltpu
from jax.sharding import Mesh
from jax.sharding import PartitionSpec as P

SPAN = 4
HEADS = ("y", "x")
BLK = ("Y", "Z", "K")
TILE = 128
NONE = -1e30
F32 = jnp.float32
BF16 = jnp.bfloat16


def eye_mask():
    rows = lax.broadcasted_iota(jnp.int32, (TILE, TILE), 0)
    lanes = lax.broadcasted_iota(jnp.int32, (TILE, TILE), 1)
    return rows == lanes


def attend_kernel(tokens, offset, lengths, reaches, q_ref, k_ref, v_ref, out_ref):
    rows, head_size = q_ref.shape
    count = lengths.shape[0]
    own_index = lax.axis_index(BLK)
    length = lengths[own_index]
    base = reaches[lax.rem(own_index + (count - offset), count)] - offset * k_ref.shape[0]
    scale = head_size**-0.5 * math.log2(math.e)
    eye = eye_mask()
    stats = []
    for start in range(0, rows, TILE):
        scores = lax.dot_general(
            q_ref[start : start + TILE, :],
            k_ref[...],
            (((1,), (1,)), ((), ())),
            preferred_element_type=F32,
        )
        row = start + lax.broadcasted_iota(jnp.int32, (TILE, 1), 0)
        limit = jnp.minimum(length, base + lax.rem(row, tokens))
        slot = lax.broadcasted_iota(jnp.int32, scores.shape, 1)
        scores = jnp.where(slot < limit, scores, NONE)
        top = jnp.max(scores, axis=1, keepdims=True)
        weights = jnp.exp2((scores - top) * scale)
        total = jnp.sum(weights, axis=1, keepdims=True)
        values = jnp.dot(weights.astype(BF16), v_ref[...], preferred_element_type=F32)
        seen = top > 0.1 * NONE
        out_ref[start : start + TILE, :] = jnp.where(seen, values / total, 0.0).astype(BF16)
        level = jnp.where(seen, top * scale + jnp.log2(total), NONE)
        spread = jnp.where(eye, jnp.broadcast_to(level, (TILE, TILE)), 0.0)
        stats.append(jnp.sum(spread, axis=0, keepdims=True))
    level = jnp.concatenate(stats, axis=0)
    high = level.astype(BF16).astype(F32)
    middle = (level - high).astype(BF16).astype(F32)
    low = level - high - middle
    out_ref[rows:, :] = jnp.concatenate(
        [high, middle, low, jnp.zeros_like(low)], axis=0
    ).astype(BF16)


def attend(tokens, offset, lengths, reaches, q, k, v):
    rows, head_size = q.shape
    slots = k.shape[0]
    extra = 4 * (rows // TILE)
    vmem = pl.BlockSpec(memory_space=pltpu.VMEM)
    return pl.pallas_call(
        functools.partial(attend_kernel, tokens, offset),
        out_shape=jax.ShapeDtypeStruct((rows + extra, head_size), BF16),
        in_specs=[pl.BlockSpec(memory_space=pltpu.SMEM)] * 2 + [vmem] * 3,
        out_specs=vmem,
        compiler_params=pltpu.CompilerParams(vmem_limit_bytes=24 << 20),
        cost_estimate=pl.CostEstimate(
            flops=4 * rows * slots * head_size,
            bytes_accessed=4 * slots * head_size,
            transcendentals=rows * slots,
        ),
        name="attend",
    )(lengths, reaches, q, k, v)


def combine_kernel(*refs):
    parts, out_ref = refs[:-1], refs[-1]
    copies, tokens, _ = out_ref.shape
    head_size = parts[0].shape[1]
    groups = parts[0].shape[0] // (TILE + 4)
    rows = groups * TILE
    levels = []
    for part in parts:
        terms = part[rows:, :].astype(F32)
        levels.append(
            terms[:groups] + terms[groups : 2 * groups] + terms[2 * groups : 3 * groups]
        )
    top = functools.reduce(jnp.maximum, levels)
    factors = [jnp.exp2(level - top) for level in levels]
    inverse = 1.0 / functools.reduce(jnp.add, factors)
    eye = eye_mask()
    per_tile = TILE // tokens
    for group in range(groups):
        total = None
        for part, factor in zip(parts, factors):
            line = jnp.broadcast_to((factor * inverse)[group : group + 1, :], (TILE, TILE))
            column = jnp.sum(jnp.where(eye, line, 0.0), axis=1, keepdims=True)
            term = part[group * TILE : (group + 1) * TILE, :].astype(F32) * column
            total = term if total is None else total + term
        total = total.astype(BF16)
        for i in range(per_tile):
            head = group * per_tile + i
            piece = total[i * tokens : (i + 1) * tokens]
            for copy in range(copies):
                out_ref[copy, :, head * head_size : (head + 1) * head_size] = piece


def combine(parts, copies, tokens, heads):
    head_size = parts[0].shape[1]
    vmem = pl.BlockSpec(memory_space=pltpu.VMEM)
    return pl.pallas_call(
        combine_kernel,
        out_shape=jax.ShapeDtypeStruct((copies, tokens, heads * head_size), BF16),
        in_specs=[vmem] * len(parts),
        out_specs=vmem,
        compiler_params=pltpu.CompilerParams(vmem_limit_bytes=8 << 20),
        cost_estimate=pl.CostEstimate(
            flops=1 << 20, bytes_accessed=1 << 20, transcendentals=0
        ),
        name="combine",
    )(*parts)


def project_kernel(own_ref, other_ref, w0, w1, w2, w3a, w3b, out_ref):
    columns = w0.shape[1]
    half = w3a.shape[0]
    lhs = jnp.concatenate([own_ref[0], other_ref[0]], axis=0)
    for i, w in enumerate((w0, w1, w2)):
        out_ref[0, :, i * columns : (i + 1) * columns] = jnp.dot(
            lhs, w[...], preferred_element_type=F32
        ).astype(BF16)
    last = jnp.dot(lhs[:, :half], w3a[...], preferred_element_type=F32)
    last += jnp.dot(lhs[:, half:], w3b[...], preferred_element_type=F32)
    out_ref[0, :, 3 * columns :] = last.astype(BF16)


def project(own, other, pieces):
    groups, rows, depth = own.shape
    columns = pieces[0].shape[1]
    whole = lambda w: pl.BlockSpec(w.shape, lambda i: (0, 0))
    side = pl.BlockSpec((1, rows, depth), lambda i: (i, 0, 0))
    return pl.pallas_call(
        project_kernel,
        grid=(groups,),
        out_shape=pltpu.HBM((groups, 2 * rows, 4 * columns), BF16),
        in_specs=[side, side] + [whole(w) for w in pieces],
        out_specs=pl.BlockSpec((1, 2 * rows, 4 * columns), lambda i: (i, 0, 0)),
        compiler_params=pltpu.CompilerParams(vmem_limit_bytes=24 << 20),
        cost_estimate=pl.CostEstimate(
            flops=16 * groups * rows * depth * columns,
            bytes_accessed=6 << 20,
            transcendentals=0,
        ),
        name="project",
    )(own, other, *pieces)


def total_kernel(place, in_ref, out_ref):
    half = out_ref.shape[1] // 2
    total = in_ref[0].astype(F32)
    for i in range(1, in_ref.shape[0]):
        total += in_ref[i].astype(F32)
    total = total.astype(BF16)
    core = place[4]
    out_ref[0, pl.ds(pl.multiple_of(core * half, half), half), :] = total[:half]
    out_ref[0, pl.ds(pl.multiple_of((1 - core) * half, half), half), :] = total[half:]


def totals(place, received, count):
    sources, rows, width = received.shape
    columns = width // count
    return pl.pallas_call(
        total_kernel,
        grid_spec=pltpu.PrefetchScalarGridSpec(
            num_scalar_prefetch=1,
            grid=(count,),
            in_specs=[pl.BlockSpec((sources, rows, columns), lambda i, place: (0, 0, i))],
            out_specs=pl.BlockSpec((1, rows, columns), lambda i, place: (place[i], 0, 0)),
        ),
        out_shape=jax.ShapeDtypeStruct((count, rows, columns), BF16),
        compiler_params=pltpu.CompilerParams(vmem_limit_bytes=16 << 20),
        cost_estimate=pl.CostEstimate(
            flops=sources * rows * width, bytes_accessed=3 << 20, transcendentals=0
        ),
        name="totals",
    )(place, received)


def passed_along(value, axis, steps):
    count = lax.axis_size(axis)
    return lax.ppermute(value, axis, [(i, (i + steps) % count) for i in range(count)])


def on_device(queries, prefix_keys, cached_prefix_values, shard_len, reach, w_out):
    shard_count = lax.axis_size(BLK)
    group_count = lax.axis_size(HEADS)
    y_count, z_count, k_count = (lax.axis_size(a) for a in BLK)
    tokens, heads, head_size = queries.shape
    depth, columns = w_out.shape
    per_group = shard_count // group_count
    keys = prefix_keys[0]
    values = cached_prefix_values[0]
    q_own = queries.transpose(1, 0, 2).reshape(heads * tokens, head_size)

    def home(block):
        slot = block % per_group
        return ((slot // k_count) * z_count + block // per_group) * k_count + slot % k_count

    visitors = [q_own]
    for j in range(1, SPAN):
        visitors.append(passed_along(q_own, BLK, j))
    half = depth // 2
    w_before = passed_along(w_out, "Y", 1)
    w_after = passed_along(w_out, "Y", -1)
    w_far_a = passed_along(w_before[:half], "Y", 1)
    w_far_b = passed_along(w_after[half:], "Y", -1)

    parts = []
    for j in range(SPAN):
        part = attend(tokens, j, shard_len, reach, visitors[j], keys, values)
        pairs = [(s, home((s - j) % shard_count)) for s in range(shard_count)]
        parts.append(lax.ppermute(part, BLK, pairs))
    spread = combine(parts, z_count, tokens, heads)
    own = lax.all_to_all(spread, "Z", split_axis=0, concat_axis=0, tiled=True)
    other = passed_along(own, "K", 1)
    partial = project(own, other, (w_out, w_before, w_after, w_far_a, w_far_b))
    received = lax.all_to_all(partial, HEADS, split_axis=0, concat_axis=0, tiled=True)
    y_index = lax.axis_index("Y")
    place = jnp.stack(
        [
            y_index,
            (y_index + y_count - 1) % y_count,
            (y_index + 1) % y_count,
            (y_index + 2) % y_count,
            lax.axis_index("K"),
        ]
    ).astype(jnp.int32)
    summed = totals(place, received, y_count)
    ordered = lax.all_to_all(summed, "Y", split_axis=0, concat_axis=0, tiled=True)
    return ordered.reshape(-1, columns)


def solution(mesh):
    finer = Mesh(mesh.devices.reshape(2, 4, 4, 8, 2), HEADS + BLK)
    placed = (
        P(BLK, HEADS, None),
        P(HEADS, BLK, None),
        P(HEADS, BLK, None),
        P(),
        P(),
        P(HEADS, BLK),
    )

    return jax.shard_map(
        on_device, mesh=finer, in_specs=placed, out_specs=P(HEADS, BLK), check_vma=False
    )
```

time: 241 us -> 201 us (0.83)
  the two profiles are of different devices: /device:TPU:16 before, /device:TPU:8 now
where the time goes in v1:
time: 201 us; the launch traced here: 200 us
  starting transfers between devices  62.1 us (31%)
  waiting for transfers between devices  59.8 us (30%)
  blocking collectives  54 us (27%)
  Pallas kernels  18.9 us (9%)
  local copies, waits for them, and re-layouts  5.14 us (3%)
    all_to_all x1, blocking collectives, on_device(): own = lax.all_to_all(spread, 'Z', split_axis=0, concat_axis=0, tiled=True)  37.9 us
    ppermute x8, starting transfers between devices, passed_along(): lax.ppermute(value, axis, [(i, (i + steps) % count) for i in range(count)])  34.7 us
    ppermute x8, waiting for transfers between devices, passed_along(): lax.ppermute(value, axis, [(i, (i + steps) % count) for i in range(count)])  30.8 us
    all_to_all x1, waiting for transfers between devices, on_device(): lax.all_to_all(partial, HEADS, split_axis=0, concat_axis=0, tiled=True)  25 us
    ppermute x4, starting transfers between devices, on_device(): parts.append(lax.ppermute(part, BLK, pairs))  21.4 us
    all_to_all x1, blocking collectives, on_device(): lax.all_to_all(summed, 'Y', split_axis=0, concat_axis=0, tiled=True)  16.2 us
    pallas_call x4, Pallas kernels, attend(): pl.pallas_call(functools.partial(attend_kernel, tokens, offset), out_shap...  12.1 us
    all_to_all x1, starting transfers between devices, on_device(): lax.all_to_all(partial, HEADS, split_axis=0, concat_axis=0, tiled=True)  5.95 us
  transfers between devices with their start and end apart: 13, of which 5 were waited for; matrix products, arithmetic and copies ran while one was open for 0% of the time, Pallas kernels for 6%

profile of v1, /device:TPU:8, one launch (start us, length us, event | category | flops | bytes accessed | tf_op | source)
XLA Modules:
  0.0 200.2 jit_solution(14284628727709810319)
XLA Ops:
  0.0 0.9 copy.7
  0.9 1.9 collective-permute-start.1
  2.9 4.3 %collective-permute-start.3 = (bf16[512,128]{1,0:T(8,128)(2,1)S(1)}, bf16[512,128]{1,0:T(8,128)(2,1)S(1)}, u32[]{:S(2)}, u32[]{:S(2)}) collective-permute-start(bf16[512,128]{1,0:T(8,128)(2,1)S(1)} %bitcast.11), channel_id=1, source_target_pairs={{0,2},{1,3},{2,4},{3,5},{4,6},{5,7},{6,8},{7,9},{8,10},{9,11},{10,... | collective-permute-start | bytes 393224 | tf_op jit(solution)/shard_map/ppermute | solution.py:200
  7.1 6.1 %collective-permute-start.5 = (bf16[512,128]{1,0:T(8,128)(2,1)S(1)}, bf16[512,128]{1,0:T(8,128)(2,1)S(1)}, u32[]{:S(2)}, u32[]{:S(2)}) collective-permute-start(bf16[512,128]{1,0:T(8,128)(2,1)S(1)} %bitcast.12), channel_id=1, source_target_pairs={{0,3},{1,4},{2,5},{3,6},{4,7},{5,8},{6,9},{7,10},{8,11},{9,12},{10... | collective-permute-start | bytes 393224 | tf_op jit(solution)/shard_map/ppermute | solution.py:200
  13.2 0.0 copy-start
  13.2 1.0 copy-done
  14.3 0.0 copy-start.1
  14.3 1.0 copy-done.1
  15.3 0.0 copy-start.3
  15.3 0.7 copy-done.3
  16.0 0.0 copy-start.4
  16.0 0.7 copy-done.4
  16.6 3.0 %attend.4 = bf16[528,128]{1,0:T(8,128)(2,1)S(1)} custom-call(s32[64]{0:T(128)S(1)} %copy-done.3, s32[64]{0:T(128)S(1)} %copy-done.4, bf16[512,128]{1,0:T(8,128)(2,1)S(1)} %bitcast.13, bf16[2048,128]{1,0:T(8,128)(2,1)S(1)} %bitcast.14, bf16[2048,128]{1,0:T(8,128)(2,1)S(1)} %bitcast.18), custom_call_target="tpu_custom_call" | custom-call | flops 536870912 | bytes 1048576 | tf_op jit(solution)/shard_map/attend/pallas_call | solution.py:70
  19.7 0.7 collective-permute-start
  20.3 0.0 collective-permute-done.1.q_ref
  20.4 3.0 %attend.5 = bf16[528,128]{1,0:T(8,128)(2,1)S(1)} custom-call(s32[64]{0:T(128)S(1)} %copy-done.3, s32[64]{0:T(128)S(1)} %copy-done.4, bf16[512,128]{1,0:T(8,128)(2,1)S(1)} %collective-permute-done.1.q_ref, bf16[2048,128]{1,0:T(8,128)(2,1)S(1)} %bitcast.15, bf16[2048,128]{1,0:T(8,128)(2,1)S(1)} %bitcast.19), custom_call_target="tpu_custom_call" | custom-call | flops 536870912 | bytes 1048576 | tf_op jit(solution)/shard_map/attend/pallas_call | solution.py:70
  23.4 6.7 %collective-permute-start.2 = (bf16[528,128]{1,0:T(8,128)(2,1)S(1)}, bf16[528,128]{1,0:T(8,128)(2,1)S(1)}, u32[]{:S(2)}, u32[]{:S(2)}) collective-permute-start(bf16[528,128]{1,0:T(8,128)(2,1)S(1)} %attend.5), channel_id=1, source_target_pairs={{0,63},{1,0},{2,1},{3,16},{4,17},{5,32},{6,33},{7,48},{8,49},{9,2}... | collective-permute-start | bytes 405512 | tf_op jit(solution)/shard_map/ppermute | solution.py:231
  30.1 0.0 collective-permute-done.3.q_ref
  30.1 3.0 %attend.6 = bf16[528,128]{1,0:T(8,128)(2,1)S(1)} custom-call(s32[64]{0:T(128)S(1)} %copy-done.3, s32[64]{0:T(128)S(1)} %copy-done.4, bf16[512,128]{1,0:T(8,128)(2,1)S(1)} %collective-permute-done.3.q_ref, bf16[2048,128]{1,0:T(8,128)(2,1)S(1)} %bitcast.16, bf16[2048,128]{1,0:T(8,128)(2,1)S(1)} %bitcast.20), custom_call_target="tpu_custom_call" | custom-call | flops 536870912 | bytes 1048576 | tf_op jit(solution)/shard_map/attend/pallas_call | solution.py:70
  33.1 8.7 %collective-permute-start.4 = (bf16[528,128]{1,0:T(8,128)(2,1)S(1)}, bf16[528,128]{1,0:T(8,128)(2,1)S(1)}, u32[]{:S(2)}, u32[]{:S(2)}) collective-permute-start(bf16[528,128]{1,0:T(8,128)(2,1)S(1)} %attend.6), channel_id=1, source_target_pairs={{0,62},{1,63},{2,0},{3,1},{4,16},{5,17},{6,32},{7,33},{8,48},{9,49... | collective-permute-start | bytes 405512 | tf_op jit(solution)/shard_map/ppermute | solution.py:231
  41.8 0.0 collective-permute-done.5.q_ref
  41.8 3.0 %attend.7 = bf16[528,128]{1,0:T(8,128)(2,1)S(1)} custom-call(s32[64]{0:T(128)S(1)} %copy-done.3, s32[64]{0:T(128)S(1)} %copy-done.4, bf16[512,128]{1,0:T(8,128)(2,1)S(1)} %collective-permute-done.5.q_ref, bf16[2048,128]{1,0:T(8,128)(2,1)S(1)} %bitcast.17, bf16[2048,128]{1,0:T(8,128)(2,1)S(1)} %bitcast.21), custom_call_target="tpu_custom_call" | custom-call | flops 536870912 | bytes 1048576 | tf_op jit(solution)/shard_map/attend/pallas_call | solution.py:70
  44.9 0.0 copy-start.2
  44.9 5.4 %collective-permute-start.6 = (bf16[528,128]{1,0:T(8,128)(2,1)S(1)}, bf16[528,128]{1,0:T(8,128)(2,1)S(1)}, u32[]{:S(2)}, u32[]{:S(2)}) collective-permute-start(bf16[528,128]{1,0:T(8,128)(2,1)S(1)} %attend.7), channel_id=1, source_target_pairs={{0,47},{1,62},{2,63},{3,0},{4,1},{5,16},{6,17},{7,32},{8,33},{9,48... | collective-permute-start | bytes 405512 | tf_op jit(solution)/shard_map/ppermute | solution.py:231
  50.3 0.0 collective-permute-done.refs_0_
  50.3 0.0 collective-permute-done.2.refs_1_
  50.3 0.0 collective-permute-done.4.refs_2_
  50.4 3.9 %collective-permute-done.6.refs_3_ = bf16[528,128]{1,0:T(8,128)(2,1)S(1)} collective-permute-done((bf16[528,128]{1,0:T(8,128)(2,1)S(1)}, bf16[528,128]{1,0:T(8,128)(2,1)S(1)}, u32[]{:S(2)}, u32[]{:S(2)}) %collective-permute-start.6) | collective-permute-done | bytes 135200 | tf_op jit(solution)/shard_map/ppermute | solution.py:231
  54.3 0.5 combine.1
  54.8 37.9 %all_to_all.15.own_ref = bf16[8,64,1024]{2,1,0:T(8,128)(2,1)S(1)} all-to-all(bf16[8,64,1024]{2,1,0:T(8,128)(2,1)S(1)} %combine.1), channel_id=1, replica_groups=mesh['y'=2,'x'=4,'Y'=4,'Z'=8,'K'=2] {'Z'}, dimensions={0} | all-to-all | bytes 2097152 | tf_op jit(solution)/shard_map/all_to_all | solution.py:233
  92.7 5.7 %collective-permute-start.7 = (bf16[8,64,1024]{2,1,0:T(8,128)(2,1)S(1)}, bf16[8,64,1024]{2,1,0:T(8,128)(2,1)S(1)}, u32[]{:S(2)}, u32[]{:S(2)}) collective-permute-start(bf16[8,64,1024]{2,1,0:T(8,128)(2,1)S(1)} %all_to_all.15.own_ref), channel_id=1, source_target_pairs={{0,1},{1,0},{2,3},{3,2},{4,5},{5,4},{6,7},{7,6},{8,9},{9,8},{10,11... | collective-permute-start | bytes 3145736 | tf_op jit(solution)/shard_map/ppermute | solution.py:200
  98.4 0.0 copy-done.2
  98.4 4.2 %collective-permute-start.8 = (bf16[1024,256]{1,0:T(8,128)(2,1)S(1)}, bf16[1024,256]{1,0:T(8,128)(2,1)S(1)}, u32[]{:S(2)}, u32[]{:S(2)}) collective-permute-start(bf16[1024,256]{1,0:T(8,128)(2,1)S(1)} %copy-done.2), channel_id=1, source_target_pairs={{0,16},{16,32},{32,48},{48,0},{1,17},{17,33},{33,49},{49,1},{2,18}... | collective-permute-start | bytes 1572872 | tf_op jit(solution)/shard_map/ppermute | solution.py:200
  102.6 3.7 %collective-permute-start.9 = (bf16[1024,256]{1,0:T(8,128)(2,1)S(1)}, bf16[1024,256]{1,0:T(8,128)(2,1)S(1)}, u32[]{:S(2)}, u32[]{:S(2)}) collective-permute-start(bf16[1024,256]{1,0:T(8,128)(2,1)S(1)} %copy-done.2), channel_id=1, source_target_pairs={{0,48},{16,0},{32,16},{48,32},{1,49},{17,1},{33,17},{49,33},{2,50}... | collective-permute-start | bytes 1572872 | tf_op jit(solution)/shard_map/ppermute | solution.py:200
  106.4 15.9 %collective-permute-done.8.w1 = bf16[1024,256]{1,0:T(8,128)(2,1)S(1)} collective-permute-done((bf16[1024,256]{1,0:T(8,128)(2,1)S(1)}, bf16[1024,256]{1,0:T(8,128)(2,1)S(1)}, u32[]{:S(2)}, u32[]{:S(2)}) %collective-permute-start.8) | collective-permute-done | bytes 524320 | tf_op jit(solution)/shard_map/ppermute | solution.py:200
  122.3 4.4 %collective-permute-start.10 = (bf16[512,256]{1,0:T(8,128)(2,1)S(1)}, bf16[512,256]{1,0:T(8,128)(2,1)S(1)}, u32[]{:S(2)}, u32[]{:S(2)}) collective-permute-start(bf16[512,256]{1,0:T(8,128)(2,1)S(1)} %slice.8), channel_id=1, source_target_pairs={{0,16},{16,32},{32,48},{48,0},{1,17},{17,33},{33,49},{49,1},{2,18}... | collective-permute-start | bytes 786440 | tf_op jit(solution)/shard_map/ppermute | solution.py:200
  126.7 4.3 %collective-permute-done.9.w2 = bf16[1024,256]{1,0:T(8,128)(2,1)S(1)} collective-permute-done((bf16[1024,256]{1,0:T(8,128)(2,1)S(1)}, bf16[1024,256]{1,0:T(8,128)(2,1)S(1)}, u32[]{:S(2)}, u32[]{:S(2)}) %collective-permute-start.9) | collective-permute-done | bytes 524320 | tf_op jit(solution)/shard_map/ppermute | solution.py:200
  131.0 4.4 %collective-permute-start.11 = (bf16[512,256]{1,0:T(8,128)(2,1)S(1)}, bf16[512,256]{1,0:T(8,128)(2,1)S(1)}, u32[]{:S(2)}, u32[]{:S(2)}) collective-permute-start(bf16[512,256]{1,0:T(8,128)(2,1)S(1)} %slice.9), channel_id=1, source_target_pairs={{0,48},{16,0},{32,16},{48,32},{1,49},{17,1},{33,17},{49,33},{2,50}... | collective-permute-start | bytes 786440 | tf_op jit(solution)/shard_map/ppermute | solution.py:200
  135.4 0.0 collective-permute-done.10.w3a
  135.4 10.6 %collective-permute-done.11.w3b = bf16[512,256]{1,0:T(8,128)(2,1)S(1)} collective-permute-done((bf16[512,256]{1,0:T(8,128)(2,1)S(1)}, bf16[512,256]{1,0:T(8,128)(2,1)S(1)}, u32[]{:S(2)}, u32[]{:S(2)}) %collective-permute-start.11) | collective-permute-done | bytes 262176 | tf_op jit(solution)/shard_map/ppermute | solution.py:200
  146.0 0.0 collective-permute-done.7.other_ref
  146.0 5.1 %project.1 = bf16[8,128,1024]{2,1,0:T(8,128)(2,1)} custom-call(bf16[8,64,1024]{2,1,0:T(8,128)(2,1)S(1)} %all_to_all.15.own_ref, bf16[8,64,1024]{2,1,0:T(8,128)(2,1)S(1)} %collective-permute-done.7.other_ref, bf16[1024,256]{1,0:T(8,128)(2,1)S(1)} %copy-done.2, bf16[1024,256]{1,0:T(8,128)(2,1)S(1)} %collective-permute-done.8.w1, ...), custom_call_target="tpu_custom_call" | custom-call | flops 2147483648 | bytes 6291456 | tf_op jit(solution)/shard_map/project/pallas_call | solution.py:151
  151.1 5.9 %all-to-all-start.1 = ((bf16[8,128,1024]{2,1,0:T(8,128)(2,1)}), bf16[8,128,1024]{2,1,0:T(8,128)(2,1)S(1)}, u32[]{:S(2)}, u32[]{:S(2)}) async-start(bf16[8,128,1024]{2,1,0:T(8,128)(2,1)} %project.1), calls=%async_computation.1 | async-start | bytes 4194304 | tf_op jit(solution)/shard_map/all_to_all | solution.py:236
  157.0 0.1 stack.23.place
  157.1 25.0 %all-to-all-done.1.in_ref = bf16[8,128,1024]{2,1,0:T(8,128)(2,1)S(1)} async-done(((bf16[8,128,1024]{2,1,0:T(8,128)(2,1)}), bf16[8,128,1024]{2,1,0:T(8,128)(2,1)S(1)}, u32[]{:S(2)}, u32[]{:S(2)}) %all-to-all-start.1) | async-done | bytes 2097184 | tf_op jit(solution)/shard_map/all_to_all | solution.py:236
  182.2 1.2 totals.1
  183.3 16.2 %all_to_all.16 = bf16[4,128,256]{2,1,0:T(8,128)(2,1)S(1)} all-to-all(bf16[4,128,256]{2,1,0:T(8,128)(2,1)S(1)} %totals.1), channel_id=1, replica_groups=mesh['y'=2,'x'=4,'Y'=4,'Z'=8,'K'=2] {'Y'}, dimensions={0} | all-to-all | bytes 524288 | tf_op jit(solution)/shard_map/all_to_all | solution.py:248
  199.5 0.7 copy.9
  (2 shorter events, 0.0 us)
Async XLA Ops:
  0.9 19.4 %collective-permute-start.1 = (bf16[512,128]{1,0:T(8,128)(2,1)S(1)}, bf16[512,128]{1,0:T(8,128)(2,1)S(1)}, u32[]{:S(2)}, u32[]{:S(2)}) collective-permute-start(bf16[512,128]{1,0:T(8,128)(2,1)S(1)} %bitcast.10), channel_id=1, source_target_pairs={{0,1},{1,2},{2,3},{3,4},{4,5},{5,6},{6,7},{7,8},{8,9},{9,10},{10,1... | collective-permute-start | bytes 393224 | tf_op jit(solution)/shard_map/ppermute | solution.py:200
  2.9 27.2 %collective-permute-start.3 = (bf16[512,128]{1,0:T(8,128)(2,1)S(1)}, bf16[512,128]{1,0:T(8,128)(2,1)S(1)}, u32[]{:S(2)}, u32[]{:S(2)}) collective-permute-start(bf16[512,128]{1,0:T(8,128)(2,1)S(1)} %bitcast.11), channel_id=1, source_target_pairs={{0,2},{1,3},{2,4},{3,5},{4,6},{5,7},{6,8},{7,9},{8,10},{9,11},{10,... | collective-permute-start | bytes 393224 | tf_op jit(solution)/shard_map/ppermute | solution.py:200
  7.1 34.7 %collective-permute-start.5 = (bf16[512,128]{1,0:T(8,128)(2,1)S(1)}, bf16[512,128]{1,0:T(8,128)(2,1)S(1)}, u32[]{:S(2)}, u32[]{:S(2)}) collective-permute-start(bf16[512,128]{1,0:T(8,128)(2,1)S(1)} %bitcast.12), channel_id=1, source_target_pairs={{0,3},{1,4},{2,5},{3,6},{4,7},{5,8},{6,9},{7,10},{8,11},{9,12},{10... | collective-permute-start | bytes 393224 | tf_op jit(solution)/shard_map/ppermute | solution.py:200
  13.2 1.0 copy-start
  14.3 1.0 copy-start.1
  15.3 0.7 copy-start.3
  16.0 0.7 copy-start.4
  19.7 30.7 %collective-permute-start = (bf16[528,128]{1,0:T(8,128)(2,1)S(1)}, bf16[528,128]{1,0:T(8,128)(2,1)S(1)}, u32[]{:S(2)}, u32[]{:S(2)}) collective-permute-start(bf16[528,128]{1,0:T(8,128)(2,1)S(1)} %attend.4), channel_id=1, source_target_pairs={{0,0},{1,1},{2,16},{3,17},{4,32},{5,33},{6,48},{7,49},{8,2},{9,3},... | collective-permute-start | bytes 405512 | tf_op jit(solution)/shard_map/ppermute | solution.py:231
  23.4 26.9 %collective-permute-start.2 = (bf16[528,128]{1,0:T(8,128)(2,1)S(1)}, bf16[528,128]{1,0:T(8,128)(2,1)S(1)}, u32[]{:S(2)}, u32[]{:S(2)}) collective-permute-start(bf16[528,128]{1,0:T(8,128)(2,1)S(1)} %attend.5), channel_id=1, source_target_pairs={{0,63},{1,0},{2,1},{3,16},{4,17},{5,32},{6,33},{7,48},{8,49},{9,2}... | collective-permute-start | bytes 405512 | tf_op jit(solution)/shard_map/ppermute | solution.py:231
  33.1 17.2 %collective-permute-start.4 = (bf16[528,128]{1,0:T(8,128)(2,1)S(1)}, bf16[528,128]{1,0:T(8,128)(2,1)S(1)}, u32[]{:S(2)}, u32[]{:S(2)}) collective-permute-start(bf16[528,128]{1,0:T(8,128)(2,1)S(1)} %attend.6), channel_id=1, source_target_pairs={{0,62},{1,63},{2,0},{3,1},{4,16},{5,17},{6,32},{7,33},{8,48},{9,49... | collective-permute-start | bytes 405512 | tf_op jit(solution)/shard_map/ppermute | solution.py:231
  44.9 53.5 %copy-start.2 = (bf16[1024,256]{1,0:T(8,128)(2,1)S(1)}, bf16[1024,256]{1,0:T(8,128)(2,1)}, u32[]{:S(2)}) copy-start(bf16[1024,256]{1,0:T(8,128)(2,1)} %w0.1) | copy-start | bytes 1572868
  44.9 9.4 %collective-permute-start.6 = (bf16[528,128]{1,0:T(8,128)(2,1)S(1)}, bf16[528,128]{1,0:T(8,128)(2,1)S(1)}, u32[]{:S(2)}, u32[]{:S(2)}) collective-permute-start(bf16[528,128]{1,0:T(8,128)(2,1)S(1)} %attend.7), channel_id=1, source_target_pairs={{0,47},{1,62},{2,63},{3,0},{4,1},{5,16},{6,17},{7,32},{8,33},{9,48... | collective-permute-start | bytes 405512 | tf_op jit(solution)/shard_map/ppermute | solution.py:231
  92.7 53.4 %collective-permute-start.7 = (bf16[8,64,1024]{2,1,0:T(8,128)(2,1)S(1)}, bf16[8,64,1024]{2,1,0:T(8,128)(2,1)S(1)}, u32[]{:S(2)}, u32[]{:S(2)}) collective-permute-start(bf16[8,64,1024]{2,1,0:T(8,128)(2,1)S(1)} %all_to_all.15.own_ref), channel_id=1, source_target_pairs={{0,1},{1,0},{2,3},{3,2},{4,5},{5,4},{6,7},{7,6},{8,9},{9,8},{10,11... | collective-permute-start | bytes 3145736 | tf_op jit(solution)/shard_map/ppermute | solution.py:200
  98.4 23.9 %collective-permute-start.8 = (bf16[1024,256]{1,0:T(8,128)(2,1)S(1)}, bf16[1024,256]{1,0:T(8,128)(2,1)S(1)}, u32[]{:S(2)}, u32[]{:S(2)}) collective-permute-start(bf16[1024,256]{1,0:T(8,128)(2,1)S(1)} %copy-done.2), channel_id=1, source_target_pairs={{0,16},{16,32},{32,48},{48,0},{1,17},{17,33},{33,49},{49,1},{2,18}... | collective-permute-start | bytes 1572872 | tf_op jit(solution)/shard_map/ppermute | solution.py:200
  102.6 28.3 %collective-permute-start.9 = (bf16[1024,256]{1,0:T(8,128)(2,1)S(1)}, bf16[1024,256]{1,0:T(8,128)(2,1)S(1)}, u32[]{:S(2)}, u32[]{:S(2)}) collective-permute-start(bf16[1024,256]{1,0:T(8,128)(2,1)S(1)} %copy-done.2), channel_id=1, source_target_pairs={{0,48},{16,0},{32,16},{48,32},{1,49},{17,1},{33,17},{49,33},{2,50}... | collective-permute-start | bytes 1572872 | tf_op jit(solution)/shard_map/ppermute | solution.py:200
  122.3 13.1 %collective-permute-start.10 = (bf16[512,256]{1,0:T(8,128)(2,1)S(1)}, bf16[512,256]{1,0:T(8,128)(2,1)S(1)}, u32[]{:S(2)}, u32[]{:S(2)}) collective-permute-start(bf16[512,256]{1,0:T(8,128)(2,1)S(1)} %slice.8), channel_id=1, source_target_pairs={{0,16},{16,32},{32,48},{48,0},{1,17},{17,33},{33,49},{49,1},{2,18}... | collective-permute-start | bytes 786440 | tf_op jit(solution)/shard_map/ppermute | solution.py:200
  131.0 15.1 %collective-permute-start.11 = (bf16[512,256]{1,0:T(8,128)(2,1)S(1)}, bf16[512,256]{1,0:T(8,128)(2,1)S(1)}, u32[]{:S(2)}, u32[]{:S(2)}) collective-permute-start(bf16[512,256]{1,0:T(8,128)(2,1)S(1)} %slice.9), channel_id=1, source_target_pairs={{0,48},{16,0},{32,16},{48,32},{1,49},{17,1},{33,17},{49,33},{2,50}... | collective-permute-start | bytes 786440 | tf_op jit(solution)/shard_map/ppermute | solution.py:200
  151.1 31.1 %all-to-all-start.1 = ((bf16[8,128,1024]{2,1,0:T(8,128)(2,1)}), bf16[8,128,1024]{2,1,0:T(8,128)(2,1)S(1)}, u32[]{:S(2)}, u32[]{:S(2)}) async-start(bf16[8,128,1024]{2,1,0:T(8,128)(2,1)} %project.1), calls=%async_computation.1 | async-start | bytes 4194304 | tf_op jit(solution)/shard_map/all_to_all | solution.py:236

commit v2 on v1

v2 whole, which is shorter than its diff:
```python
import functools
import math

import jax
import jax.numpy as jnp
from jax import lax
from jax.experimental import pallas as pl
from jax.experimental.pallas import tpu as pltpu
from jax.sharding import Mesh
from jax.sharding import PartitionSpec as P

SPAN = 4
HEADS = ("y", "x")
BLK = ("Y", "Z", "K")
TILE = 128
NONE = -1e30
F32 = jnp.float32
BF16 = jnp.bfloat16


def eye_mask():
    rows = lax.broadcasted_iota(jnp.int32, (TILE, TILE), 0)
    lanes = lax.broadcasted_iota(jnp.int32, (TILE, TILE), 1)
    return rows == lanes


def part_body(offset, tokens, meta_ref, q_ref, k_ref, v_ref, out_ref):
    rows, head_size = q_ref.shape
    scale = head_size**-0.5 * math.log2(math.e)
    eye = eye_mask()
    length = meta_ref[SPAN : SPAN + 1, 0:1]
    base = meta_ref[offset : offset + 1, 0:1]
    stats = []
    for start in range(0, rows, TILE):
        scores = lax.dot_general(
            q_ref[start : start + TILE, :],
            k_ref[...],
            (((1,), (1,)), ((), ())),
            preferred_element_type=F32,
        )
        row = start + lax.broadcasted_iota(jnp.int32, (TILE, 1), 0)
        limit = jnp.minimum(length, base + row // (rows // tokens))
        slot = lax.broadcasted_iota(jnp.int32, scores.shape, 1)
        scores = jnp.where(slot < limit, scores, NONE)
        top = jnp.max(scores, axis=1, keepdims=True)
        weights = jnp.exp2((scores - top) * scale)
        total = jnp.sum(weights, axis=1, keepdims=True)
        values = jnp.dot(weights.astype(BF16), v_ref[...], preferred_element_type=F32)
        seen = top > 0.1 * NONE
        out_ref[start : start + TILE, :] = jnp.where(seen, values / total, 0.0).astype(BF16)
        level = jnp.where(seen, top * scale + jnp.log2(total), NONE)
        spread = jnp.where(eye, jnp.broadcast_to(level, (TILE, TILE)), 0.0)
        stats.append(jnp.sum(spread, axis=0, keepdims=True))
    level = jnp.concatenate(stats, axis=0)
    high = level.astype(BF16).astype(F32)
    middle = (level - high).astype(BF16).astype(F32)
    low = level - high - middle
    out_ref[rows:, :] = jnp.concatenate(
        [high, middle, low, jnp.zeros_like(low)], axis=0
    ).astype(BF16)


def first_kernel(tokens, *refs):
    out_ref, k_ref, v_ref, meta_ref, lengths, reaches, q_ref, sems = refs[5:]
    copies = [
        pltpu.make_async_copy(source, target, sems.at[i])
        for i, (source, target) in enumerate(zip(refs[:5], (lengths, reaches, q_ref, k_ref, v_ref)))
    ]
    for copy in copies:
        copy.start()
    copies[0].wait()
    copies[1].wait()
    count = lengths.shape[0]
    own_index = lax.axis_index(BLK)
    row = lax.broadcasted_iota(jnp.int32, meta_ref.shape, 0)
    meta = jnp.full(meta_ref.shape, lengths[own_index], jnp.int32)
    for j in range(SPAN):
        base = reaches[lax.rem(own_index + (count - j), count)] - j * k_ref.shape[0]
        meta = jnp.where(row == j, base, meta)
    meta_ref[...] = meta
    for copy in copies[2:]:
        copy.wait()
    part_body(0, tokens, meta_ref, q_ref, k_ref, v_ref, out_ref)


def part_cost(rows, slots, head_size):
    return pl.CostEstimate(
        flops=4 * rows * slots * head_size,
        bytes_accessed=4 * slots * head_size,
        transcendentals=rows * slots,
    )


VMEM = pl.BlockSpec(memory_space=pltpu.VMEM)


def first_part(tokens, lengths, reaches, q, k, v):
    rows, head_size = q.shape
    extra = 4 * (rows // TILE)
    hbm = pl.BlockSpec(memory_space=pltpu.HBM)
    return pl.pallas_call(
        functools.partial(first_kernel, tokens),
        out_shape=(
            jax.ShapeDtypeStruct((rows + extra, head_size), BF16),
            jax.ShapeDtypeStruct(k.shape, BF16),
            jax.ShapeDtypeStruct(v.shape, BF16),
            jax.ShapeDtypeStruct((8, 128), jnp.int32),
        ),
        in_specs=[hbm] * 5,
        out_specs=(VMEM,) * 4,
        scratch_shapes=[
            pltpu.SMEM(lengths.shape, jnp.int32),
            pltpu.SMEM(reaches.shape, jnp.int32),
            pltpu.VMEM(q.shape, BF16),
            pltpu.SemaphoreType.DMA((5,)),
        ],
        compiler_params=pltpu.CompilerParams(vmem_limit_bytes=24 << 20),
        cost_estimate=part_cost(rows, k.shape[0], head_size),
        name="first_part",
    )(*(pltpu.with_memory_space_constraint(a, pltpu.HBM) for a in (lengths, reaches, q, k, v)))


def later_part(tokens, offset, meta, q, k, v):
    rows, head_size = q.shape
    extra = 4 * (rows // TILE)
    return pl.pallas_call(
        functools.partial(part_body, offset, tokens),
        out_shape=jax.ShapeDtypeStruct((rows + extra, head_size), BF16),
        in_specs=[VMEM] * 4,
        out_specs=VMEM,
        compiler_params=pltpu.CompilerParams(vmem_limit_bytes=24 << 20),
        cost_estimate=part_cost(rows, k.shape[0], head_size),
        name="later_part",
    )(meta, q, k, v)


def combine_kernel(*refs):
    parts, out_ref, total_ref = refs[:-2], refs[-2], refs[-1]
    copies, tokens, _ = out_ref.shape
    head_size = parts[0].shape[1]
    groups = parts[0].shape[0] // (TILE + 4)
    rows = groups * TILE
    levels = []
    for part in parts:
        terms = part[rows:, :].astype(F32)
        levels.append(
            terms[:groups] + terms[groups : 2 * groups] + terms[2 * groups : 3 * groups]
        )
    top = functools.reduce(jnp.maximum, levels)
    factors = [jnp.exp2(level - top) for level in levels]
    inverse = 1.0 / functools.reduce(jnp.add, factors)
    eye = eye_mask()
    for group in range(groups):
        total = None
        for part, factor in zip(parts, factors):
            line = jnp.broadcast_to((factor * inverse)[group : group + 1, :], (TILE, TILE))
            column = jnp.sum(jnp.where(eye, line, 0.0), axis=1, keepdims=True)
            term = part[group * TILE : (group + 1) * TILE, :].astype(F32) * column
            total = term if total is None else total + term
        total_ref[group * TILE : (group + 1) * TILE, :] = total
    heads = rows // tokens
    for head in range(heads):
        piece = total_ref[pl.ds(head, tokens, stride=heads), :].astype(BF16)
        for copy in range(copies):
            out_ref[copy, :, head * head_size : (head + 1) * head_size] = piece


def combine(parts, copies, tokens, heads):
    head_size = parts[0].shape[1]
    vmem = pl.BlockSpec(memory_space=pltpu.VMEM)
    return pl.pallas_call(
        combine_kernel,
        out_shape=jax.ShapeDtypeStruct((copies, tokens, heads * head_size), BF16),
        in_specs=[vmem] * len(parts),
        out_specs=vmem,
        scratch_shapes=[pltpu.VMEM((heads * tokens, head_size), F32)],
        compiler_params=pltpu.CompilerParams(vmem_limit_bytes=8 << 20),
        cost_estimate=pl.CostEstimate(
            flops=1 << 20, bytes_accessed=1 << 20, transcendentals=0
        ),
        name="combine",
    )(*parts)


def project_kernel(own_ref, other_ref, w0, w1, w2, w3, out_ref):
    columns = w0.shape[1]
    lhs = jnp.concatenate([own_ref[0], other_ref[0]], axis=0)
    for i, w in enumerate((w0, w1, w2, w3)):
        out_ref[0, :, i * columns : (i + 1) * columns] = jnp.dot(
            lhs, w[...], preferred_element_type=F32
        ).astype(BF16)


def project(own, other, pieces):
    groups, rows, depth = own.shape
    columns = pieces[0].shape[1]
    half = groups // 2
    whole = lambda w: pl.BlockSpec(w.shape, lambda i: (0, 0))
    side = pl.BlockSpec((1, rows, depth), lambda i: ((i % 2) * half + i // 2, 0, 0))
    return pl.pallas_call(
        project_kernel,
        grid=(groups,),
        out_shape=pltpu.HBM((groups, 2 * rows, 4 * columns), BF16),
        in_specs=[side, side] + [whole(w) for w in pieces],
        out_specs=pl.BlockSpec((1, 2 * rows, 4 * columns), lambda i: (i, 0, 0)),
        compiler_params=pltpu.CompilerParams(vmem_limit_bytes=24 << 20),
        cost_estimate=pl.CostEstimate(
            flops=16 * groups * rows * depth * columns,
            bytes_accessed=6 << 20,
            transcendentals=0,
        ),
        name="project",
    )(own, other, *pieces)


def total_kernel(place, in_ref, *out_refs):
    half = in_ref.shape[1] // 2
    total = in_ref[0].astype(F32)
    for i in range(1, in_ref.shape[0]):
        total += in_ref[i].astype(F32)
    total = total.astype(BF16)
    core = lax.axis_index("K")
    for k, out_ref in enumerate(out_refs):

        @pl.when(pl.program_id(0) == k)
        def _():
            out_ref[pl.ds(pl.multiple_of(core * half, half), half), :] = total[:half]
            out_ref[pl.ds(pl.multiple_of((1 - core) * half, half), half), :] = total[half:]


def totals(place, received, count):
    sources, rows, width = received.shape
    columns = width // count
    return pl.pallas_call(
        total_kernel,
        grid_spec=pltpu.PrefetchScalarGridSpec(
            num_scalar_prefetch=1,
            grid=(count,),
            in_specs=[pl.BlockSpec((sources, rows, columns), lambda i, place: (0, 0, place[i]))],
            out_specs=[pl.BlockSpec((rows, columns), lambda i, place: (0, 0))] * count,
        ),
        out_shape=[jax.ShapeDtypeStruct((rows, columns), BF16)] * count,
        compiler_params=pltpu.CompilerParams(vmem_limit_bytes=16 << 20),
        cost_estimate=pl.CostEstimate(
            flops=sources * rows * width, bytes_accessed=3 << 20, transcendentals=0
        ),
        name="totals",
    )(place, received)


def order_kernel(*refs):
    pieces, out_ref = refs[:-1], refs[-1]
    count = len(pieces)
    rows = pieces[0].shape[0]
    own = lax.axis_index("Y")
    for k, piece in enumerate(pieces):
        slot = lax.rem(own + (count - k), count)
        out_ref[pl.ds(pl.multiple_of(slot * rows, rows), rows), :] = piece[...]


def in_order(pieces):
    rows, columns = pieces[0].shape
    return pl.pallas_call(
        order_kernel,
        out_shape=jax.ShapeDtypeStruct((len(pieces) * rows, columns), BF16),
        in_specs=[VMEM] * len(pieces),
        out_specs=VMEM,
        compiler_params=pltpu.CompilerParams(vmem_limit_bytes=4 << 20),
        cost_estimate=pl.CostEstimate(
            flops=1 << 18, bytes_accessed=1 << 19, transcendentals=0
        ),
        name="in_order",
    )(*pieces)


def passed_along(value, axis, steps):
    count = lax.axis_size(axis)
    return lax.ppermute(value, axis, [(i, (i + steps) % count) for i in range(count)])


def on_device(queries, prefix_keys, cached_prefix_values, shard_len, reach, w_out):
    y_count, z_count, _ = (lax.axis_size(a) for a in BLK)
    tokens, heads, head_size = queries.shape
    q_own = queries.reshape(tokens * heads, head_size)

    visitors = []
    for j in range(1, SPAN):
        visitors.append(passed_along(q_own, BLK, j))
    w_before = passed_along(w_out, "Y", 1)
    w_after = passed_along(w_out, "Y", -1)
    w_far = passed_along(w_out, "Y", 2)

    part, keys, values, meta = first_part(
        tokens, shard_len, reach, q_own, prefix_keys[0], cached_prefix_values[0]
    )
    parts = [part]
    for j in range(1, SPAN):
        part = later_part(tokens, j, meta, visitors[j - 1], keys, values)
        parts.append(passed_along(part, BLK, -j))
    spread = combine(parts, z_count, tokens, heads)
    own = lax.all_to_all(spread, "Z", split_axis=0, concat_axis=0, tiled=True)
    other = passed_along(own, "K", 1)
    partial = project(own, other, (w_out, w_before, w_after, w_far))
    received = lax.all_to_all(partial, HEADS, split_axis=0, concat_axis=0, tiled=True)
    x_half = lax.axis_size("x") // 2
    held = lax.axis_index("y") * x_half + lax.axis_index("x") // 2
    shift = (held + jnp.arange(y_count, dtype=jnp.int32) - lax.axis_index("Y")) % y_count
    place = jnp.where(shift == 0, 0, jnp.where(shift == y_count - 1, 1, shift + 1))
    summed = totals(place.astype(jnp.int32), received, y_count)
    moved = []
    for k in range(y_count):
        pairs = []
        for y in range(lax.axis_size("y")):
            for x in range(lax.axis_size("x")):
                for big in range(y_count):
                    target = (y * x_half + x // 2 + k) % y_count
                    group = (big // x_half) * 2 * x_half + (big % x_half) * 2 + x % 2
                    pairs.append(((y * 2 * x_half + x) * y_count + big, group * y_count + target))
        moved.append(lax.ppermute(summed[k], ("y", "x", "Y"), pairs))
    return in_order(moved)


def solution(mesh):
    finer = Mesh(mesh.devices.reshape(2, 4, 4, 8, 2), HEADS + BLK)
    placed = (
        P(BLK, HEADS, None),
        P(HEADS, BLK, None),
        P(HEADS, BLK, None),
        P(),
        P(),
        P(HEADS, BLK),
    )

    return jax.shard_map(
        on_device, mesh=finer, in_specs=placed, out_specs=P(HEADS, BLK), check_vma=False
    )
```

time: 201 us -> 194 us (0.965)
  waiting for transfers between devices: 59.8 us -> 82.7 us
  blocking collectives: 54 us -> 33.9 us
  local copies, waits for them, and re-layouts: 5.14 us -> 0.01 us
  starting transfers between devices: 62.1 us -> 58.1 us
    ppermute x8 -> x10, waiting for transfers between devices: 30.8 us -> 48.4 us  [passed_along(): lax.ppermute(value, axis, [(i, (i + steps) % count) for i in range(count)])]
    all_to_all x1 -> x0, blocking collectives: 16.2 us -> none  [on_device(): lax.all_to_all(summed, 'Y', split_axis=0, concat_axis=0, tiled=True)]
    ppermute x4, starting transfers between devices: 21.4 us -> 13.1 us  [on_device(): moved.append(lax.ppermute(summed[k], ('y', 'x', 'Y'), pairs))]
    ppermute x4, waiting for transfers between devices: 3.92 us -> 9.73 us  [on_device(): moved.append(lax.ppermute(summed[k], ('y', 'x', 'Y'), pairs))]
    ppermute x8 -> x10, starting transfers between devices: 34.7 us -> 39.3 us  [passed_along(): lax.ppermute(value, axis, [(i, (i + steps) % count) for i in range(count)])]
    unnamed x11 -> x2, local copies, waits for them, and re-layouts: 4.1 us -> 0.01 us
    all_to_all x1, blocking collectives: 37.9 us -> 33.9 us  [on_device(): own = lax.all_to_all(spread, 'Z', split_axis=0, concat_axis=0, tiled=True)]
    pallas_call x4 -> x5, Pallas kernels: 12.1 us -> 12 us  [the longest x3 7.43 us: later_part(): pl.pallas_call(functools.partial(part_body, offset, tokens), out_shape=ja...]
  transfers between devices with their start and end apart: 13 -> 15, of which waited for: 5 -> 9; matrix products, arithmetic and copies ran while one was open for 0% -> 0% of each run, Pallas kernels for 6% -> 6%
where the time goes in v2:
time: 194 us
  waiting for transfers between devices  82.7 us (43%)
  starting transfers between devices  58.1 us (30%)
  blocking collectives  33.9 us (17%)
  Pallas kernels  18.8 us (10%)
    ppermute x10, waiting for transfers between devices, passed_along(): lax.ppermute(value, axis, [(i, (i + steps) % count) for i in range(count)])  48.4 us
    ppermute x10, starting transfers between devices, passed_along(): lax.ppermute(value, axis, [(i, (i + steps) % count) for i in range(count)])  39.3 us
    all_to_all x1, blocking collectives, on_device(): own = lax.all_to_all(spread, 'Z', split_axis=0, concat_axis=0, tiled=True)  33.9 us
    all_to_all x1, waiting for transfers between devices, on_device(): lax.all_to_all(partial, HEADS, split_axis=0, concat_axis=0, tiled=True)  24.5 us
    ppermute x4, starting transfers between devices, on_device(): moved.append(lax.ppermute(summed[k], ('y', 'x', 'Y'), pairs))  13.1 us
    ppermute x4, waiting for transfers between devices, on_device(): moved.append(lax.ppermute(summed[k], ('y', 'x', 'Y'), pairs))  9.73 us
    pallas_call x3, Pallas kernels, later_part(): pl.pallas_call(functools.partial(part_body, offset, tokens), out_shape=ja...  7.43 us
    all_to_all x1, starting transfers between devices, on_device(): lax.all_to_all(partial, HEADS, split_axis=0, concat_axis=0, tiled=True)  5.76 us
  transfers between devices with their start and end apart: 15, of which 9 were waited for; matrix products, arithmetic and copies ran while one was open for 0% of the time, Pallas kernels for 6%

profile of v2, /device:TPU:8, one launch (start us, length us, event | category | flops | bytes accessed | tf_op | source)
XLA Modules:
  0.0 193.7 jit_solution(17840472091204833184)
XLA Ops:
  0.0 3.7 %collective-permute-start.4 = (bf16[512,128]{1,0:T(8,128)(2,1)}, bf16[512,128]{1,0:T(8,128)(2,1)S(1)}, u32[]{:S(2)}, u32[]{:S(2)}) collective-permute-start(bf16[512,128]{1,0:T(8,128)(2,1)} %bitcast.5), channel_id=1, source_target_pairs={{0,3},{1,4},{2,5},{3,6},{4,7},{5,8},{6,9},{7,10},{8,11},{9,12},{10... | collective-permute-start | bytes 393224 | tf_op jit(solution)/shard_map/ppermute | solution.py:278
  3.7 4.3 %collective-permute-start.2 = (bf16[512,128]{1,0:T(8,128)(2,1)}, bf16[512,128]{1,0:T(8,128)(2,1)S(1)}, u32[]{:S(2)}, u32[]{:S(2)}) collective-permute-start(bf16[512,128]{1,0:T(8,128)(2,1)} %bitcast.6), channel_id=1, source_target_pairs={{0,2},{1,3},{2,4},{3,5},{4,6},{5,7},{6,8},{7,9},{8,10},{9,11},{10,... | collective-permute-start | bytes 393224 | tf_op jit(solution)/shard_map/ppermute | solution.py:278
  8.0 4.1 %collective-permute-start = (bf16[512,128]{1,0:T(8,128)(2,1)}, bf16[512,128]{1,0:T(8,128)(2,1)S(1)}, u32[]{:S(2)}, u32[]{:S(2)}) collective-permute-start(bf16[512,128]{1,0:T(8,128)(2,1)} %bitcast.7), channel_id=1, source_target_pairs={{0,1},{1,2},{2,3},{3,4},{4,5},{5,6},{6,7},{7,8},{8,9},{9,10},{10,1... | collective-permute-start | bytes 393224 | tf_op jit(solution)/shard_map/ppermute | solution.py:278
  12.1 3.8 %first_part.1 = (bf16[528,128]{1,0:T(8,128)(2,1)S(1)}, bf16[2048,128]{1,0:T(8,128)(2,1)S(1)}, bf16[2048,128]{1,0:T(8,128)(2,1)S(1)}, s32[8,128]{1,0:T(8,128)S(1)}) custom-call(s32[64]{0:T(128)} %refs_0_.1, s32[64]{0:T(128)} %refs_1_.1, bf16[512,128]{1,0:T(8,128)(2,1)} %bitcast.8, bf16[2048,128]{1,0:T(8,128)(2,1)} %bitcast.3, bf16[2048,128]{1,0:T(8,128)(2,1)} %bitcast.4), custom_call_target="tpu_custom_call" | custom-call | flops 536870912 | bytes 1048576 | tf_op jit(solution)/shard_map/first_part/pallas_call | solution.py:101
  15.9 1.5 collective-permute-done.4.q_ref
  17.4 2.5 %later_part.5 = bf16[528,128]{1,0:T(8,128)(2,1)S(1)} custom-call(s32[8,128]{1,0:T(8,128)S(1)} %get-tuple-element.14.meta_ref, bf16[512,128]{1,0:T(8,128)(2,1)S(1)} %collective-permute-done.4.q_ref, bf16[2048,128]{1,0:T(8,128)(2,1)S(1)} %get-tuple-element.15.k_ref, bf16[2048,128]{1,0:T(8,128)(2,1)S(1)} %get-tuple-element.16.v_ref), custom_call_target="tpu_custom_call" | custom-call | flops 536870912 | bytes 1048576 | tf_op jit(solution)/shard_map/later_part/pallas_call | solution.py:126
  19.9 7.1 %collective-permute-start.5 = (bf16[528,128]{1,0:T(8,128)(2,1)S(1)}, bf16[528,128]{1,0:T(8,128)(2,1)S(1)}, u32[]{:S(2)}, u32[]{:S(2)}) collective-permute-start(bf16[528,128]{1,0:T(8,128)(2,1)S(1)} %later_part.5), channel_id=1, source_target_pairs={{0,61},{1,62},{2,63},{3,0},{4,1},{5,2},{6,3},{7,4},{8,5},{9,6},{10... | collective-permute-start | bytes 405512 | tf_op jit(solution)/shard_map/ppermute | solution.py:278
  27.0 1.1 collective-permute-done.2.q_ref
  28.1 2.5 %later_part.4 = bf16[528,128]{1,0:T(8,128)(2,1)S(1)} custom-call(s32[8,128]{1,0:T(8,128)S(1)} %get-tuple-element.14.meta_ref, bf16[512,128]{1,0:T(8,128)(2,1)S(1)} %collective-permute-done.2.q_ref, bf16[2048,128]{1,0:T(8,128)(2,1)S(1)} %get-tuple-element.15.k_ref, bf16[2048,128]{1,0:T(8,128)(2,1)S(1)} %get-tuple-element.16.v_ref), custom_call_target="tpu_custom_call" | custom-call | flops 536870912 | bytes 1048576 | tf_op jit(solution)/shard_map/later_part/pallas_call | solution.py:126
  30.6 2.8 %collective-permute-start.3 = (bf16[528,128]{1,0:T(8,128)(2,1)S(1)}, bf16[528,128]{1,0:T(8,128)(2,1)S(1)}, u32[]{:S(2)}, u32[]{:S(2)}) collective-permute-start(bf16[528,128]{1,0:T(8,128)(2,1)S(1)} %later_part.4), channel_id=1, source_target_pairs={{0,62},{1,63},{2,0},{3,1},{4,2},{5,3},{6,4},{7,5},{8,6},{9,7},{10,... | collective-permute-start | bytes 405512 | tf_op jit(solution)/shard_map/ppermute | solution.py:278
  33.4 0.0 collective-permute-done.q_ref
  33.4 2.5 %later_part.3 = bf16[528,128]{1,0:T(8,128)(2,1)S(1)} custom-call(s32[8,128]{1,0:T(8,128)S(1)} %get-tuple-element.14.meta_ref, bf16[512,128]{1,0:T(8,128)(2,1)S(1)} %collective-permute-done.q_ref, bf16[2048,128]{1,0:T(8,128)(2,1)S(1)} %get-tuple-element.15.k_ref, bf16[2048,128]{1,0:T(8,128)(2,1)S(1)} %get-tuple-element.16.v_ref), custom_call_target="tpu_custom_call" | custom-call | flops 536870912 | bytes 1048576 | tf_op jit(solution)/shard_map/later_part/pallas_call | solution.py:126
  35.9 0.0 copy-start
  35.9 2.1 %collective-permute-start.1 = (bf16[528,128]{1,0:T(8,128)(2,1)S(1)}, bf16[528,128]{1,0:T(8,128)(2,1)S(1)}, u32[]{:S(2)}, u32[]{:S(2)}) collective-permute-start(bf16[528,128]{1,0:T(8,128)(2,1)S(1)} %later_part.3), channel_id=1, source_target_pairs={{0,63},{1,0},{2,1},{3,2},{4,3},{5,4},{6,5},{7,6},{8,7},{9,8},{10,9... | collective-permute-start | bytes 405512 | tf_op jit(solution)/shard_map/ppermute | solution.py:278
  38.0 0.0 collective-permute-done.5.refs_3_
  38.0 0.0 collective-permute-done.3.refs_2_
  38.0 2.5 %collective-permute-done.1.refs_1_ = bf16[528,128]{1,0:T(8,128)(2,1)S(1)} collective-permute-done((bf16[528,128]{1,0:T(8,128)(2,1)S(1)}, bf16[528,128]{1,0:T(8,128)(2,1)S(1)}, u32[]{:S(2)}, u32[]{:S(2)}) %collective-permute-start.1) | collective-permute-done | bytes 135200 | tf_op jit(solution)/shard_map/ppermute | solution.py:278
  40.5 0.5 combine.1
  41.0 33.9 %all_to_all.10.own_ref = bf16[8,64,1024]{2,1,0:T(8,128)(2,1)S(1)} all-to-all(bf16[8,64,1024]{2,1,0:T(8,128)(2,1)S(1)} %combine.1), channel_id=1, replica_groups=mesh['y'=2,'x'=4,'Y'=4,'Z'=8,'K'=2] {'Z'}, dimensions={0} | all-to-all | bytes 2097152 | tf_op jit(solution)/shard_map/all_to_all | solution.py:301
  74.9 2.0 %collective-permute-start.6 = (bf16[8,64,1024]{2,1,0:T(8,128)(2,1)S(1)}, bf16[8,64,1024]{2,1,0:T(8,128)(2,1)S(1)}, u32[]{:S(2)}, u32[]{:S(2)}) collective-permute-start(bf16[8,64,1024]{2,1,0:T(8,128)(2,1)S(1)} %all_to_all.10.own_ref), channel_id=1, source_target_pairs={{0,1},{1,0},{2,3},{3,2},{4,5},{5,4},{6,7},{7,6},{8,9},{9,8},{10,11... | collective-permute-start | bytes 3145736 | tf_op jit(solution)/shard_map/ppermute | solution.py:278
  76.9 0.0 copy-done
  76.9 4.4 %collective-permute-start.7 = (bf16[1024,256]{1,0:T(8,128)(2,1)S(1)}, bf16[1024,256]{1,0:T(8,128)(2,1)S(1)}, u32[]{:S(2)}, u32[]{:S(2)}) collective-permute-start(bf16[1024,256]{1,0:T(8,128)(2,1)S(1)} %copy-done), channel_id=1, source_target_pairs={{0,16},{16,32},{32,48},{48,0},{1,17},{17,33},{33,49},{49,1},{2,18}... | collective-permute-start | bytes 1572872 | tf_op jit(solution)/shard_map/ppermute | solution.py:278
  81.4 3.5 %collective-permute-start.8 = (bf16[1024,256]{1,0:T(8,128)(2,1)S(1)}, bf16[1024,256]{1,0:T(8,128)(2,1)S(1)}, u32[]{:S(2)}, u32[]{:S(2)}) collective-permute-start(bf16[1024,256]{1,0:T(8,128)(2,1)S(1)} %copy-done), channel_id=1, source_target_pairs={{0,48},{16,0},{32,16},{48,32},{1,49},{17,1},{33,17},{49,33},{2,50}... | collective-permute-start | bytes 1572872 | tf_op jit(solution)/shard_map/ppermute | solution.py:278
  84.9 5.3 %collective-permute-start.9 = (bf16[1024,256]{1,0:T(8,128)(2,1)S(1)}, bf16[1024,256]{1,0:T(8,128)(2,1)S(1)}, u32[]{:S(2)}, u32[]{:S(2)}) collective-permute-start(bf16[1024,256]{1,0:T(8,128)(2,1)S(1)} %copy-done), channel_id=1, source_target_pairs={{0,32},{16,48},{32,0},{48,16},{1,33},{17,49},{33,1},{49,17},{2,34}... | collective-permute-start | bytes 1572872 | tf_op jit(solution)/shard_map/ppermute | solution.py:278
  90.2 38.7 %collective-permute-done.7.w1 = bf16[1024,256]{1,0:T(8,128)(2,1)S(1)} collective-permute-done((bf16[1024,256]{1,0:T(8,128)(2,1)S(1)}, bf16[1024,256]{1,0:T(8,128)(2,1)S(1)}, u32[]{:S(2)}, u32[]{:S(2)}) %collective-permute-start.7) | collective-permute-done | bytes 524320 | tf_op jit(solution)/shard_map/ppermute | solution.py:278
  128.8 0.0 collective-permute-done.8.w2
  128.8 4.6 %collective-permute-done.9.w3 = bf16[1024,256]{1,0:T(8,128)(2,1)S(1)} collective-permute-done((bf16[1024,256]{1,0:T(8,128)(2,1)S(1)}, bf16[1024,256]{1,0:T(8,128)(2,1)S(1)}, u32[]{:S(2)}, u32[]{:S(2)}) %collective-permute-start.9) | collective-permute-done | bytes 524320 | tf_op jit(solution)/shard_map/ppermute | solution.py:278
  133.4 0.0 collective-permute-done.6.other_ref
  133.4 5.1 %project.1 = bf16[8,128,1024]{2,1,0:T(8,128)(2,1)} custom-call(bf16[8,64,1024]{2,1,0:T(8,128)(2,1)S(1)} %all_to_all.10.own_ref, bf16[8,64,1024]{2,1,0:T(8,128)(2,1)S(1)} %collective-permute-done.6.other_ref, bf16[1024,256]{1,0:T(8,128)(2,1)S(1)} %copy-done, bf16[1024,256]{1,0:T(8,128)(2,1)S(1)} %collective-permute-done.7.w1, ...), custom_call_target="tpu_custom_call" | custom-call | flops 2147483648 | bytes 6291456 | tf_op jit(solution)/shard_map/project/pallas_call | solution.py:200
  138.5 5.8 %all-to-all-start.1 = ((bf16[8,128,1024]{2,1,0:T(8,128)(2,1)}), bf16[8,128,1024]{2,1,0:T(8,128)(2,1)S(1)}, u32[]{:S(2)}, u32[]{:S(2)}) async-start(bf16[8,128,1024]{2,1,0:T(8,128)(2,1)} %project.1), calls=%async_computation.1 | async-start | bytes 4194304 | tf_op jit(solution)/shard_map/all_to_all | solution.py:304
  144.3 24.5 %all-to-all-done.1.in_ref = bf16[8,128,1024]{2,1,0:T(8,128)(2,1)S(1)} async-done(((bf16[8,128,1024]{2,1,0:T(8,128)(2,1)}), bf16[8,128,1024]{2,1,0:T(8,128)(2,1)S(1)}, u32[]{:S(2)}, u32[]{:S(2)}) %all-to-all-start.1) | async-done | bytes 2097184 | tf_op jit(solution)/shard_map/all_to_all | solution.py:304
  168.8 1.3 totals.1
  170.1 3.7 %collective-permute-start.10 = (bf16[128,256]{1,0:T(8,128)(2,1)S(1)}, bf16[128,256]{1,0:T(8,128)(2,1)S(1)}, u32[]{:S(2)}, u32[]{:S(2)}) collective-permute-start(bf16[128,256]{1,0:T(8,128)(2,1)S(1)} %get-tuple-element.17), channel_id=1, source_target_pairs={{0,0},{16,128},{32,256},{48,384},{64,64},{80,192},{96,320},{112,44... | collective-permute-start | bytes 196616 | tf_op jit(solution)/shard_map/ppermute | solution.py:319
  173.8 5.5 %collective-permute-start.11 = (bf16[128,256]{1,0:T(8,128)(2,1)S(1)}, bf16[128,256]{1,0:T(8,128)(2,1)S(1)}, u32[]{:S(2)}, u32[]{:S(2)}) collective-permute-start(bf16[128,256]{1,0:T(8,128)(2,1)S(1)} %get-tuple-element.18), channel_id=1, source_target_pairs={{0,16},{16,144},{32,272},{48,400},{64,80},{80,208},{96,336},{112,4... | collective-permute-start | bytes 196616 | tf_op jit(solution)/shard_map/ppermute | solution.py:319
  179.3 1.9 collective-permute-start.12
  181.3 1.9 collective-permute-start.13
  183.2 0.0 collective-permute-done.10.refs_0_
  183.2 4.1 %collective-permute-done.11.refs_1_ = bf16[128,256]{1,0:T(8,128)(2,1)S(1)} collective-permute-done((bf16[128,256]{1,0:T(8,128)(2,1)S(1)}, bf16[128,256]{1,0:T(8,128)(2,1)S(1)}, u32[]{:S(2)}, u32[]{:S(2)}) %collective-permute-start.11) | collective-permute-done | bytes 65568 | tf_op jit(solution)/shard_map/ppermute | solution.py:319
  187.3 2.2 %collective-permute-done.12.refs_2_ = bf16[128,256]{1,0:T(8,128)(2,1)S(1)} collective-permute-done((bf16[128,256]{1,0:T(8,128)(2,1)S(1)}, bf16[128,256]{1,0:T(8,128)(2,1)S(1)}, u32[]{:S(2)}, u32[]{:S(2)}) %collective-permute-start.12) | collective-permute-done | bytes 65568 | tf_op jit(solution)/shard_map/ppermute | solution.py:319
  189.5 3.4 %collective-permute-done.13.refs_3_ = bf16[128,256]{1,0:T(8,128)(2,1)S(1)} collective-permute-done((bf16[128,256]{1,0:T(8,128)(2,1)S(1)}, bf16[128,256]{1,0:T(8,128)(2,1)S(1)}, u32[]{:S(2)}, u32[]{:S(2)}) %collective-permute-start.13) | collective-permute-done | bytes 65568 | tf_op jit(solution)/shard_map/ppermute | solution.py:319
  192.9 0.7 in_order.1
  (1 shorter events, 0.0 us)
Async XLA Ops:
  0.0 17.4 %collective-permute-start.4 = (bf16[512,128]{1,0:T(8,128)(2,1)}, bf16[512,128]{1,0:T(8,128)(2,1)S(1)}, u32[]{:S(2)}, u32[]{:S(2)}) collective-permute-start(bf16[512,128]{1,0:T(8,128)(2,1)} %bitcast.5), channel_id=1, source_target_pairs={{0,3},{1,4},{2,5},{3,6},{4,7},{5,8},{6,9},{7,10},{8,11},{9,12},{10... | collective-permute-start | bytes 393224 | tf_op jit(solution)/shard_map/ppermute | solution.py:278
  3.7 24.4 %collective-permute-start.2 = (bf16[512,128]{1,0:T(8,128)(2,1)}, bf16[512,128]{1,0:T(8,128)(2,1)S(1)}, u32[]{:S(2)}, u32[]{:S(2)}) collective-permute-start(bf16[512,128]{1,0:T(8,128)(2,1)} %bitcast.6), channel_id=1, source_target_pairs={{0,2},{1,3},{2,4},{3,5},{4,6},{5,7},{6,8},{7,9},{8,10},{9,11},{10,... | collective-permute-start | bytes 393224 | tf_op jit(solution)/shard_map/ppermute | solution.py:278
  8.0 25.4 %collective-permute-start = (bf16[512,128]{1,0:T(8,128)(2,1)}, bf16[512,128]{1,0:T(8,128)(2,1)S(1)}, u32[]{:S(2)}, u32[]{:S(2)}) collective-permute-start(bf16[512,128]{1,0:T(8,128)(2,1)} %bitcast.7), channel_id=1, source_target_pairs={{0,1},{1,2},{2,3},{3,4},{4,5},{5,6},{6,7},{7,8},{8,9},{9,10},{10,1... | collective-permute-start | bytes 393224 | tf_op jit(solution)/shard_map/ppermute | solution.py:278
  19.9 18.0 %collective-permute-start.5 = (bf16[528,128]{1,0:T(8,128)(2,1)S(1)}, bf16[528,128]{1,0:T(8,128)(2,1)S(1)}, u32[]{:S(2)}, u32[]{:S(2)}) collective-permute-start(bf16[528,128]{1,0:T(8,128)(2,1)S(1)} %later_part.5), channel_id=1, source_target_pairs={{0,61},{1,62},{2,63},{3,0},{4,1},{5,2},{6,3},{7,4},{8,5},{9,6},{10... | collective-permute-start | bytes 405512 | tf_op jit(solution)/shard_map/ppermute | solution.py:278
  30.6 7.4 %collective-permute-start.3 = (bf16[528,128]{1,0:T(8,128)(2,1)S(1)}, bf16[528,128]{1,0:T(8,128)(2,1)S(1)}, u32[]{:S(2)}, u32[]{:S(2)}) collective-permute-start(bf16[528,128]{1,0:T(8,128)(2,1)S(1)} %later_part.4), channel_id=1, source_target_pairs={{0,62},{1,63},{2,0},{3,1},{4,2},{5,3},{6,4},{7,5},{8,6},{9,7},{10,... | collective-permute-start | bytes 405512 | tf_op jit(solution)/shard_map/ppermute | solution.py:278
  35.9 41.0 %copy-start = (bf16[1024,256]{1,0:T(8,128)(2,1)S(1)}, bf16[1024,256]{1,0:T(8,128)(2,1)}, u32[]{:S(2)}) copy-start(bf16[1024,256]{1,0:T(8,128)(2,1)} %w0.1) | copy-start | bytes 1572868
  35.9 4.6 %collective-permute-start.1 = (bf16[528,128]{1,0:T(8,128)(2,1)S(1)}, bf16[528,128]{1,0:T(8,128)(2,1)S(1)}, u32[]{:S(2)}, u32[]{:S(2)}) collective-permute-start(bf16[528,128]{1,0:T(8,128)(2,1)S(1)} %later_part.3), channel_id=1, source_target_pairs={{0,63},{1,0},{2,1},{3,2},{4,3},{5,4},{6,5},{7,6},{8,7},{9,8},{10,9... | collective-permute-start | bytes 405512 | tf_op jit(solution)/shard_map/ppermute | solution.py:278
  74.9 58.5 %collective-permute-start.6 = (bf16[8,64,1024]{2,1,0:T(8,128)(2,1)S(1)}, bf16[8,64,1024]{2,1,0:T(8,128)(2,1)S(1)}, u32[]{:S(2)}, u32[]{:S(2)}) collective-permute-start(bf16[8,64,1024]{2,1,0:T(8,128)(2,1)S(1)} %all_to_all.10.own_ref), channel_id=1, source_target_pairs={{0,1},{1,0},{2,3},{3,2},{4,5},{5,4},{6,7},{7,6},{8,9},{9,8},{10,11... | collective-permute-start | bytes 3145736 | tf_op jit(solution)/shard_map/ppermute | solution.py:278
  76.9 51.9 %collective-permute-start.7 = (bf16[1024,256]{1,0:T(8,128)(2,1)S(1)}, bf16[1024,256]{1,0:T(8,128)(2,1)S(1)}, u32[]{:S(2)}, u32[]{:S(2)}) collective-permute-start(bf16[1024,256]{1,0:T(8,128)(2,1)S(1)} %copy-done), channel_id=1, source_target_pairs={{0,16},{16,32},{32,48},{48,0},{1,17},{17,33},{33,49},{49,1},{2,18}... | collective-permute-start | bytes 1572872 | tf_op jit(solution)/shard_map/ppermute | solution.py:278
  81.4 47.5 %collective-permute-start.8 = (bf16[1024,256]{1,0:T(8,128)(2,1)S(1)}, bf16[1024,256]{1,0:T(8,128)(2,1)S(1)}, u32[]{:S(2)}, u32[]{:S(2)}) collective-permute-start(bf16[1024,256]{1,0:T(8,128)(2,1)S(1)} %copy-done), channel_id=1, source_target_pairs={{0,48},{16,0},{32,16},{48,32},{1,49},{17,1},{33,17},{49,33},{2,50}... | collective-permute-start | bytes 1572872 | tf_op jit(solution)/shard_map/ppermute | solution.py:278
  84.9 48.5 %collective-permute-start.9 = (bf16[1024,256]{1,0:T(8,128)(2,1)S(1)}, bf16[1024,256]{1,0:T(8,128)(2,1)S(1)}, u32[]{:S(2)}, u32[]{:S(2)}) collective-permute-start(bf16[1024,256]{1,0:T(8,128)(2,1)S(1)} %copy-done), channel_id=1, source_target_pairs={{0,32},{16,48},{32,0},{48,16},{1,33},{17,49},{33,1},{49,17},{2,34}... | collective-permute-start | bytes 1572872 | tf_op jit(solution)/shard_map/ppermute | solution.py:278
  138.5 30.3 %all-to-all-start.1 = ((bf16[8,128,1024]{2,1,0:T(8,128)(2,1)}), bf16[8,128,1024]{2,1,0:T(8,128)(2,1)S(1)}, u32[]{:S(2)}, u32[]{:S(2)}) async-start(bf16[8,128,1024]{2,1,0:T(8,128)(2,1)} %project.1), calls=%async_computation.1 | async-start | bytes 4194304 | tf_op jit(solution)/shard_map/all_to_all | solution.py:304
  170.1 13.1 %collective-permute-start.10 = (bf16[128,256]{1,0:T(8,128)(2,1)S(1)}, bf16[128,256]{1,0:T(8,128)(2,1)S(1)}, u32[]{:S(2)}, u32[]{:S(2)}) collective-permute-start(bf16[128,256]{1,0:T(8,128)(2,1)S(1)} %get-tuple-element.17), channel_id=1, source_target_pairs={{0,0},{16,128},{32,256},{48,384},{64,64},{80,192},{96,320},{112,44... | collective-permute-start | bytes 196616 | tf_op jit(solution)/shard_map/ppermute | solution.py:319
  173.8 13.5 %collective-permute-start.11 = (bf16[128,256]{1,0:T(8,128)(2,1)S(1)}, bf16[128,256]{1,0:T(8,128)(2,1)S(1)}, u32[]{:S(2)}, u32[]{:S(2)}) collective-permute-start(bf16[128,256]{1,0:T(8,128)(2,1)S(1)} %get-tuple-element.18), channel_id=1, source_target_pairs={{0,16},{16,144},{32,272},{48,400},{64,80},{80,208},{96,336},{112,4... | collective-permute-start | bytes 196616 | tf_op jit(solution)/shard_map/ppermute | solution.py:319
  179.3 10.2 %collective-permute-start.12 = (bf16[128,256]{1,0:T(8,128)(2,1)S(1)}, bf16[128,256]{1,0:T(8,128)(2,1)S(1)}, u32[]{:S(2)}, u32[]{:S(2)}) collective-permute-start(bf16[128,256]{1,0:T(8,128)(2,1)S(1)} %get-tuple-element.19), channel_id=1, source_target_pairs={{0,32},{16,160},{32,288},{48,416},{64,96},{80,224},{96,352},{112,4... | collective-permute-start | bytes 196616 | tf_op jit(solution)/shard_map/ppermute | solution.py:319
  181.3 11.7 %collective-permute-start.13 = (bf16[128,256]{1,0:T(8,128)(2,1)S(1)}, bf16[128,256]{1,0:T(8,128)(2,1)S(1)}, u32[]{:S(2)}, u32[]{:S(2)}) collective-permute-start(bf16[128,256]{1,0:T(8,128)(2,1)S(1)} %get-tuple-element.20), channel_id=1, source_target_pairs={{0,48},{16,176},{32,304},{48,432},{64,112},{80,240},{96,368},{112,... | collective-permute-start | bytes 196616 | tf_op jit(solution)/shard_map/ppermute | solution.py:319

commit v3 on v2

--- a/solution.py
+++ b/solution.py
@@ -182,95 +182,59 @@
     )(*parts)
 
 
-def project_kernel(own_ref, other_ref, w0, w1, w2, w3, out_ref):
-    columns = w0.shape[1]
+def project_kernel(own_ref, other_ref, w_ref, out_ref):
+    rows = own_ref.shape[1]
+    core = lax.axis_index("K")
     lhs = jnp.concatenate([own_ref[0], other_ref[0]], axis=0)
-    for i, w in enumerate((w0, w1, w2, w3)):
-        out_ref[0, :, i * columns : (i + 1) * columns] = jnp.dot(
-            lhs, w[...], preferred_element_type=F32
-        ).astype(BF16)
-
-
-def project(own, other, pieces):
+    for i in range(w_ref.shape[0]):
+        part = jnp.dot(lhs, w_ref[i], preferred_element_type=F32).astype(BF16)
+        out_ref[i, 0, pl.ds(pl.multiple_of(core * rows, rows), rows), :] = part[:rows]
+        out_ref[i, 0, pl.ds(pl.multiple_of((1 - core) * rows, rows), rows), :] = part[rows:]
+
+
+def project(own, other, weights, halves):
     groups, rows, depth = own.shape
-    columns = pieces[0].shape[1]
-    half = groups // 2
-    whole = lambda w: pl.BlockSpec(w.shape, lambda i: (0, 0))
-    side = pl.BlockSpec((1, rows, depth), lambda i: ((i % 2) * half + i // 2, 0, 0))
+    pieces, _, columns = weights.shape
+    runs = groups // halves
+    side = pl.BlockSpec((1, rows, depth), lambda i, j: (i * runs + j, 0, 0))
     return pl.pallas_call(
         project_kernel,
-        grid=(groups,),
-        out_shape=pltpu.HBM((groups, 2 * rows, 4 * columns), BF16),
-        in_specs=[side, side] + [whole(w) for w in pieces],
-        out_specs=pl.BlockSpec((1, 2 * rows, 4 * columns), lambda i: (i, 0, 0)),
+        grid=(halves, runs),
+        out_shape=pltpu.HBM((pieces, halves, 2 * rows * runs, columns), BF16),
+        in_specs=[side, side, pl.BlockSpec(weights.shape, lambda i, j: (0, 0, 0))],
+        out_specs=pl.BlockSpec((pieces, 1, 2 * rows, columns), lambda i, j: (0, i, j, 0)),
         compiler_params=pltpu.CompilerParams(vmem_limit_bytes=24 << 20),
         cost_estimate=pl.CostEstimate(
-            flops=16 * groups * rows * depth * columns,
+            flops=4 * groups * rows * depth * columns * pieces,
             bytes_accessed=6 << 20,
             transcendentals=0,
         ),
         name="project",
-    )(own, other, *pieces)
-
-
-def total_kernel(place, in_ref, *out_refs):
-    half = in_ref.shape[1] // 2
+    )(own, other, weights)
+
+
+def total_kernel(in_ref, out_ref):
     total = in_ref[0].astype(F32)
     for i in range(1, in_ref.shape[0]):
         total += in_ref[i].astype(F32)
-    total = total.astype(BF16)
-    core = lax.axis_index("K")
-    for k, out_ref in enumerate(out_refs):
-
-        @pl.when(pl.program_id(0) == k)
-        def _():
-            out_ref[pl.ds(pl.multiple_of(core * half, half), half), :] = total[:half]
-            out_ref[pl.ds(pl.multiple_of((1 - core) * half, half), half), :] = total[half:]
-
-
-def totals(place, received, count):
-    sources, rows, width = received.shape
-    columns = width // count
+    out_ref[...] = total.astype(BF16)
+
+
+def totals(received, steps):
+    sources, rows, columns = received.shape
+    step = rows // steps
     return pl.pallas_call(
         total_kernel,
-        grid_spec=pltpu.PrefetchScalarGridSpec(
-            num_scalar_prefetch=1,
-            grid=(count,),
-            in_specs=[pl.BlockSpec((sources, rows, columns), lambda i, place: (0, 0, place[i]))],
-            out_specs=[pl.BlockSpec((rows, columns), lambda i, place: (0, 0))] * count,
-        ),
-        out_shape=[jax.ShapeDtypeStruct((rows, columns), BF16)] * count,
+        grid=(steps,),
+        out_shape=jax.ShapeDtypeStruct((rows, columns), BF16),
+        in_specs=[pl.BlockSpec((sources, step, columns), lambda i: (0, i, 0))],
+        out_specs=pl.BlockSpec((step, columns), lambda i: (i, 0)),
         compiler_params=pltpu.CompilerParams(vmem_limit_bytes=16 << 20),
         cost_estimate=pl.CostEstimate(
-            flops=sources * rows * width, bytes_accessed=3 << 20, transcendentals=0
+            flops=sources * rows * columns, bytes_accessed=3 << 20, transcendentals=0
         ),
         name="totals",
-    )(place, received)
-
-
-def order_kernel(*refs):
-    pieces, out_ref = refs[:-1], refs[-1]
-    count = len(pieces)
-    rows = pieces[0].shape[0]
-    own = lax.axis_index("Y")
-    for k, piece in enumerate(pieces):
-        slot = lax.rem(own + (count - k), count)
-        out_ref[pl.ds(pl.multiple_of(slot * rows, rows), rows), :] = piece[...]
-
-
-def in_order(pieces):
-    rows, columns = pieces[0].shape
-    return pl.pallas_call(
-        order_kernel,
-        out_shape=jax.ShapeDtypeStruct((len(pieces) * rows, columns), BF16),
-        in_specs=[VMEM] * len(pieces),
-        out_specs=VMEM,
-        compiler_params=pltpu.CompilerParams(vmem_limit_bytes=4 << 20),
-        cost_estimate=pl.CostEstimate(
-            flops=1 << 18, bytes_accessed=1 << 19, transcendentals=0
-        ),
-        name="in_order",
-    )(*pieces)
+    )(received)
 
 
 def passed_along(value, axis, steps):
@@ -279,16 +243,14 @@
 
 
 def on_device(queries, prefix_keys, cached_prefix_values, shard_len, reach, w_out):
-    y_count, z_count, _ = (lax.axis_size(a) for a in BLK)
+    y_count, z_count = lax.axis_size("Y"), lax.axis_size("Z")
     tokens, heads, head_size = queries.shape
     q_own = queries.reshape(tokens * heads, head_size)
 
     visitors = []
     for j in range(1, SPAN):
         visitors.append(passed_along(q_own, BLK, j))
-    w_before = passed_along(w_out, "Y", 1)
-    w_after = passed_along(w_out, "Y", -1)
-    w_far = passed_along(w_out, "Y", 2)
+    weights = lax.all_gather(w_out, "Y", axis=0, tiled=False)
 
     part, keys, values, meta = first_part(
         tokens, shard_len, reach, q_own, prefix_keys[0], cached_prefix_values[0]
@@ -300,24 +262,19 @@
     spread = combine(parts, z_count, tokens, heads)
     own = lax.all_to_all(spread, "Z", split_axis=0, concat_axis=0, tiled=True)
     other = passed_along(own, "K", 1)
-    partial = project(own, other, (w_out, w_before, w_after, w_far))
+    x_half = lax.axis_size("x") // 2
+    partial = project(own, other, weights, 2)
+    partial = partial.reshape(-1, *partial.shape[2:])
     received = lax.all_to_all(partial, HEADS, split_axis=0, concat_axis=0, tiled=True)
-    x_half = lax.axis_size("x") // 2
-    held = lax.axis_index("y") * x_half + lax.axis_index("x") // 2
-    shift = (held + jnp.arange(y_count, dtype=jnp.int32) - lax.axis_index("Y")) % y_count
-    place = jnp.where(shift == 0, 0, jnp.where(shift == y_count - 1, 1, shift + 1))
-    summed = totals(place.astype(jnp.int32), received, y_count)
-    moved = []
-    for k in range(y_count):
-        pairs = []
-        for y in range(lax.axis_size("y")):
-            for x in range(lax.axis_size("x")):
-                for big in range(y_count):
-                    target = (y * x_half + x // 2 + k) % y_count
-                    group = (big // x_half) * 2 * x_half + (big % x_half) * 2 + x % 2
-                    pairs.append(((y * 2 * x_half + x) * y_count + big, group * y_count + target))
-        moved.append(lax.ppermute(summed[k], ("y", "x", "Y"), pairs))
-    return in_order(moved)
+    summed = totals(received, 4)
+    pairs = []
+    for y in range(lax.axis_size("y")):
+        for x in range(lax.axis_size("x")):
+            for big in range(y_count):
+                head = (big // x_half) * 2 * x_half + (big % x_half) * 2 + x % 2
+                target = head * y_count + y * x_half + x // 2
+                pairs.append(((y * 2 * x_half + x) * y_count + big, target))
+    return lax.ppermute(summed, ("y", "x", "Y"), pairs)
 
 
 def solution(mesh):

time: 194 us -> 166 us (0.86)
  the two profiles are of different devices: /device:TPU:8 before, /device:TPU:59 now
where the time goes in v3:
time: 166 us; the launch traced here: 165 us
  blocking collectives  70.5 us (42%)
  waiting for transfers between devices  32.5 us (20%)
  starting transfers between devices  29.1 us (18%)
  Pallas kernels  17.1 us (10%)
  between operations  13.5 us (8%)
  local copies, waits for them, and re-layouts  2.29 us (1%)
    all_to_all x1, blocking collectives, on_device(): own = lax.all_to_all(spread, 'Z', split_axis=0, concat_axis=0, tiled=True)  38.3 us
    all_to_all x1, blocking collectives, on_device(): lax.all_to_all(partial, HEADS, split_axis=0, concat_axis=0, tiled=True)  32.2 us
    ppermute x7, starting transfers between devices, passed_along(): lax.ppermute(value, axis, [(i, (i + steps) % count) for i in range(count)])  27.2 us
    ppermute x1, waiting for transfers between devices, on_device(): return lax.ppermute(summed, ('y', 'x', 'Y'), pairs)  17 us
    ppermute x7, waiting for transfers between devices, passed_along(): lax.ppermute(value, axis, [(i, (i + steps) % count) for i in range(count)])  15.4 us
    pallas_call x3, Pallas kernels, later_part(): pl.pallas_call(functools.partial(part_body, offset, tokens), out_shape=ja...  7.32 us
    pallas_call x1, Pallas kernels, project(): pl.pallas_call(project_kernel, grid=(halves, runs), out_shape=pltpu.HBM((...  5.11 us
    pallas_call x1, Pallas kernels, first_part(): pl.pallas_call(functools.partial(first_kernel, tokens), out_shape=(jax.Sh...  3.75 us
  transfers between devices with their start and end apart: 9, of which 5 were waited for; matrix products, arithmetic and copies ran while one was open for 0% of the time, Pallas kernels for 7%

profile of v3, /device:TPU:59, one launch (start us, length us, event | category | flops | bytes accessed | tf_op | source)
XLA Modules:
  0.0 165.1 jit_solution(9689091223194278995)
XLA Ops:
  6.5 0.0 all-gather.3.cloned.1.call-start
  6.5 4.5 %collective-permute-start = (bf16[512,128]{1,0:T(8,128)(2,1)}, bf16[512,128]{1,0:T(8,128)(2,1)S(1)}, u32[]{:S(2)}, u32[]{:S(2)}) collective-permute-start(bf16[512,128]{1,0:T(8,128)(2,1)} %bitcast.9), channel_id=1, source_target_pairs={{0,1},{1,2},{2,3},{3,4},{4,5},{5,6},{6,7},{7,8},{8,9},{9,10},{10,1... | collective-permute-start | bytes 393224 | tf_op jit(solution)/shard_map/ppermute | solution.py:242
  11.1 4.0 %collective-permute-start.2 = (bf16[512,128]{1,0:T(8,128)(2,1)}, bf16[512,128]{1,0:T(8,128)(2,1)S(1)}, u32[]{:S(2)}, u32[]{:S(2)}) collective-permute-start(bf16[512,128]{1,0:T(8,128)(2,1)} %bitcast.10), channel_id=1, source_target_pairs={{0,2},{1,3},{2,4},{3,5},{4,6},{5,7},{6,8},{7,9},{8,10},{9,11},{10,... | collective-permute-start | bytes 393224 | tf_op jit(solution)/shard_map/ppermute | solution.py:242
  15.1 4.0 %collective-permute-start.4 = (bf16[512,128]{1,0:T(8,128)(2,1)}, bf16[512,128]{1,0:T(8,128)(2,1)S(1)}, u32[]{:S(2)}, u32[]{:S(2)}) collective-permute-start(bf16[512,128]{1,0:T(8,128)(2,1)} %bitcast.11), channel_id=1, source_target_pairs={{0,3},{1,4},{2,5},{3,6},{4,7},{5,8},{6,9},{7,10},{8,11},{9,12},{10... | collective-permute-start | bytes 393224 | tf_op jit(solution)/shard_map/ppermute | solution.py:242
  19.1 0.0 all-gather.3.cloned.1.call-update
  19.1 3.7 %first_part.1 = (bf16[528,128]{1,0:T(8,128)(2,1)S(1)}, bf16[2048,128]{1,0:T(8,128)(2,1)S(1)}, bf16[2048,128]{1,0:T(8,128)(2,1)S(1)}, s32[8,128]{1,0:T(8,128)S(1)}) custom-call(s32[64]{0:T(128)} %refs_0_.1, s32[64]{0:T(128)} %refs_1_.1, bf16[512,128]{1,0:T(8,128)(2,1)} %bitcast.12, bf16[2048,128]{1,0:T(8,128)(2,1)} %bitcast.7, bf16[2048,128]{1,0:T(8,128)(2,1)} %bitcast.8), custom_call_target="tpu_custom_call" | custom-call | flops 536870912 | bytes 1048576 | tf_op jit(solution)/shard_map/first_part/pallas_call | solution.py:101
  22.9 0.0 collective-permute-done.q_ref
  22.9 2.4 %later_part.3 = bf16[528,128]{1,0:T(8,128)(2,1)S(1)} custom-call(s32[8,128]{1,0:T(8,128)S(1)} %get-tuple-element.10.meta_ref, bf16[512,128]{1,0:T(8,128)(2,1)S(1)} %collective-permute-done.q_ref, bf16[2048,128]{1,0:T(8,128)(2,1)S(1)} %get-tuple-element.11.k_ref, bf16[2048,128]{1,0:T(8,128)(2,1)S(1)} %get-tuple-element.12.v_ref), custom_call_target="tpu_custom_call" | custom-call | flops 536870912 | bytes 1048576 | tf_op jit(solution)/shard_map/later_part/pallas_call | solution.py:126
  25.4 3.2 %collective-permute-start.1 = (bf16[528,128]{1,0:T(8,128)(2,1)S(1)}, bf16[528,128]{1,0:T(8,128)(2,1)S(1)}, u32[]{:S(2)}, u32[]{:S(2)}) collective-permute-start(bf16[528,128]{1,0:T(8,128)(2,1)S(1)} %later_part.3), channel_id=1, source_target_pairs={{0,63},{1,0},{2,1},{3,2},{4,3},{5,4},{6,5},{7,6},{8,7},{9,8},{10,9... | collective-permute-start | bytes 405512 | tf_op jit(solution)/shard_map/ppermute | solution.py:242
  28.5 0.6 collective-permute-done.2.q_ref
  29.1 2.4 %later_part.4 = bf16[528,128]{1,0:T(8,128)(2,1)S(1)} custom-call(s32[8,128]{1,0:T(8,128)S(1)} %get-tuple-element.10.meta_ref, bf16[512,128]{1,0:T(8,128)(2,1)S(1)} %collective-permute-done.2.q_ref, bf16[2048,128]{1,0:T(8,128)(2,1)S(1)} %get-tuple-element.11.k_ref, bf16[2048,128]{1,0:T(8,128)(2,1)S(1)} %get-tuple-element.12.v_ref), custom_call_target="tpu_custom_call" | custom-call | flops 536870912 | bytes 1048576 | tf_op jit(solution)/shard_map/later_part/pallas_call | solution.py:126
  31.5 4.3 %collective-permute-start.3 = (bf16[528,128]{1,0:T(8,128)(2,1)S(1)}, bf16[528,128]{1,0:T(8,128)(2,1)S(1)}, u32[]{:S(2)}, u32[]{:S(2)}) collective-permute-start(bf16[528,128]{1,0:T(8,128)(2,1)S(1)} %later_part.4), channel_id=1, source_target_pairs={{0,62},{1,63},{2,0},{3,1},{4,2},{5,3},{6,4},{7,5},{8,6},{9,7},{10,... | collective-permute-start | bytes 405512 | tf_op jit(solution)/shard_map/ppermute | solution.py:242
  35.8 0.0 collective-permute-done.4.q_ref
  35.8 2.4 %later_part.5 = bf16[528,128]{1,0:T(8,128)(2,1)S(1)} custom-call(s32[8,128]{1,0:T(8,128)S(1)} %get-tuple-element.10.meta_ref, bf16[512,128]{1,0:T(8,128)(2,1)S(1)} %collective-permute-done.4.q_ref, bf16[2048,128]{1,0:T(8,128)(2,1)S(1)} %get-tuple-element.11.k_ref, bf16[2048,128]{1,0:T(8,128)(2,1)S(1)} %get-tuple-element.12.v_ref), custom_call_target="tpu_custom_call" | custom-call | flops 536870912 | bytes 1048576 | tf_op jit(solution)/shard_map/later_part/pallas_call | solution.py:126
  38.3 5.3 %collective-permute-start.5 = (bf16[528,128]{1,0:T(8,128)(2,1)S(1)}, bf16[528,128]{1,0:T(8,128)(2,1)S(1)}, u32[]{:S(2)}, u32[]{:S(2)}) collective-permute-start(bf16[528,128]{1,0:T(8,128)(2,1)S(1)} %later_part.5), channel_id=1, source_target_pairs={{0,61},{1,62},{2,63},{3,0},{4,1},{5,2},{6,3},{7,4},{8,5},{9,6},{10... | collective-permute-start | bytes 405512 | tf_op jit(solution)/shard_map/ppermute | solution.py:242
  43.6 0.0 collective-permute-done.1.refs_1_
  43.6 1.7 %collective-permute-done.3.refs_2_ = bf16[528,128]{1,0:T(8,128)(2,1)S(1)} collective-permute-done((bf16[528,128]{1,0:T(8,128)(2,1)S(1)}, bf16[528,128]{1,0:T(8,128)(2,1)S(1)}, u32[]{:S(2)}, u32[]{:S(2)}) %collective-permute-start.3) | collective-permute-done | bytes 135200 | tf_op jit(solution)/shard_map/ppermute | solution.py:242
  45.3 10.5 %collective-permute-done.5.refs_3_ = bf16[528,128]{1,0:T(8,128)(2,1)S(1)} collective-permute-done((bf16[528,128]{1,0:T(8,128)(2,1)S(1)}, bf16[528,128]{1,0:T(8,128)(2,1)S(1)}, u32[]{:S(2)}, u32[]{:S(2)}) %collective-permute-start.5) | collective-permute-done | bytes 135200 | tf_op jit(solution)/shard_map/ppermute | solution.py:242
  55.9 0.5 combine.1
  56.3 38.3 %all_to_all.10.own_ref = bf16[8,64,1024]{2,1,0:T(8,128)(2,1)S(1)} all-to-all(bf16[8,64,1024]{2,1,0:T(8,128)(2,1)S(1)} %combine.1), channel_id=1, replica_groups=mesh['y'=2,'x'=4,'Y'=4,'Z'=8,'K'=2] {'Z'}, dimensions={0} | all-to-all | bytes 2097152 | tf_op jit(solution)/shard_map/all_to_all | solution.py:263
  94.7 1.9 %collective-permute-start.6 = (bf16[8,64,1024]{2,1,0:T(8,128)(2,1)S(1)}, bf16[8,64,1024]{2,1,0:T(8,128)(2,1)S(1)}, u32[]{:S(2)}, u32[]{:S(2)}) collective-permute-start(bf16[8,64,1024]{2,1,0:T(8,128)(2,1)S(1)} %all_to_all.10.own_ref), channel_id=1, source_target_pairs={{0,1},{1,0},{2,3},{3,2},{4,5},{5,4},{6,7},{7,6},{8,9},{9,8},{10,11... | collective-permute-start | bytes 3145736 | tf_op jit(solution)/shard_map/ppermute | solution.py:242
  96.6 0.0 all-gather.3.cloned.1.call-done
  96.6 2.6 %collective-permute-done.6.other_ref = bf16[8,64,1024]{2,1,0:T(8,128)(2,1)S(1)} collective-permute-done((bf16[8,64,1024]{2,1,0:T(8,128)(2,1)S(1)}, bf16[8,64,1024]{2,1,0:T(8,128)(2,1)S(1)}, u32[]{:S(2)}, u32[]{:S(2)}) %collective-permute-start.6) | collective-permute-done | bytes 1048608 | tf_op jit(solution)/shard_map/ppermute | solution.py:242
  99.2 0.0 copy-start
  99.2 1.6 copy-done
  100.8 5.1 %project.1 = bf16[4,2,512,256]{3,2,1,0:T(8,128)(2,1)} custom-call(bf16[8,64,1024]{2,1,0:T(8,128)(2,1)S(1)} %all_to_all.10.own_ref, bf16[8,64,1024]{2,1,0:T(8,128)(2,1)S(1)} %collective-permute-done.6.other_ref, bf16[4,1024,256]{2,1,0:T(8,128)(2,1)S(1)} %bitcast.5), custom_call_target="tpu_custom_call" | custom-call | flops 2147483648 | bytes 6291456 | tf_op jit(solution)/shard_map/project/pallas_call | solution.py:200
  105.9 32.2 %all_to_all.11.in_ref = bf16[8,512,256]{2,1,0:T(8,128)(2,1)S(1)} all-to-all(bf16[8,512,256]{2,1,0:T(8,128)(2,1)} %bitcast.6), channel_id=1, replica_groups=mesh['y'=2,'x'=4,'Y'=4,'Z'=8,'K'=2] {'y','x'}, dimensions={0} | all-to-all | bytes 4194304 | tf_op jit(solution)/shard_map/all_to_all | solution.py:268
  138.1 0.5 totals.1
  138.6 1.9 %collective-permute-start.7 = (bf16[512,256]{1,0:T(8,128)(2,1)S(1)}, bf16[512,256]{1,0:T(8,128)(2,1)S(1)}, u32[]{:S(2)}, u32[]{:S(2)}) collective-permute-start(bf16[512,256]{1,0:T(8,128)(2,1)S(1)} %totals.1), channel_id=1, source_target_pairs={{0,0},{16,128},{32,256},{48,384},{64,64},{80,192},{96,320},{112,44... | collective-permute-start | bytes 786440 | tf_op jit(solution)/shard_map/ppermute | solution.py:277
  140.5 17.0 %collective-permute-done.7 = bf16[512,256]{1,0:T(8,128)(2,1)S(1)} collective-permute-done((bf16[512,256]{1,0:T(8,128)(2,1)S(1)}, bf16[512,256]{1,0:T(8,128)(2,1)S(1)}, u32[]{:S(2)}, u32[]{:S(2)}) %collective-permute-start.7) | collective-permute-done | bytes 262176 | tf_op jit(solution)/shard_map/ppermute | solution.py:277
  157.5 0.7 copy.8
Async XLA Ops:
  6.5 90.1 %all-gather.3.cloned.1.call-start = ((), (), s32[]{:S(2)}) async-start(), calls=%async_computation.2 | async-start | bytes 2621440 | tf_op jit(solution)/shard_map/all_gather | solution.py:253
  6.5 16.4 %collective-permute-start = (bf16[512,128]{1,0:T(8,128)(2,1)}, bf16[512,128]{1,0:T(8,128)(2,1)S(1)}, u32[]{:S(2)}, u32[]{:S(2)}) collective-permute-start(bf16[512,128]{1,0:T(8,128)(2,1)} %bitcast.9), channel_id=1, source_target_pairs={{0,1},{1,2},{2,3},{3,4},{4,5},{5,6},{6,7},{7,8},{8,9},{9,10},{10,1... | collective-permute-start | bytes 393224 | tf_op jit(solution)/shard_map/ppermute | solution.py:242
  11.1 18.0 %collective-permute-start.2 = (bf16[512,128]{1,0:T(8,128)(2,1)}, bf16[512,128]{1,0:T(8,128)(2,1)S(1)}, u32[]{:S(2)}, u32[]{:S(2)}) collective-permute-start(bf16[512,128]{1,0:T(8,128)(2,1)} %bitcast.10), channel_id=1, source_target_pairs={{0,2},{1,3},{2,4},{3,5},{4,6},{5,7},{6,8},{7,9},{8,10},{9,11},{10,... | collective-permute-start | bytes 393224 | tf_op jit(solution)/shard_map/ppermute | solution.py:242
  15.1 20.7 %collective-permute-start.4 = (bf16[512,128]{1,0:T(8,128)(2,1)}, bf16[512,128]{1,0:T(8,128)(2,1)S(1)}, u32[]{:S(2)}, u32[]{:S(2)}) collective-permute-start(bf16[512,128]{1,0:T(8,128)(2,1)} %bitcast.11), channel_id=1, source_target_pairs={{0,3},{1,4},{2,5},{3,6},{4,7},{5,8},{6,9},{7,10},{8,11},{9,12},{10... | collective-permute-start | bytes 393224 | tf_op jit(solution)/shard_map/ppermute | solution.py:242
  25.4 18.2 %collective-permute-start.1 = (bf16[528,128]{1,0:T(8,128)(2,1)S(1)}, bf16[528,128]{1,0:T(8,128)(2,1)S(1)}, u32[]{:S(2)}, u32[]{:S(2)}) collective-permute-start(bf16[528,128]{1,0:T(8,128)(2,1)S(1)} %later_part.3), channel_id=1, source_target_pairs={{0,63},{1,0},{2,1},{3,2},{4,3},{5,4},{6,5},{7,6},{8,7},{9,8},{10,9... | collective-permute-start | bytes 405512 | tf_op jit(solution)/shard_map/ppermute | solution.py:242
  31.5 13.8 %collective-permute-start.3 = (bf16[528,128]{1,0:T(8,128)(2,1)S(1)}, bf16[528,128]{1,0:T(8,128)(2,1)S(1)}, u32[]{:S(2)}, u32[]{:S(2)}) collective-permute-start(bf16[528,128]{1,0:T(8,128)(2,1)S(1)} %later_part.4), channel_id=1, source_target_pairs={{0,62},{1,63},{2,0},{3,1},{4,2},{5,3},{6,4},{7,5},{8,6},{9,7},{10,... | collective-permute-start | bytes 405512 | tf_op jit(solution)/shard_map/ppermute | solution.py:242
  38.3 17.6 %collective-permute-start.5 = (bf16[528,128]{1,0:T(8,128)(2,1)S(1)}, bf16[528,128]{1,0:T(8,128)(2,1)S(1)}, u32[]{:S(2)}, u32[]{:S(2)}) collective-permute-start(bf16[528,128]{1,0:T(8,128)(2,1)S(1)} %later_part.5), channel_id=1, source_target_pairs={{0,61},{1,62},{2,63},{3,0},{4,1},{5,2},{6,3},{7,4},{8,5},{9,6},{10... | collective-permute-start | bytes 405512 | tf_op jit(solution)/shard_map/ppermute | solution.py:242
  94.7 4.5 %collective-permute-start.6 = (bf16[8,64,1024]{2,1,0:T(8,128)(2,1)S(1)}, bf16[8,64,1024]{2,1,0:T(8,128)(2,1)S(1)}, u32[]{:S(2)}, u32[]{:S(2)}) collective-permute-start(bf16[8,64,1024]{2,1,0:T(8,128)(2,1)S(1)} %all_to_all.10.own_ref), channel_id=1, source_target_pairs={{0,1},{1,0},{2,3},{3,2},{4,5},{5,4},{6,7},{7,6},{8,9},{9,8},{10,11... | collective-permute-start | bytes 3145736 | tf_op jit(solution)/shard_map/ppermute | solution.py:242
  99.2 1.6 copy-start
  138.6 18.9 %collective-permute-start.7 = (bf16[512,256]{1,0:T(8,128)(2,1)S(1)}, bf16[512,256]{1,0:T(8,128)(2,1)S(1)}, u32[]{:S(2)}, u32[]{:S(2)}) collective-permute-start(bf16[512,256]{1,0:T(8,128)(2,1)S(1)} %totals.1), channel_id=1, source_target_pairs={{0,0},{16,128},{32,256},{48,384},{64,64},{80,192},{96,320},{112,44... | collective-permute-start | bytes 786440 | tf_op jit(solution)/shard_map/ppermute | solution.py:277
Sparse Core Ops, SparseCore 0:
  19.3 63.1 all-gather.2

commit v4 on v3

--- a/solution.py
+++ b/solution.py
@@ -9,7 +9,6 @@
 from jax.sharding import Mesh
 from jax.sharding import PartitionSpec as P
 
-SPAN = 4
 HEADS = ("y", "x")
 BLK = ("Y", "Z", "K")
 TILE = 128
@@ -24,28 +23,32 @@
     return rows == lanes
 
 
-def part_body(offset, tokens, meta_ref, q_ref, k_ref, v_ref, out_ref):
+def part_body(q_ref, shards, out_ref, tokens):
     rows, head_size = q_ref.shape
     scale = head_size**-0.5 * math.log2(math.e)
     eye = eye_mask()
-    length = meta_ref[SPAN : SPAN + 1, 0:1]
-    base = meta_ref[offset : offset + 1, 0:1]
     stats = []
     for start in range(0, rows, TILE):
-        scores = lax.dot_general(
-            q_ref[start : start + TILE, :],
-            k_ref[...],
-            (((1,), (1,)), ((), ())),
-            preferred_element_type=F32,
+        row = start + lax.broadcasted_iota(jnp.int32, (TILE, 1), 0)
+        scored = []
+        for k_ref, _, length, base in shards:
+            scores = lax.dot_general(
+                q_ref[start : start + TILE, :],
+                k_ref[...],
+                (((1,), (1,)), ((), ())),
+                preferred_element_type=F32,
+            )
+            limit = jnp.minimum(length, base + row // (rows // tokens))
+            slot = lax.broadcasted_iota(jnp.int32, scores.shape, 1)
+            scored.append(jnp.where(slot < limit, scores, NONE))
+        top = functools.reduce(
+            jnp.maximum, [jnp.max(scores, axis=1, keepdims=True) for scores in scored]
         )
-        row = start + lax.broadcasted_iota(jnp.int32, (TILE, 1), 0)
-        limit = jnp.minimum(length, base + row // (rows // tokens))
-        slot = lax.broadcasted_iota(jnp.int32, scores.shape, 1)
-        scores = jnp.where(slot < limit, scores, NONE)
-        top = jnp.max(scores, axis=1, keepdims=True)
-        weights = jnp.exp2((scores - top) * scale)
-        total = jnp.sum(weights, axis=1, keepdims=True)
-        values = jnp.dot(weights.astype(BF16), v_ref[...], preferred_element_type=F32)
+        total, values = 0.0, 0.0
+        for scores, (_, v_ref, _, _) in zip(scored, shards):
+            weights = jnp.exp2((scores - top) * scale)
+            total += jnp.sum(weights, axis=1, keepdims=True)
+            values += jnp.dot(weights.astype(BF16), v_ref[...], preferred_element_type=F32)
         seen = top > 0.1 * NONE
         out_ref[start : start + TILE, :] = jnp.where(seen, values / total, 0.0).astype(BF16)
         level = jnp.where(seen, top * scale + jnp.log2(total), NONE)
@@ -60,6 +63,10 @@
     ).astype(BF16)
 
 
+def known(meta_ref, i):
+    return meta_ref[i : i + 1, 0:1]
+
+
 def first_kernel(tokens, *refs):
     out_ref, k_ref, v_ref, meta_ref, lengths, reaches, q_ref, sems = refs[5:]
     copies = [
@@ -71,16 +78,40 @@
     copies[0].wait()
     copies[1].wait()
     count = lengths.shape[0]
-    own_index = lax.axis_index(BLK)
+    slots = k_ref.shape[0]
+    own = lax.axis_index(BLK)
+    core = lax.axis_index("K")
+    reach = lambda back: reaches[lax.rem(own + (count - back), count)]
+    facts = (
+        lengths[own],
+        lengths[own + 1 - 2 * core],
+        reach(0),
+        reach(2) - 2 * slots,
+        reach(2) - (3 - 2 * core) * slots,
+        reach(4 * core) - (1 + 2 * core) * slots,
+    )
     row = lax.broadcasted_iota(jnp.int32, meta_ref.shape, 0)
-    meta = jnp.full(meta_ref.shape, lengths[own_index], jnp.int32)
-    for j in range(SPAN):
-        base = reaches[lax.rem(own_index + (count - j), count)] - j * k_ref.shape[0]
-        meta = jnp.where(row == j, base, meta)
+    meta = jnp.zeros(meta_ref.shape, jnp.int32)
+    for i, fact in enumerate(facts):
+        meta = jnp.where(row == i, fact, meta)
     meta_ref[...] = meta
     for copy in copies[2:]:
         copy.wait()
-    part_body(0, tokens, meta_ref, q_ref, k_ref, v_ref, out_ref)
+    part_body(q_ref, [(k_ref, v_ref, known(meta_ref, 0), known(meta_ref, 2))], out_ref, tokens)
+
+
+def second_kernel(tokens, meta_ref, q_ref, k_ref, v_ref, k_other, v_other, out_ref):
+    shards = [
+        (k_ref, v_ref, known(meta_ref, 0), known(meta_ref, 3)),
+        (k_other, v_other, known(meta_ref, 1), known(meta_ref, 4)),
+    ]
+    part_body(q_ref, shards, out_ref, tokens)
+
+
+def third_kernel(tokens, meta_ref, q_own, q_visit, k_other, v_other, out_ref, q_ref):
+    q_ref[...] = jnp.where(lax.axis_index("K") == 0, q_own[...], q_visit[...])
+    shards = [(k_other, v_other, known(meta_ref, 1), known(meta_ref, 5))]
+    part_body(q_ref, shards, out_ref, tokens)
 
 
 def part_cost(rows, slots, head_size):
@@ -120,18 +151,18 @@
     )(*(pltpu.with_memory_space_constraint(a, pltpu.HBM) for a in (lengths, reaches, q, k, v)))
 
 
-def later_part(tokens, offset, meta, q, k, v):
-    rows, head_size = q.shape
+def later_part(kernel, tokens, slots, scratch, *arrays):
+    rows, head_size = arrays[1].shape
     extra = 4 * (rows // TILE)
     return pl.pallas_call(
-        functools.partial(part_body, offset, tokens),
+        functools.partial(kernel, tokens),
         out_shape=jax.ShapeDtypeStruct((rows + extra, head_size), BF16),
-        in_specs=[VMEM] * 4,
+        in_specs=[VMEM] * len(arrays),
         out_specs=VMEM,
+        scratch_shapes=scratch,
         compiler_params=pltpu.CompilerParams(vmem_limit_bytes=24 << 20),
-        cost_estimate=part_cost(rows, k.shape[0], head_size),
-        name="later_part",
-    )(meta, q, k, v)
+        cost_estimate=part_cost(rows, slots, head_size),
+    )(*arrays)
 
 
 def combine_kernel(*refs):
@@ -140,9 +171,17 @@
     head_size = parts[0].shape[1]
     groups = parts[0].shape[0] // (TILE + 4)
     rows = groups * TILE
+    south = lax.axis_index("K") == 0
+
+    def taken(part, start, stop):
+        if isinstance(part, tuple):
+            return jnp.where(south, part[0][start:stop, :], part[1][start:stop, :])
+        return part[start:stop, :]
+
+    parts = list(parts[:-2]) + [tuple(parts[-2:])]
     levels = []
     for part in parts:
-        terms = part[rows:, :].astype(F32)
+        terms = taken(part, rows, rows + 4 * groups).astype(F32)
         levels.append(
             terms[:groups] + terms[groups : 2 * groups] + terms[2 * groups : 3 * groups]
         )
@@ -155,7 +194,7 @@
         for part, factor in zip(parts, factors):
             line = jnp.broadcast_to((factor * inverse)[group : group + 1, :], (TILE, TILE))
             column = jnp.sum(jnp.where(eye, line, 0.0), axis=1, keepdims=True)
-            term = part[group * TILE : (group + 1) * TILE, :].astype(F32) * column
+            term = taken(part, group * TILE, (group + 1) * TILE).astype(F32) * column
             total = term if total is None else total + term
         total_ref[group * TILE : (group + 1) * TILE, :] = total
     heads = rows // tokens
@@ -182,35 +221,34 @@
     )(*parts)
 
 
-def project_kernel(own_ref, other_ref, w_ref, out_ref):
-    rows = own_ref.shape[1]
-    core = lax.axis_index("K")
-    lhs = jnp.concatenate([own_ref[0], other_ref[0]], axis=0)
+def project_kernel(side_ref, w_ref, out_ref):
+    count, rows, depth = side_ref.shape
+    lhs = side_ref[...].reshape(count * rows, depth)
     for i in range(w_ref.shape[0]):
-        part = jnp.dot(lhs, w_ref[i], preferred_element_type=F32).astype(BF16)
-        out_ref[i, 0, pl.ds(pl.multiple_of(core * rows, rows), rows), :] = part[:rows]
-        out_ref[i, 0, pl.ds(pl.multiple_of((1 - core) * rows, rows), rows), :] = part[rows:]
-
-
-def project(own, other, weights, halves):
-    groups, rows, depth = own.shape
+        out_ref[i, 0] = jnp.dot(lhs, w_ref[i], preferred_element_type=F32).astype(BF16)
+
+
+def project(side, weights, halves):
+    groups, rows, depth = side.shape
     pieces, _, columns = weights.shape
     runs = groups // halves
-    side = pl.BlockSpec((1, rows, depth), lambda i, j: (i * runs + j, 0, 0))
     return pl.pallas_call(
         project_kernel,
-        grid=(halves, runs),
-        out_shape=pltpu.HBM((pieces, halves, 2 * rows * runs, columns), BF16),
-        in_specs=[side, side, pl.BlockSpec(weights.shape, lambda i, j: (0, 0, 0))],
+        grid=(halves, runs // 2),
+        out_shape=pltpu.HBM((pieces, halves, rows * runs, columns), BF16),
+        in_specs=[
+            pl.BlockSpec((2, rows, depth), lambda i, j: (i * (runs // 2) + j, 0, 0)),
+            pl.BlockSpec(weights.shape, lambda i, j: (0, 0, 0)),
+        ],
         out_specs=pl.BlockSpec((pieces, 1, 2 * rows, columns), lambda i, j: (0, i, j, 0)),
         compiler_params=pltpu.CompilerParams(vmem_limit_bytes=24 << 20),
         cost_estimate=pl.CostEstimate(
-            flops=4 * groups * rows * depth * columns * pieces,
-            bytes_accessed=6 << 20,
+            flops=2 * groups * rows * depth * columns * pieces,
+            bytes_accessed=4 << 20,
             transcendentals=0,
         ),
         name="project",
-    )(own, other, weights)
+    )(side, weights)
 
 
 def total_kernel(in_ref, out_ref):
@@ -237,6 +275,30 @@
     )(received)
 
 
+def order_kernel(runs, own_ref, other_ref, out_ref):
+    rows = own_ref.shape[0] // runs
+    core = lax.axis_index("K")
+    for i in range(runs):
+        for ref, slot in ((own_ref, core), (other_ref, 1 - core)):
+            start = pl.multiple_of(slot * rows + 2 * i * rows, rows)
+            out_ref[pl.ds(start, rows), :] = ref[i * rows : (i + 1) * rows, :]
+
+
+def in_order(runs, own, other):
+    rows, columns = own.shape
+    return pl.pallas_call(
+        functools.partial(order_kernel, runs),
+        out_shape=jax.ShapeDtypeStruct((2 * rows, columns), BF16),
+        in_specs=[VMEM] * 2,
+        out_specs=VMEM,
+        compiler_params=pltpu.CompilerParams(vmem_limit_bytes=4 << 20),
+        cost_estimate=pl.CostEstimate(
+            flops=1 << 18, bytes_accessed=1 << 19, transcendentals=0
+        ),
+        name="in_order",
+    )(own, other)
+
+
 def passed_along(value, axis, steps):
     count = lax.axis_size(axis)
     return lax.ppermute(value, axis, [(i, (i + steps) % count) for i in range(count)])
@@ -244,29 +306,34 @@
 
 def on_device(queries, prefix_keys, cached_prefix_values, shard_len, reach, w_out):
     y_count, z_count = lax.axis_size("Y"), lax.axis_size("Z")
+    shard_count = lax.axis_size(BLK)
     tokens, heads, head_size = queries.shape
     q_own = queries.reshape(tokens * heads, head_size)
-
-    visitors = []
-    for j in range(1, SPAN):
-        visitors.append(passed_along(q_own, BLK, j))
+    slots = prefix_keys.shape[1]
+    odd = range(1, shard_count, 2)
+    q_near = passed_along(q_own, BLK, 2)
+    q_far = lax.ppermute(q_own, BLK, [(i, (i + 4) % shard_count) for i in odd])
+    k_other = passed_along(prefix_keys[0], "K", 1)
+    v_other = passed_along(cached_prefix_values[0], "K", 1)
     weights = lax.all_gather(w_out, "Y", axis=0, tiled=False)
 
-    part, keys, values, meta = first_part(
+    part_own, keys, values, meta = first_part(
         tokens, shard_len, reach, q_own, prefix_keys[0], cached_prefix_values[0]
     )
-    parts = [part]
-    for j in range(1, SPAN):
-        part = later_part(tokens, j, meta, visitors[j - 1], keys, values)
-        parts.append(passed_along(part, BLK, -j))
-    spread = combine(parts, z_count, tokens, heads)
+    part_near = later_part(
+        second_kernel, tokens, 2 * slots, [],
+        meta, q_near, keys, values, k_other, v_other,
+    )
+    back_near = passed_along(part_near, BLK, -2)
+    part_far = later_part(
+        third_kernel, tokens, slots, [pltpu.VMEM(q_own.shape, BF16)],
+        meta, q_own, q_far, k_other, v_other,
+    )
+    back_far = lax.ppermute(part_far, BLK, [(i, (i - 4) % shard_count) for i in odd])
+    spread = combine([part_own, back_near, part_far, back_far], z_count, tokens, heads)
     own = lax.all_to_all(spread, "Z", split_axis=0, concat_axis=0, tiled=True)
     other = passed_along(own, "K", 1)
     x_half = lax.axis_size("x") // 2
-    partial = project(own, other, weights, 2)
-    partial = partial.reshape(-1, *partial.shape[2:])
-    received = lax.all_to_all(partial, HEADS, split_axis=0, concat_axis=0, tiled=True)
-    summed = totals(received, 4)
     pairs = []
     for y in range(lax.axis_size("y")):
         for x in range(lax.axis_size("x")):
@@ -274,7 +341,14 @@
                 head = (big // x_half) * 2 * x_half + (big % x_half) * 2 + x % 2
                 target = head * y_count + y * x_half + x // 2
                 pairs.append(((y * 2 * x_half + x) * y_count + big, target))
-    return lax.ppermute(summed, ("y", "x", "Y"), pairs)
+    placed = []
+    for side in (own, other):
+        partial = project(side, weights, 2)
+        partial = partial.reshape(-1, *partial.shape[2:])
+        received = lax.all_to_all(partial, HEADS, split_axis=0, concat_axis=0, tiled=True)
+        summed = totals(received, 2)
+        placed.append(lax.ppermute(summed, ("y", "x", "Y"), pairs))
+    return in_order(z_count // 2, *placed)
 
 
 def solution(mesh):

time: 166 us -> 152 us (0.916)
  the two profiles are of different devices: /device:TPU:59 before, /device:TPU:27 now
where the time goes in v4:
time: 152 us
  waiting for transfers between devices  48.4 us (32%)
  starting transfers between devices  38 us (25%)
  blocking collectives  31.8 us (21%)
  Pallas kernels  18.2 us (12%)
  between operations  13.5 us (9%)
  local copies, waits for them, and re-layouts  1.98 us (1%)
    all_to_all x1, blocking collectives, on_device(): own = lax.all_to_all(spread, 'Z', split_axis=0, concat_axis=0, tiled=True)  31.8 us
    all_to_all x2, waiting for transfers between devices, on_device(): lax.all_to_all(partial, HEADS, split_axis=0, concat_axis=0, tiled=True)  14.9 us
    ppermute x5, waiting for transfers between devices, passed_along(): lax.ppermute(value, axis, [(i, (i + steps) % count) for i in range(count)])  13.9 us
    all_to_all x2, starting transfers between devices, on_device(): lax.all_to_all(partial, HEADS, split_axis=0, concat_axis=0, tiled=True)  12.7 us
    ppermute x5, starting transfers between devices, passed_along(): lax.ppermute(value, axis, [(i, (i + steps) % count) for i in range(count)])  12.3 us
    ppermute x2, waiting for transfers between devices, on_device(): placed.append(lax.ppermute(summed, ('y', 'x', 'Y'), pairs))  11.1 us
    ppermute x1, waiting for transfers between devices, on_device(): lax.ppermute(part_far, BLK, [(i, (i - 4) % shard_count) for i in odd])  7.72 us
    pallas_call x2, Pallas kernels, later_part(): pl.pallas_call(functools.partial(kernel, tokens), out_shape=jax.ShapeDtyp...  7.22 us
  transfers between devices with their start and end apart: 12, of which 7 were waited for; matrix products, arithmetic and copies ran while one was open for 0% of the time, Pallas kernels for 10%

profile of v4, /device:TPU:27, one launch (start us, length us, event | category | flops | bytes accessed | tf_op | source)
XLA Modules:
  0.0 151.9 jit_solution(11905836815721325858)
XLA Ops:
  6.5 0.0 all-gather.3.cloned.1.call-start
  6.5 0.7 all-gather.3.cloned.1.call-update
  7.3 2.6 %collective-permute-start.1 = (bf16[2048,128]{1,0:T(8,128)(2,1)}, bf16[2048,128]{1,0:T(8,128)(2,1)S(1)}, u32[]{:S(2)}, u32[]{:S(2)}) collective-permute-start(bf16[2048,128]{1,0:T(8,128)(2,1)} %bitcast.14), channel_id=1, source_target_pairs={{0,1},{1,0},{2,3},{3,2},{4,5},{5,4},{6,7},{7,6},{8,9},{9,8},{10,11... | collective-permute-start | bytes 1572872 | tf_op jit(solution)/shard_map/ppermute | solution.py:304
  9.8 1.9 %collective-permute-start.2 = (bf16[2048,128]{1,0:T(8,128)(2,1)}, bf16[2048,128]{1,0:T(8,128)(2,1)S(1)}, u32[]{:S(2)}, u32[]{:S(2)}) collective-permute-start(bf16[2048,128]{1,0:T(8,128)(2,1)} %bitcast.16), channel_id=1, source_target_pairs={{0,1},{1,0},{2,3},{3,2},{4,5},{5,4},{6,7},{7,6},{8,9},{9,8},{10,11... | collective-permute-start | bytes 1572872 | tf_op jit(solution)/shard_map/ppermute | solution.py:304
  11.8 4.0 %collective-permute-start = (bf16[512,128]{1,0:T(8,128)(2,1)}, bf16[512,128]{1,0:T(8,128)(2,1)S(1)}, u32[]{:S(2)}, u32[]{:S(2)}) collective-permute-start(bf16[512,128]{1,0:T(8,128)(2,1)} %bitcast.8), channel_id=1, source_target_pairs={{0,2},{1,3},{2,4},{3,5},{4,6},{5,7},{6,8},{7,9},{8,10},{9,11},{10,... | collective-permute-start | bytes 393224 | tf_op jit(solution)/shard_map/ppermute | solution.py:304
  15.8 5.8 %collective-permute-start.4 = (bf16[512,128]{1,0:T(8,128)(2,1)}, bf16[512,128]{1,0:T(8,128)(2,1)S(1)}, u32[]{:S(2)}, u32[]{:S(2)}) collective-permute-start(bf16[512,128]{1,0:T(8,128)(2,1)} %bitcast.9), channel_id=1, source_target_pairs={{1,5},{3,7},{5,9},{7,11},{9,13},{11,15},{13,17},{15,19},{17,21},{1... | collective-permute-start | bytes 393224 | tf_op jit(solution)/shard_map/ppermute | solution.py:315
  21.6 3.8 %first_part.1 = (bf16[528,128]{1,0:T(8,128)(2,1)S(1)}, bf16[2048,128]{1,0:T(8,128)(2,1)S(1)}, bf16[2048,128]{1,0:T(8,128)(2,1)S(1)}, s32[8,128]{1,0:T(8,128)S(1)}) custom-call(s32[64]{0:T(128)} %refs_0_.1, s32[64]{0:T(128)} %refs_1_.1, bf16[512,128]{1,0:T(8,128)(2,1)} %bitcast.10, bf16[2048,128]{1,0:T(8,128)(2,1)} %bitcast.15, bf16[2048,128]{1,0:T(8,128)(2,1)} %bitcast.17), custom_call_target="tpu_custom_call" | custom-call | flops 536870912 | bytes 1048576 | tf_op jit(solution)/shard_map/first_part/pallas_call | solution.py:132
  25.4 0.0 copy-start.3
  25.4 5.7 %collective-permute-done.q_ref = bf16[512,128]{1,0:T(8,128)(2,1)S(1)} collective-permute-done((bf16[512,128]{1,0:T(8,128)(2,1)}, bf16[512,128]{1,0:T(8,128)(2,1)S(1)}, u32[]{:S(2)}, u32[]{:S(2)}) %collective-permute-start) | collective-permute-done | bytes 131104 | tf_op jit(solution)/shard_map/ppermute | solution.py:304
  31.1 0.0 collective-permute-done.1.k_other
  31.1 0.0 collective-permute-done.2.v_other
  31.1 4.8 %shard_map.64 = bf16[528,128]{1,0:T(8,128)(2,1)S(1)} custom-call(s32[8,128]{1,0:T(8,128)S(1)} %get-tuple-element.10.meta_ref, bf16[512,128]{1,0:T(8,128)(2,1)S(1)} %collective-permute-done.q_ref, bf16[2048,128]{1,0:T(8,128)(2,1)S(1)} %get-tuple-element.11.k_ref, bf16[2048,128]{1,0:T(8,128)(2,1)S(1)} %get-tuple-element.12.v_ref, ...), custom_call_target="tpu_custom_call" | custom-call | flops 1073741824 | bytes 2097152 | tf_op jit(solution)/shard_map/pallas_call | solution.py:157
  35.9 1.9 %collective-permute-start.3 = (bf16[528,128]{1,0:T(8,128)(2,1)S(1)}, bf16[528,128]{1,0:T(8,128)(2,1)S(1)}, u32[]{:S(2)}, u32[]{:S(2)}) collective-permute-start(bf16[528,128]{1,0:T(8,128)(2,1)S(1)} %shard_map.64), channel_id=1, source_target_pairs={{0,62},{1,63},{2,0},{3,1},{4,2},{5,3},{6,4},{7,5},{8,6},{9,7},{10,... | collective-permute-start | bytes 405512 | tf_op jit(solution)/shard_map/ppermute | solution.py:304
  37.8 0.0 collective-permute-done.4.q_visit
  37.8 0.0 copy-done.3
  37.8 2.5 %shard_map.65.refs_2_ = bf16[528,128]{1,0:T(8,128)(2,1)S(1)} custom-call(s32[8,128]{1,0:T(8,128)S(1)} %get-tuple-element.10.meta_ref, bf16[512,128]{1,0:T(8,128)(2,1)S(1)} %bitcast.11, bf16[512,128]{1,0:T(8,128)(2,1)S(1)} %collective-permute-done.4.q_visit, bf16[2048,128]{1,0:T(8,128)(2,1)S(1)} %collective-permute-done.1.k_other, ...), custom_call_target="tpu_custom_call" | custom-call | flops 536870912 | bytes 1048576 | tf_op jit(solution)/shard_map/pallas_call | solution.py:157
  40.3 1.9 %collective-permute-start.5 = (bf16[528,128]{1,0:T(8,128)(2,1)S(1)}, bf16[528,128]{1,0:T(8,128)(2,1)S(1)}, u32[]{:S(2)}, u32[]{:S(2)}) collective-permute-start(bf16[528,128]{1,0:T(8,128)(2,1)S(1)} %shard_map.65.refs_2_), channel_id=1, source_target_pairs={{1,61},{3,63},{5,1},{7,3},{9,5},{11,7},{13,9},{15,11},{17,13},{19,... | collective-permute-start | bytes 405512 | tf_op jit(solution)/shard_map/ppermute | solution.py:332
  42.2 5.4 %collective-permute-done.3.refs_1_ = bf16[528,128]{1,0:T(8,128)(2,1)S(1)} collective-permute-done((bf16[528,128]{1,0:T(8,128)(2,1)S(1)}, bf16[528,128]{1,0:T(8,128)(2,1)S(1)}, u32[]{:S(2)}, u32[]{:S(2)}) %collective-permute-start.3) | collective-permute-done | bytes 135200 | tf_op jit(solution)/shard_map/ppermute | solution.py:304
  47.6 7.7 %collective-permute-done.5.refs_3_ = bf16[528,128]{1,0:T(8,128)(2,1)S(1)} collective-permute-done((bf16[528,128]{1,0:T(8,128)(2,1)S(1)}, bf16[528,128]{1,0:T(8,128)(2,1)S(1)}, u32[]{:S(2)}, u32[]{:S(2)}) %collective-permute-start.5) | collective-permute-done | bytes 135200 | tf_op jit(solution)/shard_map/ppermute | solution.py:332
  55.3 0.4 combine.1
  55.7 31.8 %all_to_all.15.side_ref = bf16[8,64,1024]{2,1,0:T(8,128)(2,1)S(1)} all-to-all(bf16[8,64,1024]{2,1,0:T(8,128)(2,1)S(1)} %combine.1), channel_id=1, replica_groups=mesh['y'=2,'x'=4,'Y'=4,'Z'=8,'K'=2] {'Z'}, dimensions={0} | all-to-all | bytes 2097152 | tf_op jit(solution)/shard_map/all_to_all | solution.py:334
  87.5 0.0 copy-start.2
  87.5 0.0 all-gather.3.cloned.1.call-done
  87.5 0.0 copy-start
  87.5 2.0 %copy-done = bf16[4096,256]{1,0:T(8,128)(2,1)S(1)} copy-done((bf16[4096,256]{1,0:T(8,128)(2,1)S(1)}, bf16[4096,256]{1,0:T(8,128)(2,1)}, u32[]{:S(2)}) %copy-start) | copy-done | bytes 2097176
  89.5 2.8 %project.2 = bf16[4,2,256,256]{3,2,1,0:T(8,128)(2,1)} custom-call(bf16[8,64,1024]{2,1,0:T(8,128)(2,1)S(1)} %all_to_all.15.side_ref, bf16[4,1024,256]{2,1,0:T(8,128)(2,1)S(1)} %bitcast.6), custom_call_target="tpu_custom_call" | custom-call | flops 1073741824 | bytes 4194304 | tf_op jit(solution)/shard_map/project/pallas_call | solution.py:235
  92.3 0.0 copy-done.2
  92.3 0.0 copy-start.1
  92.3 8.3 %all-to-all-start.1 = ((bf16[8,256,256]{2,1,0:T(8,128)(2,1)}), bf16[8,256,256]{2,1,0:T(8,128)(2,1)S(1)}, u32[]{:S(2)}, u32[]{:S(2)}) async-start(bf16[8,256,256]{2,1,0:T(8,128)(2,1)} %bitcast.13), calls=%async_computation.1 | async-start | bytes 2097152 | tf_op jit(solution)/shard_map/all_to_all | solution.py:348
  100.6 1.9 %collective-permute-start.7 = (bf16[8,64,1024]{2,1,0:T(8,128)(2,1)}, bf16[8,64,1024]{2,1,0:T(8,128)(2,1)S(1)}, u32[]{:S(2)}, u32[]{:S(2)}) collective-permute-start(bf16[8,64,1024]{2,1,0:T(8,128)(2,1)} %copy-done.2), channel_id=1, source_target_pairs={{0,1},{1,0},{2,3},{3,2},{4,5},{5,4},{6,7},{7,6},{8,9},{9,8},{10,11... | collective-permute-start | bytes 3145736 | tf_op jit(solution)/shard_map/ppermute | solution.py:304
  102.6 2.8 %collective-permute-done.7.side_ref = bf16[8,64,1024]{2,1,0:T(8,128)(2,1)S(1)} collective-permute-done((bf16[8,64,1024]{2,1,0:T(8,128)(2,1)}, bf16[8,64,1024]{2,1,0:T(8,128)(2,1)S(1)}, u32[]{:S(2)}, u32[]{:S(2)}) %collective-permute-start.7) | collective-permute-done | bytes 1048608 | tf_op jit(solution)/shard_map/ppermute | solution.py:304
  105.4 0.0 copy-done.1
  105.4 2.8 %project.3 = bf16[4,2,256,256]{3,2,1,0:T(8,128)(2,1)} custom-call(bf16[8,64,1024]{2,1,0:T(8,128)(2,1)S(1)} %collective-permute-done.7.side_ref, bf16[4,1024,256]{2,1,0:T(8,128)(2,1)S(1)} %bitcast.7), custom_call_target="tpu_custom_call" | custom-call | flops 1073741824 | bytes 4194304 | tf_op jit(solution)/shard_map/project/pallas_call | solution.py:235
  108.2 1.0 all-to-all-done.1.in_ref
  109.2 4.4 %all-to-all-start.2 = ((bf16[8,256,256]{2,1,0:T(8,128)(2,1)}), bf16[8,256,256]{2,1,0:T(8,128)(2,1)S(1)}, u32[]{:S(2)}, u32[]{:S(2)}) async-start(bf16[8,256,256]{2,1,0:T(8,128)(2,1)} %bitcast.12), calls=%async_computation.2 | async-start | bytes 2097152 | tf_op jit(solution)/shard_map/all_to_all | solution.py:348
  113.6 0.3 totals.2
  113.8 3.1 %collective-permute-start.6 = (bf16[256,256]{1,0:T(8,128)(2,1)S(1)}, bf16[256,256]{1,0:T(8,128)(2,1)S(1)}, u32[]{:S(2)}, u32[]{:S(2)}) collective-permute-start(bf16[256,256]{1,0:T(8,128)(2,1)S(1)} %totals.2), channel_id=1, source_target_pairs={{0,0},{16,128},{32,256},{48,384},{64,64},{80,192},{96,320},{112,44... | collective-permute-start | bytes 393224 | tf_op jit(solution)/shard_map/ppermute | solution.py:350
  116.9 13.9 %all-to-all-done.2.in_ref = bf16[8,256,256]{2,1,0:T(8,128)(2,1)S(1)} async-done(((bf16[8,256,256]{2,1,0:T(8,128)(2,1)}), bf16[8,256,256]{2,1,0:T(8,128)(2,1)S(1)}, u32[]{:S(2)}, u32[]{:S(2)}) %all-to-all-start.2) | async-done | bytes 1048608 | tf_op jit(solution)/shard_map/all_to_all | solution.py:348
  130.8 0.3 totals.3
  131.1 2.1 %collective-permute-start.8 = (bf16[256,256]{1,0:T(8,128)(2,1)S(1)}, bf16[256,256]{1,0:T(8,128)(2,1)S(1)}, u32[]{:S(2)}, u32[]{:S(2)}) collective-permute-start(bf16[256,256]{1,0:T(8,128)(2,1)S(1)} %totals.3), channel_id=1, source_target_pairs={{0,0},{16,128},{32,256},{48,384},{64,64},{80,192},{96,320},{112,44... | collective-permute-start | bytes 393224 | tf_op jit(solution)/shard_map/ppermute | solution.py:350
  133.2 0.0 collective-permute-done.6.own_ref
  133.2 11.1 %collective-permute-done.8.other_ref = bf16[256,256]{1,0:T(8,128)(2,1)S(1)} collective-permute-done((bf16[256,256]{1,0:T(8,128)(2,1)S(1)}, bf16[256,256]{1,0:T(8,128)(2,1)S(1)}, u32[]{:S(2)}, u32[]{:S(2)}) %collective-permute-start.8) | collective-permute-done | bytes 131104 | tf_op jit(solution)/shard_map/ppermute | solution.py:350
  144.3 0.7 in_order.1
Async XLA Ops:
  6.5 81.0 %all-gather.3.cloned.1.call-start = ((), (), s32[]{:S(2)}) async-start(), calls=%async_computation.3 | async-start | bytes 2621440 | tf_op jit(solution)/shard_map/all_gather | solution.py:318
  7.3 23.9 %collective-permute-start.1 = (bf16[2048,128]{1,0:T(8,128)(2,1)}, bf16[2048,128]{1,0:T(8,128)(2,1)S(1)}, u32[]{:S(2)}, u32[]{:S(2)}) collective-permute-start(bf16[2048,128]{1,0:T(8,128)(2,1)} %bitcast.14), channel_id=1, source_target_pairs={{0,1},{1,0},{2,3},{3,2},{4,5},{5,4},{6,7},{7,6},{8,9},{9,8},{10,11... | collective-permute-start | bytes 1572872 | tf_op jit(solution)/shard_map/ppermute | solution.py:304
  9.8 21.3 %collective-permute-start.2 = (bf16[2048,128]{1,0:T(8,128)(2,1)}, bf16[2048,128]{1,0:T(8,128)(2,1)S(1)}, u32[]{:S(2)}, u32[]{:S(2)}) collective-permute-start(bf16[2048,128]{1,0:T(8,128)(2,1)} %bitcast.16), channel_id=1, source_target_pairs={{0,1},{1,0},{2,3},{3,2},{4,5},{5,4},{6,7},{7,6},{8,9},{9,8},{10,11... | collective-permute-start | bytes 1572872 | tf_op jit(solution)/shard_map/ppermute | solution.py:304
  11.8 19.4 %collective-permute-start = (bf16[512,128]{1,0:T(8,128)(2,1)}, bf16[512,128]{1,0:T(8,128)(2,1)S(1)}, u32[]{:S(2)}, u32[]{:S(2)}) collective-permute-start(bf16[512,128]{1,0:T(8,128)(2,1)} %bitcast.8), channel_id=1, source_target_pairs={{0,2},{1,3},{2,4},{3,5},{4,6},{5,7},{6,8},{7,9},{8,10},{9,11},{10,... | collective-permute-start | bytes 393224 | tf_op jit(solution)/shard_map/ppermute | solution.py:304
  15.8 22.0 %collective-permute-start.4 = (bf16[512,128]{1,0:T(8,128)(2,1)}, bf16[512,128]{1,0:T(8,128)(2,1)S(1)}, u32[]{:S(2)}, u32[]{:S(2)}) collective-permute-start(bf16[512,128]{1,0:T(8,128)(2,1)} %bitcast.9), channel_id=1, source_target_pairs={{1,5},{3,7},{5,9},{7,11},{9,13},{11,15},{13,17},{15,19},{17,21},{1... | collective-permute-start | bytes 393224 | tf_op jit(solution)/shard_map/ppermute | solution.py:315
  25.4 12.4 %copy-start.3 = (bf16[64,8,128]{2,1,0:T(8,128)(2,1)S(1)}, bf16[64,8,128]{2,1,0:T(8,128)(2,1)}, u32[]{:S(2)}) copy-start(bf16[64,8,128]{2,1,0:T(8,128)(2,1)} %param.6) | copy-start | bytes 393220
  35.9 11.7 %collective-permute-start.3 = (bf16[528,128]{1,0:T(8,128)(2,1)S(1)}, bf16[528,128]{1,0:T(8,128)(2,1)S(1)}, u32[]{:S(2)}, u32[]{:S(2)}) collective-permute-start(bf16[528,128]{1,0:T(8,128)(2,1)S(1)} %shard_map.64), channel_id=1, source_target_pairs={{0,62},{1,63},{2,0},{3,1},{4,2},{5,3},{6,4},{7,5},{8,6},{9,7},{10,... | collective-permute-start | bytes 405512 | tf_op jit(solution)/shard_map/ppermute | solution.py:304
  40.3 15.0 %collective-permute-start.5 = (bf16[528,128]{1,0:T(8,128)(2,1)S(1)}, bf16[528,128]{1,0:T(8,128)(2,1)S(1)}, u32[]{:S(2)}, u32[]{:S(2)}) collective-permute-start(bf16[528,128]{1,0:T(8,128)(2,1)S(1)} %shard_map.65.refs_2_), channel_id=1, source_target_pairs={{1,61},{3,63},{5,1},{7,3},{9,5},{11,7},{13,9},{15,11},{17,13},{19,... | collective-permute-start | bytes 405512 | tf_op jit(solution)/shard_map/ppermute | solution.py:332
  87.5 4.8 %copy-start.2 = (bf16[8,64,1024]{2,1,0:T(8,128)(2,1)}, bf16[8,64,1024]{2,1,0:T(8,128)(2,1)S(1)}, u32[]{:S(2)}) copy-start(bf16[8,64,1024]{2,1,0:T(8,128)(2,1)S(1)} %all_to_all.15.side_ref) | copy-start | bytes 3145732
  87.5 2.0 %copy-start = (bf16[4096,256]{1,0:T(8,128)(2,1)S(1)}, bf16[4096,256]{1,0:T(8,128)(2,1)}, u32[]{:S(2)}) copy-start(bf16[4096,256]{1,0:T(8,128)(2,1)} %all-gather.3.cloned.1.call-done) | copy-start | bytes 6291460
  92.3 13.1 %copy-start.1 = (bf16[4096,256]{1,0:T(8,128)(2,1)S(1)}, bf16[4096,256]{1,0:T(8,128)(2,1)}, u32[]{:S(2)}) copy-start(bf16[4096,256]{1,0:T(8,128)(2,1)} %all-gather.3.cloned.1.call-done) | copy-start | bytes 6291460
  92.3 16.9 %all-to-all-start.1 = ((bf16[8,256,256]{2,1,0:T(8,128)(2,1)}), bf16[8,256,256]{2,1,0:T(8,128)(2,1)S(1)}, u32[]{:S(2)}, u32[]{:S(2)}) async-start(bf16[8,256,256]{2,1,0:T(8,128)(2,1)} %bitcast.13), calls=%async_computation.1 | async-start | bytes 2097152 | tf_op jit(solution)/shard_map/all_to_all | solution.py:348
  100.6 4.8 %collective-permute-start.7 = (bf16[8,64,1024]{2,1,0:T(8,128)(2,1)}, bf16[8,64,1024]{2,1,0:T(8,128)(2,1)S(1)}, u32[]{:S(2)}, u32[]{:S(2)}) collective-permute-start(bf16[8,64,1024]{2,1,0:T(8,128)(2,1)} %copy-done.2), channel_id=1, source_target_pairs={{0,1},{1,0},{2,3},{3,2},{4,5},{5,4},{6,7},{7,6},{8,9},{9,8},{10,11... | collective-permute-start | bytes 3145736 | tf_op jit(solution)/shard_map/ppermute | solution.py:304
  109.2 21.6 %all-to-all-start.2 = ((bf16[8,256,256]{2,1,0:T(8,128)(2,1)}), bf16[8,256,256]{2,1,0:T(8,128)(2,1)S(1)}, u32[]{:S(2)}, u32[]{:S(2)}) async-start(bf16[8,256,256]{2,1,0:T(8,128)(2,1)} %bitcast.12), calls=%async_computation.2 | async-start | bytes 2097152 | tf_op jit(solution)/shard_map/all_to_all | solution.py:348
  113.8 19.3 %collective-permute-start.6 = (bf16[256,256]{1,0:T(8,128)(2,1)S(1)}, bf16[256,256]{1,0:T(8,128)(2,1)S(1)}, u32[]{:S(2)}, u32[]{:S(2)}) collective-permute-start(bf16[256,256]{1,0:T(8,128)(2,1)S(1)} %totals.2), channel_id=1, source_target_pairs={{0,0},{16,128},{32,256},{48,384},{64,64},{80,192},{96,320},{112,44... | collective-permute-start | bytes 393224 | tf_op jit(solution)/shard_map/ppermute | solution.py:350
  131.1 13.3 %collective-permute-start.8 = (bf16[256,256]{1,0:T(8,128)(2,1)S(1)}, bf16[256,256]{1,0:T(8,128)(2,1)S(1)}, u32[]{:S(2)}, u32[]{:S(2)}) collective-permute-start(bf16[256,256]{1,0:T(8,128)(2,1)S(1)} %totals.3), channel_id=1, source_target_pairs={{0,0},{16,128},{32,256},{48,384},{64,64},{80,192},{96,320},{112,44... | collective-permute-start | bytes 393224 | tf_op jit(solution)/shard_map/ppermute | solution.py:350
Sparse Core Ops, SparseCore 0:
  9.4 66.6 all-gather.2

commit v5 on v4

--- a/solution.py
+++ b/solution.py
@@ -224,8 +224,8 @@
 def project_kernel(side_ref, w_ref, out_ref):
     count, rows, depth = side_ref.shape
     lhs = side_ref[...].reshape(count * rows, depth)
-    for i in range(w_ref.shape[0]):
-        out_ref[i, 0] = jnp.dot(lhs, w_ref[i], preferred_element_type=F32).astype(BF16)
+    part = jnp.dot(lhs, w_ref[0], preferred_element_type=F32).astype(BF16)
+    out_ref[...] = part.reshape(out_ref.shape)
 
 
 def project(side, weights, halves):
@@ -234,13 +234,13 @@
     runs = groups // halves
     return pl.pallas_call(
         project_kernel,
-        grid=(halves, runs // 2),
+        grid=(pieces,),
         out_shape=pltpu.HBM((pieces, halves, rows * runs, columns), BF16),
         in_specs=[
-            pl.BlockSpec((2, rows, depth), lambda i, j: (i * (runs // 2) + j, 0, 0)),
-            pl.BlockSpec(weights.shape, lambda i, j: (0, 0, 0)),
+            pl.BlockSpec((groups, rows, depth), lambda i: (0, 0, 0)),
+            pl.BlockSpec((1, depth, columns), lambda i: (i, 0, 0)),
         ],
-        out_specs=pl.BlockSpec((pieces, 1, 2 * rows, columns), lambda i, j: (0, i, j, 0)),
+        out_specs=pl.BlockSpec((1, halves, rows * runs, columns), lambda i: (i, 0, 0, 0)),
         compiler_params=pltpu.CompilerParams(vmem_limit_bytes=24 << 20),
         cost_estimate=pl.CostEstimate(
             flops=2 * groups * rows * depth * columns * pieces,
@@ -248,7 +248,7 @@
             transcendentals=0,
         ),
         name="project",
-    )(side, weights)
+    )(side, pltpu.with_memory_space_constraint(weights, pltpu.HBM))
 
 
 def total_kernel(in_ref, out_ref):
@@ -320,16 +320,16 @@
     part_own, keys, values, meta = first_part(
         tokens, shard_len, reach, q_own, prefix_keys[0], cached_prefix_values[0]
     )
+    part_far = later_part(
+        third_kernel, tokens, slots, [pltpu.VMEM(q_own.shape, BF16)],
+        meta, q_own, q_far, k_other, v_other,
+    )
+    back_far = lax.ppermute(part_far, BLK, [(i, (i - 4) % shard_count) for i in odd])
     part_near = later_part(
         second_kernel, tokens, 2 * slots, [],
         meta, q_near, keys, values, k_other, v_other,
     )
     back_near = passed_along(part_near, BLK, -2)
-    part_far = later_part(
-        third_kernel, tokens, slots, [pltpu.VMEM(q_own.shape, BF16)],
-        meta, q_own, q_far, k_other, v_other,
-    )
-    back_far = lax.ppermute(part_far, BLK, [(i, (i - 4) % shard_count) for i in odd])
     spread = combine([part_own, back_near, part_far, back_far], z_count, tokens, heads)
     own = lax.all_to_all(spread, "Z", split_axis=0, concat_axis=0, tiled=True)
     other = passed_along(own, "K", 1)

time: 152 us -> 153 us (level)
  the two profiles are of different devices: /device:TPU:27 before, /device:TPU:26 now
where the time goes in v5:
time: 153 us; the launch traced here: 152 us
  waiting for transfers between devices  43.8 us (29%)
  starting transfers between devices  40.9 us (27%)
  blocking collectives  32.3 us (21%)
  Pallas kernels  21.4 us (14%)
  between operations  13.5 us (9%)
    all_to_all x1, blocking collectives, on_device(): own = lax.all_to_all(spread, 'Z', split_axis=0, concat_axis=0, tiled=True)  32.3 us
    ppermute x5, starting transfers between devices, passed_along(): lax.ppermute(value, axis, [(i, (i + steps) % count) for i in range(count)])  20.3 us
    ppermute x5, waiting for transfers between devices, passed_along(): lax.ppermute(value, axis, [(i, (i + steps) % count) for i in range(count)])  19.6 us
    all_to_all x2, waiting for transfers between devices, on_device(): lax.all_to_all(partial, HEADS, split_axis=0, concat_axis=0, tiled=True)  13.4 us
    all_to_all x2, starting transfers between devices, on_device(): lax.all_to_all(partial, HEADS, split_axis=0, concat_axis=0, tiled=True)  13.1 us
    ppermute x2, waiting for transfers between devices, on_device(): placed.append(lax.ppermute(summed, ('y', 'x', 'Y'), pairs))  10.1 us
    pallas_call x2, Pallas kernels, project(): pl.pallas_call(project_kernel, grid=(pieces,), out_shape=pltpu.HBM((piece...  8.8 us
    pallas_call x2, Pallas kernels, later_part(): pl.pallas_call(functools.partial(kernel, tokens), out_shape=jax.ShapeDtyp...  7.21 us
  transfers between devices with their start and end apart: 12, of which 5 were waited for; matrix products, arithmetic and copies ran while one was open for 0% of the time, Pallas kernels for 11%

profile of v5, /device:TPU:26, one launch (start us, length us, event | category | flops | bytes accessed | tf_op | source)
XLA Modules:
  0.0 152.0 jit_solution(6844391282630280873)
XLA Ops:
  6.5 0.0 all-gather.3.cloned.1.call-start
  6.5 0.7 all-gather.3.cloned.1.call-update
  7.3 1.9 %collective-permute-start.1 = (bf16[2048,128]{1,0:T(8,128)(2,1)}, bf16[2048,128]{1,0:T(8,128)(2,1)S(1)}, u32[]{:S(2)}, u32[]{:S(2)}) collective-permute-start(bf16[2048,128]{1,0:T(8,128)(2,1)} %bitcast.14), channel_id=1, source_target_pairs={{0,1},{1,0},{2,3},{3,2},{4,5},{5,4},{6,7},{7,6},{8,9},{9,8},{10,11... | collective-permute-start | bytes 1572872 | tf_op jit(solution)/shard_map/ppermute | solution.py:304
  9.2 2.4 %collective-permute-start.2 = (bf16[2048,128]{1,0:T(8,128)(2,1)}, bf16[2048,128]{1,0:T(8,128)(2,1)S(1)}, u32[]{:S(2)}, u32[]{:S(2)}) collective-permute-start(bf16[2048,128]{1,0:T(8,128)(2,1)} %bitcast.16), channel_id=1, source_target_pairs={{0,1},{1,0},{2,3},{3,2},{4,5},{5,4},{6,7},{7,6},{8,9},{9,8},{10,11... | collective-permute-start | bytes 1572872 | tf_op jit(solution)/shard_map/ppermute | solution.py:304
  11.6 4.3 %collective-permute-start = (bf16[512,128]{1,0:T(8,128)(2,1)}, bf16[512,128]{1,0:T(8,128)(2,1)S(1)}, u32[]{:S(2)}, u32[]{:S(2)}) collective-permute-start(bf16[512,128]{1,0:T(8,128)(2,1)} %bitcast.6), channel_id=1, source_target_pairs={{0,2},{1,3},{2,4},{3,5},{4,6},{5,7},{6,8},{7,9},{8,10},{9,11},{10,... | collective-permute-start | bytes 393224 | tf_op jit(solution)/shard_map/ppermute | solution.py:304
  15.9 0.7 collective-permute-start.4
  16.6 3.8 %first_part.1 = (bf16[528,128]{1,0:T(8,128)(2,1)S(1)}, bf16[2048,128]{1,0:T(8,128)(2,1)S(1)}, bf16[2048,128]{1,0:T(8,128)(2,1)S(1)}, s32[8,128]{1,0:T(8,128)S(1)}) custom-call(s32[64]{0:T(128)} %refs_0_.1, s32[64]{0:T(128)} %refs_1_.1, bf16[512,128]{1,0:T(8,128)(2,1)} %bitcast.8, bf16[2048,128]{1,0:T(8,128)(2,1)} %bitcast.15, bf16[2048,128]{1,0:T(8,128)(2,1)} %bitcast.17), custom_call_target="tpu_custom_call" | custom-call | flops 536870912 | bytes 1048576 | tf_op jit(solution)/shard_map/first_part/pallas_call | solution.py:132
  20.4 0.0 copy-start
  20.4 10.9 %collective-permute-done.q_ref = bf16[512,128]{1,0:T(8,128)(2,1)S(1)} collective-permute-done((bf16[512,128]{1,0:T(8,128)(2,1)}, bf16[512,128]{1,0:T(8,128)(2,1)S(1)}, u32[]{:S(2)}, u32[]{:S(2)}) %collective-permute-start) | collective-permute-done | bytes 131104 | tf_op jit(solution)/shard_map/ppermute | solution.py:304
  31.3 0.0 collective-permute-done.1.k_other
  31.3 0.0 collective-permute-done.2.v_other
  31.3 4.7 %shard_map.64 = bf16[528,128]{1,0:T(8,128)(2,1)S(1)} custom-call(s32[8,128]{1,0:T(8,128)S(1)} %get-tuple-element.10.meta_ref, bf16[512,128]{1,0:T(8,128)(2,1)S(1)} %collective-permute-done.q_ref, bf16[2048,128]{1,0:T(8,128)(2,1)S(1)} %get-tuple-element.11.k_ref, bf16[2048,128]{1,0:T(8,128)(2,1)S(1)} %get-tuple-element.12.v_ref, ...), custom_call_target="tpu_custom_call" | custom-call | flops 1073741824 | bytes 2097152 | tf_op jit(solution)/shard_map/pallas_call | solution.py:157
  36.0 1.9 %collective-permute-start.3 = (bf16[528,128]{1,0:T(8,128)(2,1)S(1)}, bf16[528,128]{1,0:T(8,128)(2,1)S(1)}, u32[]{:S(2)}, u32[]{:S(2)}) collective-permute-start(bf16[528,128]{1,0:T(8,128)(2,1)S(1)} %shard_map.64), channel_id=1, source_target_pairs={{0,62},{1,63},{2,0},{3,1},{4,2},{5,3},{6,4},{7,5},{8,6},{9,7},{10,... | collective-permute-start | bytes 405512 | tf_op jit(solution)/shard_map/ppermute | solution.py:304
  38.0 0.0 collective-permute-done.4.q_visit
  38.0 0.0 copy-done
  38.0 2.5 %shard_map.65.refs_2_ = bf16[528,128]{1,0:T(8,128)(2,1)S(1)} custom-call(s32[8,128]{1,0:T(8,128)S(1)} %get-tuple-element.10.meta_ref, bf16[512,128]{1,0:T(8,128)(2,1)S(1)} %bitcast.9, bf16[512,128]{1,0:T(8,128)(2,1)S(1)} %collective-permute-done.4.q_visit, bf16[2048,128]{1,0:T(8,128)(2,1)S(1)} %collective-permute-done.1.k_other, ...), custom_call_target="tpu_custom_call" | custom-call | flops 536870912 | bytes 1048576 | tf_op jit(solution)/shard_map/pallas_call | solution.py:157
  40.4 0.7 collective-permute-start.5
  41.1 6.5 %collective-permute-done.3.refs_1_ = bf16[528,128]{1,0:T(8,128)(2,1)S(1)} collective-permute-done((bf16[528,128]{1,0:T(8,128)(2,1)S(1)}, bf16[528,128]{1,0:T(8,128)(2,1)S(1)}, u32[]{:S(2)}, u32[]{:S(2)}) %collective-permute-start.3) | collective-permute-done | bytes 135200 | tf_op jit(solution)/shard_map/ppermute | solution.py:304
  47.6 0.0 collective-permute-done.5.refs_3_
  47.6 0.4 combine.1
  48.0 32.3 %all_to_all.15.side_ref = bf16[8,64,1024]{2,1,0:T(8,128)(2,1)S(1)} all-to-all(bf16[8,64,1024]{2,1,0:T(8,128)(2,1)S(1)} %combine.1), channel_id=1, replica_groups=mesh['y'=2,'x'=4,'Y'=4,'Z'=8,'K'=2] {'Z'}, dimensions={0} | all-to-all | bytes 2097152 | tf_op jit(solution)/shard_map/all_to_all | solution.py:334
  80.3 0.0 all-gather.3.cloned.1.call-done
  80.3 4.4 %project.2 = bf16[4,2,256,256]{3,2,1,0:T(8,128)(2,1)} custom-call(bf16[8,64,1024]{2,1,0:T(8,128)(2,1)S(1)} %all_to_all.15.side_ref, bf16[4,1024,256]{2,1,0:T(8,128)(2,1)} %bitcast.10), custom_call_target="tpu_custom_call" | custom-call | flops 1073741824 | bytes 4194304 | tf_op jit(solution)/shard_map/project/pallas_call | solution.py:235
  84.7 7.4 %all-to-all-start.1 = ((bf16[8,256,256]{2,1,0:T(8,128)(2,1)}), bf16[8,256,256]{2,1,0:T(8,128)(2,1)S(1)}, u32[]{:S(2)}, u32[]{:S(2)}) async-start(bf16[8,256,256]{2,1,0:T(8,128)(2,1)} %bitcast.13), calls=%async_computation.1 | async-start | bytes 2097152 | tf_op jit(solution)/shard_map/all_to_all | solution.py:348
  92.1 9.7 %collective-permute-start.7 = (bf16[8,64,1024]{2,1,0:T(8,128)(2,1)S(1)}, bf16[8,64,1024]{2,1,0:T(8,128)(2,1)S(1)}, u32[]{:S(2)}, u32[]{:S(2)}) collective-permute-start(bf16[8,64,1024]{2,1,0:T(8,128)(2,1)S(1)} %all_to_all.15.side_ref), channel_id=1, source_target_pairs={{0,1},{1,0},{2,3},{3,2},{4,5},{5,4},{6,7},{7,6},{8,9},{9,8},{10,11... | collective-permute-start | bytes 3145736 | tf_op jit(solution)/shard_map/ppermute | solution.py:304
  101.9 2.3 %collective-permute-done.7.side_ref = bf16[8,64,1024]{2,1,0:T(8,128)(2,1)S(1)} collective-permute-done((bf16[8,64,1024]{2,1,0:T(8,128)(2,1)S(1)}, bf16[8,64,1024]{2,1,0:T(8,128)(2,1)S(1)}, u32[]{:S(2)}, u32[]{:S(2)}) %collective-permute-start.7) | collective-permute-done | bytes 1048608 | tf_op jit(solution)/shard_map/ppermute | solution.py:304
  104.1 4.4 %project.3 = bf16[4,2,256,256]{3,2,1,0:T(8,128)(2,1)} custom-call(bf16[8,64,1024]{2,1,0:T(8,128)(2,1)S(1)} %collective-permute-done.7.side_ref, bf16[4,1024,256]{2,1,0:T(8,128)(2,1)} %bitcast.11), custom_call_target="tpu_custom_call" | custom-call | flops 1073741824 | bytes 4194304 | tf_op jit(solution)/shard_map/project/pallas_call | solution.py:235
  108.5 0.0 all-to-all-done.1.in_ref
  108.5 5.7 %all-to-all-start.2 = ((bf16[8,256,256]{2,1,0:T(8,128)(2,1)}), bf16[8,256,256]{2,1,0:T(8,128)(2,1)S(1)}, u32[]{:S(2)}, u32[]{:S(2)}) async-start(bf16[8,256,256]{2,1,0:T(8,128)(2,1)} %bitcast.12), calls=%async_computation.2 | async-start | bytes 2097152 | tf_op jit(solution)/shard_map/all_to_all | solution.py:348
  114.2 0.3 totals.2
  114.5 3.4 %collective-permute-start.6 = (bf16[256,256]{1,0:T(8,128)(2,1)S(1)}, bf16[256,256]{1,0:T(8,128)(2,1)S(1)}, u32[]{:S(2)}, u32[]{:S(2)}) collective-permute-start(bf16[256,256]{1,0:T(8,128)(2,1)S(1)} %totals.2), channel_id=1, source_target_pairs={{0,0},{16,128},{32,256},{48,384},{64,64},{80,192},{96,320},{112,44... | collective-permute-start | bytes 393224 | tf_op jit(solution)/shard_map/ppermute | solution.py:350
  117.9 13.3 %all-to-all-done.2.in_ref = bf16[8,256,256]{2,1,0:T(8,128)(2,1)S(1)} async-done(((bf16[8,256,256]{2,1,0:T(8,128)(2,1)}), bf16[8,256,256]{2,1,0:T(8,128)(2,1)S(1)}, u32[]{:S(2)}, u32[]{:S(2)}) %all-to-all-start.2) | async-done | bytes 1048608 | tf_op jit(solution)/shard_map/all_to_all | solution.py:348
  131.2 0.3 totals.3
  131.5 2.8 %collective-permute-start.8 = (bf16[256,256]{1,0:T(8,128)(2,1)S(1)}, bf16[256,256]{1,0:T(8,128)(2,1)S(1)}, u32[]{:S(2)}, u32[]{:S(2)}) collective-permute-start(bf16[256,256]{1,0:T(8,128)(2,1)S(1)} %totals.3), channel_id=1, source_target_pairs={{0,0},{16,128},{32,256},{48,384},{64,64},{80,192},{96,320},{112,44... | collective-permute-start | bytes 393224 | tf_op jit(solution)/shard_map/ppermute | solution.py:350
  134.3 0.0 collective-permute-done.6.own_ref
  134.3 10.1 %collective-permute-done.8.other_ref = bf16[256,256]{1,0:T(8,128)(2,1)S(1)} collective-permute-done((bf16[256,256]{1,0:T(8,128)(2,1)S(1)}, bf16[256,256]{1,0:T(8,128)(2,1)S(1)}, u32[]{:S(2)}, u32[]{:S(2)}) %collective-permute-start.8) | collective-permute-done | bytes 131104 | tf_op jit(solution)/shard_map/ppermute | solution.py:350
  144.4 0.7 in_order.1
Async XLA Ops:
  6.5 73.8 %all-gather.3.cloned.1.call-start = ((), (), s32[]{:S(2)}) async-start(), calls=%async_computation.3 | async-start | bytes 2621440 | tf_op jit(solution)/shard_map/all_gather | solution.py:318
  7.3 24.0 %collective-permute-start.1 = (bf16[2048,128]{1,0:T(8,128)(2,1)}, bf16[2048,128]{1,0:T(8,128)(2,1)S(1)}, u32[]{:S(2)}, u32[]{:S(2)}) collective-permute-start(bf16[2048,128]{1,0:T(8,128)(2,1)} %bitcast.14), channel_id=1, source_target_pairs={{0,1},{1,0},{2,3},{3,2},{4,5},{5,4},{6,7},{7,6},{8,9},{9,8},{10,11... | collective-permute-start | bytes 1572872 | tf_op jit(solution)/shard_map/ppermute | solution.py:304
  9.2 22.1 %collective-permute-start.2 = (bf16[2048,128]{1,0:T(8,128)(2,1)}, bf16[2048,128]{1,0:T(8,128)(2,1)S(1)}, u32[]{:S(2)}, u32[]{:S(2)}) collective-permute-start(bf16[2048,128]{1,0:T(8,128)(2,1)} %bitcast.16), channel_id=1, source_target_pairs={{0,1},{1,0},{2,3},{3,2},{4,5},{5,4},{6,7},{7,6},{8,9},{9,8},{10,11... | collective-permute-start | bytes 1572872 | tf_op jit(solution)/shard_map/ppermute | solution.py:304
  11.6 19.7 %collective-permute-start = (bf16[512,128]{1,0:T(8,128)(2,1)}, bf16[512,128]{1,0:T(8,128)(2,1)S(1)}, u32[]{:S(2)}, u32[]{:S(2)}) collective-permute-start(bf16[512,128]{1,0:T(8,128)(2,1)} %bitcast.6), channel_id=1, source_target_pairs={{0,2},{1,3},{2,4},{3,5},{4,6},{5,7},{6,8},{7,9},{8,10},{9,11},{10,... | collective-permute-start | bytes 393224 | tf_op jit(solution)/shard_map/ppermute | solution.py:304
  15.9 22.1 %collective-permute-start.4 = (bf16[512,128]{1,0:T(8,128)(2,1)}, bf16[512,128]{1,0:T(8,128)(2,1)S(1)}, u32[]{:S(2)}, u32[]{:S(2)}) collective-permute-start(bf16[512,128]{1,0:T(8,128)(2,1)} %bitcast.7), channel_id=1, source_target_pairs={{1,5},{3,7},{5,9},{7,11},{9,13},{11,15},{13,17},{15,19},{17,21},{1... | collective-permute-start | bytes 393224 | tf_op jit(solution)/shard_map/ppermute | solution.py:315
  20.4 17.6 %copy-start = (bf16[64,8,128]{2,1,0:T(8,128)(2,1)S(1)}, bf16[64,8,128]{2,1,0:T(8,128)(2,1)}, u32[]{:S(2)}) copy-start(bf16[64,8,128]{2,1,0:T(8,128)(2,1)} %param.6) | copy-start | bytes 393220
  36.0 11.6 %collective-permute-start.3 = (bf16[528,128]{1,0:T(8,128)(2,1)S(1)}, bf16[528,128]{1,0:T(8,128)(2,1)S(1)}, u32[]{:S(2)}, u32[]{:S(2)}) collective-permute-start(bf16[528,128]{1,0:T(8,128)(2,1)S(1)} %shard_map.64), channel_id=1, source_target_pairs={{0,62},{1,63},{2,0},{3,1},{4,2},{5,3},{6,4},{7,5},{8,6},{9,7},{10,... | collective-permute-start | bytes 405512 | tf_op jit(solution)/shard_map/ppermute | solution.py:304
  40.4 7.1 %collective-permute-start.5 = (bf16[528,128]{1,0:T(8,128)(2,1)S(1)}, bf16[528,128]{1,0:T(8,128)(2,1)S(1)}, u32[]{:S(2)}, u32[]{:S(2)}) collective-permute-start(bf16[528,128]{1,0:T(8,128)(2,1)S(1)} %shard_map.65.refs_2_), channel_id=1, source_target_pairs={{1,61},{3,63},{5,1},{7,3},{9,5},{11,7},{13,9},{15,11},{17,13},{19,... | collective-permute-start | bytes 405512 | tf_op jit(solution)/shard_map/ppermute | solution.py:327
  84.7 23.8 %all-to-all-start.1 = ((bf16[8,256,256]{2,1,0:T(8,128)(2,1)}), bf16[8,256,256]{2,1,0:T(8,128)(2,1)S(1)}, u32[]{:S(2)}, u32[]{:S(2)}) async-start(bf16[8,256,256]{2,1,0:T(8,128)(2,1)} %bitcast.13), calls=%async_computation.1 | async-start | bytes 2097152 | tf_op jit(solution)/shard_map/all_to_all | solution.py:348
  92.1 12.0 %collective-permute-start.7 = (bf16[8,64,1024]{2,1,0:T(8,128)(2,1)S(1)}, bf16[8,64,1024]{2,1,0:T(8,128)(2,1)S(1)}, u32[]{:S(2)}, u32[]{:S(2)}) collective-permute-start(bf16[8,64,1024]{2,1,0:T(8,128)(2,1)S(1)} %all_to_all.15.side_ref), channel_id=1, source_target_pairs={{0,1},{1,0},{2,3},{3,2},{4,5},{5,4},{6,7},{7,6},{8,9},{9,8},{10,11... | collective-permute-start | bytes 3145736 | tf_op jit(solution)/shard_map/ppermute | solution.py:304
  108.5 22.7 %all-to-all-start.2 = ((bf16[8,256,256]{2,1,0:T(8,128)(2,1)}), bf16[8,256,256]{2,1,0:T(8,128)(2,1)S(1)}, u32[]{:S(2)}, u32[]{:S(2)}) async-start(bf16[8,256,256]{2,1,0:T(8,128)(2,1)} %bitcast.12), calls=%async_computation.2 | async-start | bytes 2097152 | tf_op jit(solution)/shard_map/all_to_all | solution.py:348
  114.5 19.8 %collective-permute-start.6 = (bf16[256,256]{1,0:T(8,128)(2,1)S(1)}, bf16[256,256]{1,0:T(8,128)(2,1)S(1)}, u32[]{:S(2)}, u32[]{:S(2)}) collective-permute-start(bf16[256,256]{1,0:T(8,128)(2,1)S(1)} %totals.2), channel_id=1, source_target_pairs={{0,0},{16,128},{32,256},{48,384},{64,64},{80,192},{96,320},{112,44... | collective-permute-start | bytes 393224 | tf_op jit(solution)/shard_map/ppermute | solution.py:350
  131.5 12.9 %collective-permute-start.8 = (bf16[256,256]{1,0:T(8,128)(2,1)S(1)}, bf16[256,256]{1,0:T(8,128)(2,1)S(1)}, u32[]{:S(2)}, u32[]{:S(2)}) collective-permute-start(bf16[256,256]{1,0:T(8,128)(2,1)S(1)} %totals.3), channel_id=1, source_target_pairs={{0,0},{16,128},{32,256},{48,384},{64,64},{80,192},{96,320},{112,44... | collective-permute-start | bytes 393224 | tf_op jit(solution)/shard_map/ppermute | solution.py:350
Sparse Core Ops, SparseCore 0:
  9.4 66.4 all-gather.2

commit v6 on v4

--- a/solution.py
+++ b/solution.py
@@ -166,8 +166,7 @@
 
 
 def combine_kernel(*refs):
-    parts, out_ref, total_ref = refs[:-2], refs[-2], refs[-1]
-    copies, tokens, _ = out_ref.shape
+    parts, keep_ref, send_ref, total_ref = refs[:-3], refs[-3], refs[-2], refs[-1]
     head_size = parts[0].shape[1]
     groups = parts[0].shape[0] // (TILE + 4)
     rows = groups * TILE
@@ -197,21 +196,25 @@
             term = taken(part, group * TILE, (group + 1) * TILE).astype(F32) * column
             total = term if total is None else total + term
         total_ref[group * TILE : (group + 1) * TILE, :] = total
-    heads = rows // tokens
+    count = keep_ref.shape[0]
+    heads = rows // (2 * count)
+    lead = lax.axis_index("y") == 0
     for head in range(heads):
-        piece = total_ref[pl.ds(head, tokens, stride=heads), :].astype(BF16)
-        for copy in range(copies):
-            out_ref[copy, :, head * head_size : (head + 1) * head_size] = piece
-
-
-def combine(parts, copies, tokens, heads):
+        first = total_ref[pl.ds(head, count, stride=heads), :].astype(BF16)
+        second = total_ref[pl.ds(heads * count + head, count, stride=heads), :].astype(BF16)
+        columns = slice(head * head_size, (head + 1) * head_size)
+        keep_ref[:, columns] = jnp.where(lead, first, second)
+        send_ref[:, columns] = jnp.where(lead, second, first)
+
+
+def combine(parts, tokens, heads):
     head_size = parts[0].shape[1]
-    vmem = pl.BlockSpec(memory_space=pltpu.VMEM)
+    half = jax.ShapeDtypeStruct((tokens // 2, heads * head_size), BF16)
     return pl.pallas_call(
         combine_kernel,
-        out_shape=jax.ShapeDtypeStruct((copies, tokens, heads * head_size), BF16),
-        in_specs=[vmem] * len(parts),
-        out_specs=vmem,
+        out_shape=(half, half),
+        in_specs=[VMEM] * len(parts),
+        out_specs=(VMEM, VMEM),
         scratch_shapes=[pltpu.VMEM((heads * tokens, head_size), F32)],
         compiler_params=pltpu.CompilerParams(vmem_limit_bytes=8 << 20),
         cost_estimate=pl.CostEstimate(
@@ -221,71 +224,108 @@
     )(*parts)
 
 
-def project_kernel(side_ref, w_ref, out_ref):
-    count, rows, depth = side_ref.shape
-    lhs = side_ref[...].reshape(count * rows, depth)
-    for i in range(w_ref.shape[0]):
-        out_ref[i, 0] = jnp.dot(lhs, w_ref[i], preferred_element_type=F32).astype(BF16)
-
-
-def project(side, weights, halves):
-    groups, rows, depth = side.shape
-    pieces, _, columns = weights.shape
-    runs = groups // halves
+def widen_kernel(keep_ref, got_ref, out_ref):
+    width = keep_ref.shape[1]
+    for copy in range(out_ref.shape[0]):
+        out_ref[copy, :, :width] = keep_ref[...]
+        out_ref[copy, :, width:] = got_ref[...]
+
+
+def widen(keep, got, copies):
+    rows, width = keep.shape
+    return pl.pallas_call(
+        widen_kernel,
+        out_shape=jax.ShapeDtypeStruct((copies, rows, 2 * width), BF16),
+        in_specs=[VMEM] * 2,
+        out_specs=VMEM,
+        compiler_params=pltpu.CompilerParams(vmem_limit_bytes=8 << 20),
+        cost_estimate=pl.CostEstimate(
+            flops=1 << 18, bytes_accessed=1 << 20, transcendentals=0
+        ),
+        name="widen",
+    )(keep, got)
+
+
+def project_kernel(own_ref, other_ref, w_ref, out_ref):
+    groups, rows, width = own_ref.shape
+    depth = width // 2
+    pair = lax.axis_index("y")
+    w_own, w_other = w_ref[pair], w_ref[1 - pair]
+    for slot, ref in enumerate((own_ref, other_ref)):
+        lhs = ref[...].reshape(groups * rows, width)
+        part = jnp.dot(lhs[:, :depth], w_own, preferred_element_type=F32)
+        part += jnp.dot(lhs[:, depth:], w_other, preferred_element_type=F32)
+        part = part.astype(BF16)
+        half = groups * rows // 2
+        for i in range(2):
+            out_ref[0, i, 0, slot * half : (slot + 1) * half, :] = part[i * half : (i + 1) * half]
+
+
+def project(own, other, weights):
+    groups, rows, width = own.shape
+    depth, columns = weights.shape[1:]
+    pieces = weights.shape[0] // 2
+    side = pl.BlockSpec((groups, rows, width), lambda i: (0, 0, 0))
     return pl.pallas_call(
         project_kernel,
-        grid=(halves, runs // 2),
-        out_shape=pltpu.HBM((pieces, halves, rows * runs, columns), BF16),
-        in_specs=[
-            pl.BlockSpec((2, rows, depth), lambda i, j: (i * (runs // 2) + j, 0, 0)),
-            pl.BlockSpec(weights.shape, lambda i, j: (0, 0, 0)),
-        ],
-        out_specs=pl.BlockSpec((pieces, 1, 2 * rows, columns), lambda i, j: (0, i, j, 0)),
+        grid=(pieces,),
+        out_shape=pltpu.HBM((pieces // 2, 2, 2, groups * rows, columns), BF16),
+        in_specs=[side, side, pl.BlockSpec((2, depth, columns), lambda i: (i, 0, 0))],
+        out_specs=pl.BlockSpec(
+            (1, 2, 1, groups * rows, columns), lambda i: (i // 2, 0, i % 2, 0, 0)
+        ),
         compiler_params=pltpu.CompilerParams(vmem_limit_bytes=24 << 20),
         cost_estimate=pl.CostEstimate(
-            flops=2 * groups * rows * depth * columns * pieces,
-            bytes_accessed=4 << 20,
+            flops=4 * groups * rows * width * columns * pieces,
+            bytes_accessed=6 << 20,
             transcendentals=0,
         ),
         name="project",
-    )(side, weights)
-
-
-def total_kernel(in_ref, out_ref):
-    total = in_ref[0].astype(F32)
-    for i in range(1, in_ref.shape[0]):
-        total += in_ref[i].astype(F32)
-    out_ref[...] = total.astype(BF16)
-
-
-def totals(received, steps):
-    sources, rows, columns = received.shape
-    step = rows // steps
+    )(own, other, pltpu.with_memory_space_constraint(weights, pltpu.HBM))
+
+
+def total_kernel(in_ref, *out_refs):
+    rows = in_ref.shape[2]
+    step = 64
+    for k, out_ref in enumerate(out_refs):
+        piece = lax.rem(lax.axis_index("y") + k, 2)
+        for start in range(0, rows, step):
+            total = in_ref[0, piece, start : start + step, :].astype(F32)
+            for i in range(1, in_ref.shape[0]):
+                total += in_ref[i, piece, start : start + step, :].astype(F32)
+            out_ref[start : start + step, :] = total.astype(BF16)
+
+
+def totals(received):
+    sources, count, rows, columns = received.shape
     return pl.pallas_call(
         total_kernel,
-        grid=(steps,),
-        out_shape=jax.ShapeDtypeStruct((rows, columns), BF16),
-        in_specs=[pl.BlockSpec((sources, step, columns), lambda i: (0, i, 0))],
-        out_specs=pl.BlockSpec((step, columns), lambda i: (i, 0)),
+        out_shape=[jax.ShapeDtypeStruct((rows, columns), BF16)] * count,
+        in_specs=[VMEM],
+        out_specs=[VMEM] * count,
         compiler_params=pltpu.CompilerParams(vmem_limit_bytes=16 << 20),
         cost_estimate=pl.CostEstimate(
-            flops=sources * rows * columns, bytes_accessed=3 << 20, transcendentals=0
+            flops=sources * count * rows * columns, bytes_accessed=2 << 20, transcendentals=0
         ),
         name="totals",
     )(received)
 
 
-def order_kernel(runs, own_ref, other_ref, out_ref):
-    rows = own_ref.shape[0] // runs
-    core = lax.axis_index("K")
-    for i in range(runs):
-        for ref, slot in ((own_ref, core), (other_ref, 1 - core)):
-            start = pl.multiple_of(slot * rows + 2 * i * rows, rows)
-            out_ref[pl.ds(start, rows), :] = ref[i * rows : (i + 1) * rows, :]
-
-
-def in_order(runs, own, other):
-    rows, columns = own.shape
+def order_kernel(runs, *refs):
+    pieces, out_ref = refs[:-1], refs[-1]
+    rows = pieces[0].shape[0] // (2 * runs)
+    core, big = lax.axis_index("K"), lax.axis_index("Y")
+    for k, ref in enumerate(pieces):
+        half = lax.rem(big + k, 2)
+        for slot, held in enumerate((core, 1 - core)):
+            for i in range(runs):
+                start = pl.multiple_of(((2 * i + held) * 2 + half) * rows, rows)
+                source = (slot * runs + i) * rows
+                out_ref[pl.ds(start, rows), :] = ref[source : source + rows, :]
+
+
+def in_order(runs, pieces):
+    rows, columns = pieces[0].shape
     return pl.pallas_call(
         functools.partial(order_kernel, runs),
         out_shape=jax.ShapeDtypeStruct((2 * rows, columns), BF16),
@@ -296,7 +336,7 @@
             flops=1 << 18, bytes_accessed=1 << 19, transcendentals=0
         ),
         name="in_order",
-    )(own, other)
+    )(*pieces)
 
 
 def passed_along(value, axis, steps):
@@ -315,7 +355,7 @@
     q_far = lax.ppermute(q_own, BLK, [(i, (i + 4) % shard_count) for i in odd])
     k_other = passed_along(prefix_keys[0], "K", 1)
     v_other = passed_along(cached_prefix_values[0], "K", 1)
-    weights = lax.all_gather(w_out, "Y", axis=0, tiled=False)
+    weights = lax.all_gather(w_out, ("Y", "y"), axis=0, tiled=False)
 
     part_own, keys, values, meta = first_part(
         tokens, shard_len, reach, q_own, prefix_keys[0], cached_prefix_values[0]
@@ -330,25 +370,26 @@
         meta, q_own, q_far, k_other, v_other,
     )
     back_far = lax.ppermute(part_far, BLK, [(i, (i - 4) % shard_count) for i in odd])
-    spread = combine([part_own, back_near, part_far, back_far], z_count, tokens, heads)
-    own = lax.all_to_all(spread, "Z", split_axis=0, concat_axis=0, tiled=True)
+    keep, send = combine([part_own, back_near, part_far, back_far], tokens, heads)
+    got = passed_along(send, "y", 1)
+    wide = widen(keep, got, z_count)
+    own = lax.all_to_all(wide, "Z", split_axis=0, concat_axis=0, tiled=True)
     other = passed_along(own, "K", 1)
-    x_half = lax.axis_size("x") // 2
-    pairs = []
-    for y in range(lax.axis_size("y")):
-        for x in range(lax.axis_size("x")):
-            for big in range(y_count):
-                head = (big // x_half) * 2 * x_half + (big % x_half) * 2 + x % 2
-                target = head * y_count + y * x_half + x // 2
-                pairs.append(((y * 2 * x_half + x) * y_count + big, target))
+    partial = project(own, other, weights)
+    partial = partial.reshape(-1, *partial.shape[2:])
+    received = lax.all_to_all(partial, "x", split_axis=0, concat_axis=0, tiled=True)
+    summed = totals(received)
     placed = []
-    for side in (own, other):
-        partial = project(side, weights, 2)
-        partial = partial.reshape(-1, *partial.shape[2:])
-        received = lax.all_to_all(partial, HEADS, split_axis=0, concat_axis=0, tiled=True)
-        summed = totals(received, 2)
-        placed.append(lax.ppermute(summed, ("y", "x", "Y"), pairs))
-    return in_order(z_count // 2, *placed)
+    for k in range(2):
+        pairs = []
+        for y in range(2):
+            for x in range(lax.axis_size("x")):
+                for big in range(y_count):
+                    head = (big // 2) * 4 + (big % 2) * 2 + x % 2
+                    target = head * y_count + (x // 2) * 2 + (y + k) % 2
+                    pairs.append(((y * 4 + x) * y_count + big, target))
+        placed.append(lax.ppermute(summed[k], ("y", "x", "Y"), pairs))
+    return in_order(z_count // 2, placed)
 
 
 def solution(mesh):

time: 152 us -> 153 us (level)
  the two profiles are of different devices: /device:TPU:27 before, /device:TPU:8 now
where the time goes in v6:
time: 153 us; the launch traced here: 152 us
  blocking collectives  52.3 us (34%)
  waiting for transfers between devices  43.6 us (28%)
  starting transfers between devices  25 us (16%)
  Pallas kernels  17.7 us (12%)
  between operations  13.5 us (9%)
    all_to_all x1, blocking collectives, on_device(): own = lax.all_to_all(wide, 'Z', split_axis=0, concat_axis=0, tiled=True)  32.7 us
    ppermute x6, waiting for transfers between devices, passed_along(): lax.ppermute(value, axis, [(i, (i + steps) % count) for i in range(count)])  26.4 us
    all_to_all x1, blocking collectives, on_device(): lax.all_to_all(partial, 'x', split_axis=0, concat_axis=0, tiled=True)  19.6 us
    ppermute x6, starting transfers between devices, passed_along(): lax.ppermute(value, axis, [(i, (i + steps) % count) for i in range(count)])  18.2 us
    ppermute x2, waiting for transfers between devices, on_device(): placed.append(lax.ppermute(summed[k], ('y', 'x', 'Y'), pairs))  16.5 us
    pallas_call x2, Pallas kernels, later_part(): pl.pallas_call(functools.partial(kernel, tokens), out_shape=jax.ShapeDtyp...  7.19 us
    pallas_call x1, Pallas kernels, project(): pl.pallas_call(project_kernel, grid=(pieces,), out_shape=pltpu.HBM((piece...  5.54 us
    ppermute x2, starting transfers between devices, on_device(): placed.append(lax.ppermute(summed[k], ('y', 'x', 'Y'), pairs))  5.51 us
  transfers between devices with their start and end apart: 11, of which 5 were waited for; matrix products, arithmetic and copies ran while one was open for 0% of the time, Pallas kernels for 7%

profile of v6, /device:TPU:8, one launch (start us, length us, event | category | flops | bytes accessed | tf_op | source)
XLA Modules:
  0.0 152.3 jit_solution(13164585008603581086)
XLA Ops:
  6.5 0.0 copy-start
  6.5 0.0 all-gather.3.cloned.1.call-start
  6.5 0.7 all-gather.3.cloned.1.call-update
  7.3 1.9 %collective-permute-start.1 = (bf16[2048,128]{1,0:T(8,128)(2,1)}, bf16[2048,128]{1,0:T(8,128)(2,1)S(1)}, u32[]{:S(2)}, u32[]{:S(2)}) collective-permute-start(bf16[2048,128]{1,0:T(8,128)(2,1)} %bitcast.11), channel_id=1, source_target_pairs={{0,1},{1,0},{2,3},{3,2},{4,5},{5,4},{6,7},{7,6},{8,9},{9,8},{10,11... | collective-permute-start | bytes 1572872 | tf_op jit(solution)/shard_map/ppermute | solution.py:344
  9.2 2.4 %collective-permute-start.2 = (bf16[2048,128]{1,0:T(8,128)(2,1)}, bf16[2048,128]{1,0:T(8,128)(2,1)S(1)}, u32[]{:S(2)}, u32[]{:S(2)}) collective-permute-start(bf16[2048,128]{1,0:T(8,128)(2,1)} %bitcast.13), channel_id=1, source_target_pairs={{0,1},{1,0},{2,3},{3,2},{4,5},{5,4},{6,7},{7,6},{8,9},{9,8},{10,11... | collective-permute-start | bytes 1572872 | tf_op jit(solution)/shard_map/ppermute | solution.py:344
  11.6 4.3 %collective-permute-start = (bf16[512,128]{1,0:T(8,128)(2,1)}, bf16[512,128]{1,0:T(8,128)(2,1)S(1)}, u32[]{:S(2)}, u32[]{:S(2)}) collective-permute-start(bf16[512,128]{1,0:T(8,128)(2,1)} %bitcast.5), channel_id=1, source_target_pairs={{0,2},{1,3},{2,4},{3,5},{4,6},{5,7},{6,8},{7,9},{8,10},{9,11},{10,... | collective-permute-start | bytes 393224 | tf_op jit(solution)/shard_map/ppermute | solution.py:344
  15.9 0.7 collective-permute-start.4
  16.6 3.7 %first_part.1 = (bf16[528,128]{1,0:T(8,128)(2,1)S(1)}, bf16[2048,128]{1,0:T(8,128)(2,1)S(1)}, bf16[2048,128]{1,0:T(8,128)(2,1)S(1)}, s32[8,128]{1,0:T(8,128)S(1)}) custom-call(s32[64]{0:T(128)} %refs_0_.1, s32[64]{0:T(128)} %refs_1_.1, bf16[512,128]{1,0:T(8,128)(2,1)} %bitcast.7, bf16[2048,128]{1,0:T(8,128)(2,1)} %bitcast.12, bf16[2048,128]{1,0:T(8,128)(2,1)} %bitcast.14), custom_call_target="tpu_custom_call" | custom-call | flops 536870912 | bytes 1048576 | tf_op jit(solution)/shard_map/first_part/pallas_call | solution.py:132
  20.3 13.9 %collective-permute-done.q_ref = bf16[512,128]{1,0:T(8,128)(2,1)S(1)} collective-permute-done((bf16[512,128]{1,0:T(8,128)(2,1)}, bf16[512,128]{1,0:T(8,128)(2,1)S(1)}, u32[]{:S(2)}, u32[]{:S(2)}) %collective-permute-start) | collective-permute-done | bytes 131104 | tf_op jit(solution)/shard_map/ppermute | solution.py:344
  34.2 0.0 collective-permute-done.1.k_other
  34.2 0.0 collective-permute-done.2.v_other
  34.2 4.7 %shard_map.64 = bf16[528,128]{1,0:T(8,128)(2,1)S(1)} custom-call(s32[8,128]{1,0:T(8,128)S(1)} %get-tuple-element.14.meta_ref, bf16[512,128]{1,0:T(8,128)(2,1)S(1)} %collective-permute-done.q_ref, bf16[2048,128]{1,0:T(8,128)(2,1)S(1)} %get-tuple-element.15.k_ref, bf16[2048,128]{1,0:T(8,128)(2,1)S(1)} %get-tuple-element.16.v_ref, ...), custom_call_target="tpu_custom_call" | custom-call | flops 1073741824 | bytes 2097152 | tf_op jit(solution)/shard_map/pallas_call | solution.py:157
  38.9 1.9 %collective-permute-start.3 = (bf16[528,128]{1,0:T(8,128)(2,1)S(1)}, bf16[528,128]{1,0:T(8,128)(2,1)S(1)}, u32[]{:S(2)}, u32[]{:S(2)}) collective-permute-start(bf16[528,128]{1,0:T(8,128)(2,1)S(1)} %shard_map.64), channel_id=1, source_target_pairs={{0,62},{1,63},{2,0},{3,1},{4,2},{5,3},{6,4},{7,5},{8,6},{9,7},{10,... | collective-permute-start | bytes 405512 | tf_op jit(solution)/shard_map/ppermute | solution.py:344
  40.9 0.0 collective-permute-done.4.q_visit
  40.9 0.0 copy-done
  40.9 2.5 %shard_map.65.refs_2_ = bf16[528,128]{1,0:T(8,128)(2,1)S(1)} custom-call(s32[8,128]{1,0:T(8,128)S(1)} %get-tuple-element.14.meta_ref, bf16[512,128]{1,0:T(8,128)(2,1)S(1)} %bitcast.8, bf16[512,128]{1,0:T(8,128)(2,1)S(1)} %collective-permute-done.4.q_visit, bf16[2048,128]{1,0:T(8,128)(2,1)S(1)} %collective-permute-done.1.k_other, ...), custom_call_target="tpu_custom_call" | custom-call | flops 536870912 | bytes 1048576 | tf_op jit(solution)/shard_map/pallas_call | solution.py:157
  43.4 0.7 collective-permute-start.5
  44.0 5.0 %collective-permute-done.3.refs_1_ = bf16[528,128]{1,0:T(8,128)(2,1)S(1)} collective-permute-done((bf16[528,128]{1,0:T(8,128)(2,1)S(1)}, bf16[528,128]{1,0:T(8,128)(2,1)S(1)}, u32[]{:S(2)}, u32[]{:S(2)}) %collective-permute-start.3) | collective-permute-done | bytes 135200 | tf_op jit(solution)/shard_map/ppermute | solution.py:344
  49.1 0.0 collective-permute-done.5.refs_3_
  49.1 0.3 combine.1
  49.4 1.9 %collective-permute-start.6 = (bf16[32,1024]{1,0:T(8,128)(2,1)S(1)}, bf16[32,1024]{1,0:T(8,128)(2,1)S(1)}, u32[]{:S(2)}, u32[]{:S(2)}) collective-permute-start(bf16[32,1024]{1,0:T(8,128)(2,1)S(1)} %get-tuple-element.18), channel_id=1, source_target_pairs={{0,256},{256,0},{1,257},{257,1},{2,258},{258,2},{3,259},{259,3},{4... | collective-permute-start | bytes 196616 | tf_op jit(solution)/shard_map/ppermute | solution.py:344
  51.3 5.2 %collective-permute-done.6.got_ref = bf16[32,1024]{1,0:T(8,128)(2,1)S(1)} collective-permute-done((bf16[32,1024]{1,0:T(8,128)(2,1)S(1)}, bf16[32,1024]{1,0:T(8,128)(2,1)S(1)}, u32[]{:S(2)}, u32[]{:S(2)}) %collective-permute-start.6) | collective-permute-done | bytes 65568 | tf_op jit(solution)/shard_map/ppermute | solution.py:344
  56.6 0.1 widen.1
  56.7 32.7 %all_to_all.10.own_ref = bf16[8,32,2048]{2,1,0:T(8,128)(2,1)S(1)} all-to-all(bf16[8,32,2048]{2,1,0:T(8,128)(2,1)S(1)} %widen.1), channel_id=1, replica_groups=mesh['y'=2,'x'=4,'Y'=4,'Z'=8,'K'=2] {'Z'}, dimensions={0} | all-to-all | bytes 2097152 | tf_op jit(solution)/shard_map/all_to_all | solution.py:376
  89.4 5.7 %collective-permute-start.7 = (bf16[8,32,2048]{2,1,0:T(8,128)(2,1)S(1)}, bf16[8,32,2048]{2,1,0:T(8,128)(2,1)S(1)}, u32[]{:S(2)}, u32[]{:S(2)}) collective-permute-start(bf16[8,32,2048]{2,1,0:T(8,128)(2,1)S(1)} %all_to_all.10.own_ref), channel_id=1, source_target_pairs={{0,1},{1,0},{2,3},{3,2},{4,5},{5,4},{6,7},{7,6},{8,9},{9,8},{10,11... | collective-permute-start | bytes 3145736 | tf_op jit(solution)/shard_map/ppermute | solution.py:344
  95.1 2.3 %collective-permute-done.7.other_ref = bf16[8,32,2048]{2,1,0:T(8,128)(2,1)S(1)} collective-permute-done((bf16[8,32,2048]{2,1,0:T(8,128)(2,1)S(1)}, bf16[8,32,2048]{2,1,0:T(8,128)(2,1)S(1)}, u32[]{:S(2)}, u32[]{:S(2)}) %collective-permute-start.7) | collective-permute-done | bytes 1048608 | tf_op jit(solution)/shard_map/ppermute | solution.py:344
  97.4 0.0 all-gather.3.cloned.1.call-done
  97.4 5.5 %project.1 = bf16[2,2,2,256,256]{4,3,2,1,0:T(8,128)(2,1)} custom-call(bf16[8,32,2048]{2,1,0:T(8,128)(2,1)S(1)} %all_to_all.10.own_ref, bf16[8,32,2048]{2,1,0:T(8,128)(2,1)S(1)} %collective-permute-done.7.other_ref, bf16[8,1024,256]{2,1,0:T(8,128)(2,1)} %bitcast.10), custom_call_target="tpu_custom_call" | custom-call | flops 2147483648 | bytes 6291456 | tf_op jit(solution)/shard_map/project/pallas_call | solution.py:269
  103.0 19.6 %all_to_all.11.in_ref = bf16[4,2,256,256]{3,2,1,0:T(8,128)(2,1)S(1)} all-to-all(bf16[4,2,256,256]{3,2,1,0:T(8,128)(2,1)} %bitcast.9), channel_id=1, replica_groups=mesh['y'=2,'x'=4,'Y'=4,'Z'=8,'K'=2] {'x'}, dimensions={0} | all-to-all | bytes 2097152 | tf_op jit(solution)/shard_map/all_to_all | solution.py:380
  122.6 0.1 totals.1
  122.7 3.6 %collective-permute-start.8 = (bf16[256,256]{1,0:T(8,128)(2,1)S(1)}, bf16[256,256]{1,0:T(8,128)(2,1)S(1)}, u32[]{:S(2)}, u32[]{:S(2)}) collective-permute-start(bf16[256,256]{1,0:T(8,128)(2,1)S(1)} %get-tuple-element.19), channel_id=1, source_target_pairs={{0,0},{16,128},{32,256},{48,384},{64,64},{80,192},{96,320},{112,44... | collective-permute-start | bytes 393224 | tf_op jit(solution)/shard_map/ppermute | solution.py:391
  126.3 1.9 %collective-permute-start.9 = (bf16[256,256]{1,0:T(8,128)(2,1)S(1)}, bf16[256,256]{1,0:T(8,128)(2,1)S(1)}, u32[]{:S(2)}, u32[]{:S(2)}) collective-permute-start(bf16[256,256]{1,0:T(8,128)(2,1)S(1)} %get-tuple-element.20), channel_id=1, source_target_pairs={{0,16},{16,144},{32,272},{48,400},{64,80},{80,208},{96,336},{112,4... | collective-permute-start | bytes 393224 | tf_op jit(solution)/shard_map/ppermute | solution.py:391
  128.2 16.5 %collective-permute-done.8.refs_0_ = bf16[256,256]{1,0:T(8,128)(2,1)S(1)} collective-permute-done((bf16[256,256]{1,0:T(8,128)(2,1)S(1)}, bf16[256,256]{1,0:T(8,128)(2,1)S(1)}, u32[]{:S(2)}, u32[]{:S(2)}) %collective-permute-start.8) | collective-permute-done | bytes 131104 | tf_op jit(solution)/shard_map/ppermute | solution.py:391
  144.7 0.0 collective-permute-done.9.refs_1_
  144.7 0.7 in_order.1
Async XLA Ops:
  6.5 34.3 %copy-start = (bf16[64,8,128]{2,1,0:T(8,128)(2,1)S(1)}, bf16[64,8,128]{2,1,0:T(8,128)(2,1)}, u32[]{:S(2)}) copy-start(bf16[64,8,128]{2,1,0:T(8,128)(2,1)} %param.6) | copy-start | bytes 393220
  6.5 90.9 %all-gather.3.cloned.1.call-start = ((), (), s32[]{:S(2)}) async-start(), calls=%async_computation.2 | async-start | bytes 4718592 | tf_op jit(solution)/shard_map/all_gather | solution.py:358
  7.3 26.9 %collective-permute-start.1 = (bf16[2048,128]{1,0:T(8,128)(2,1)}, bf16[2048,128]{1,0:T(8,128)(2,1)S(1)}, u32[]{:S(2)}, u32[]{:S(2)}) collective-permute-start(bf16[2048,128]{1,0:T(8,128)(2,1)} %bitcast.11), channel_id=1, source_target_pairs={{0,1},{1,0},{2,3},{3,2},{4,5},{5,4},{6,7},{7,6},{8,9},{9,8},{10,11... | collective-permute-start | bytes 1572872 | tf_op jit(solution)/shard_map/ppermute | solution.py:344
  9.2 25.0 %collective-permute-start.2 = (bf16[2048,128]{1,0:T(8,128)(2,1)}, bf16[2048,128]{1,0:T(8,128)(2,1)S(1)}, u32[]{:S(2)}, u32[]{:S(2)}) collective-permute-start(bf16[2048,128]{1,0:T(8,128)(2,1)} %bitcast.13), channel_id=1, source_target_pairs={{0,1},{1,0},{2,3},{3,2},{4,5},{5,4},{6,7},{7,6},{8,9},{9,8},{10,11... | collective-permute-start | bytes 1572872 | tf_op jit(solution)/shard_map/ppermute | solution.py:344
  11.6 22.6 %collective-permute-start = (bf16[512,128]{1,0:T(8,128)(2,1)}, bf16[512,128]{1,0:T(8,128)(2,1)S(1)}, u32[]{:S(2)}, u32[]{:S(2)}) collective-permute-start(bf16[512,128]{1,0:T(8,128)(2,1)} %bitcast.5), channel_id=1, source_target_pairs={{0,2},{1,3},{2,4},{3,5},{4,6},{5,7},{6,8},{7,9},{8,10},{9,11},{10,... | collective-permute-start | bytes 393224 | tf_op jit(solution)/shard_map/ppermute | solution.py:344
  15.9 25.0 %collective-permute-start.4 = (bf16[512,128]{1,0:T(8,128)(2,1)}, bf16[512,128]{1,0:T(8,128)(2,1)S(1)}, u32[]{:S(2)}, u32[]{:S(2)}) collective-permute-start(bf16[512,128]{1,0:T(8,128)(2,1)} %bitcast.6), channel_id=1, source_target_pairs={{1,5},{3,7},{5,9},{7,11},{9,13},{11,15},{13,17},{15,19},{17,21},{1... | collective-permute-start | bytes 393224 | tf_op jit(solution)/shard_map/ppermute | solution.py:355
  38.9 10.1 %collective-permute-start.3 = (bf16[528,128]{1,0:T(8,128)(2,1)S(1)}, bf16[528,128]{1,0:T(8,128)(2,1)S(1)}, u32[]{:S(2)}, u32[]{:S(2)}) collective-permute-start(bf16[528,128]{1,0:T(8,128)(2,1)S(1)} %shard_map.64), channel_id=1, source_target_pairs={{0,62},{1,63},{2,0},{3,1},{4,2},{5,3},{6,4},{7,5},{8,6},{9,7},{10,... | collective-permute-start | bytes 405512 | tf_op jit(solution)/shard_map/ppermute | solution.py:344
  43.4 5.7 %collective-permute-start.5 = (bf16[528,128]{1,0:T(8,128)(2,1)S(1)}, bf16[528,128]{1,0:T(8,128)(2,1)S(1)}, u32[]{:S(2)}, u32[]{:S(2)}) collective-permute-start(bf16[528,128]{1,0:T(8,128)(2,1)S(1)} %shard_map.65.refs_2_), channel_id=1, source_target_pairs={{1,61},{3,63},{5,1},{7,3},{9,5},{11,7},{13,9},{15,11},{17,13},{19,... | collective-permute-start | bytes 405512 | tf_op jit(solution)/shard_map/ppermute | solution.py:372
  49.4 7.2 %collective-permute-start.6 = (bf16[32,1024]{1,0:T(8,128)(2,1)S(1)}, bf16[32,1024]{1,0:T(8,128)(2,1)S(1)}, u32[]{:S(2)}, u32[]{:S(2)}) collective-permute-start(bf16[32,1024]{1,0:T(8,128)(2,1)S(1)} %get-tuple-element.18), channel_id=1, source_target_pairs={{0,256},{256,0},{1,257},{257,1},{2,258},{258,2},{3,259},{259,3},{4... | collective-permute-start | bytes 196616 | tf_op jit(solution)/shard_map/ppermute | solution.py:344
  89.4 8.0 %collective-permute-start.7 = (bf16[8,32,2048]{2,1,0:T(8,128)(2,1)S(1)}, bf16[8,32,2048]{2,1,0:T(8,128)(2,1)S(1)}, u32[]{:S(2)}, u32[]{:S(2)}) collective-permute-start(bf16[8,32,2048]{2,1,0:T(8,128)(2,1)S(1)} %all_to_all.10.own_ref), channel_id=1, source_target_pairs={{0,1},{1,0},{2,3},{3,2},{4,5},{5,4},{6,7},{7,6},{8,9},{9,8},{10,11... | collective-permute-start | bytes 3145736 | tf_op jit(solution)/shard_map/ppermute | solution.py:344
  122.7 22.0 %collective-permute-start.8 = (bf16[256,256]{1,0:T(8,128)(2,1)S(1)}, bf16[256,256]{1,0:T(8,128)(2,1)S(1)}, u32[]{:S(2)}, u32[]{:S(2)}) collective-permute-start(bf16[256,256]{1,0:T(8,128)(2,1)S(1)} %get-tuple-element.19), channel_id=1, source_target_pairs={{0,0},{16,128},{32,256},{48,384},{64,64},{80,192},{96,320},{112,44... | collective-permute-start | bytes 393224 | tf_op jit(solution)/shard_map/ppermute | solution.py:391
  126.3 18.4 %collective-permute-start.9 = (bf16[256,256]{1,0:T(8,128)(2,1)S(1)}, bf16[256,256]{1,0:T(8,128)(2,1)S(1)}, u32[]{:S(2)}, u32[]{:S(2)}) collective-permute-start(bf16[256,256]{1,0:T(8,128)(2,1)S(1)} %get-tuple-element.20), channel_id=1, source_target_pairs={{0,16},{16,144},{32,272},{48,400},{64,80},{80,208},{96,336},{112,4... | collective-permute-start | bytes 393224 | tf_op jit(solution)/shard_map/ppermute | solution.py:391
Sparse Core Ops, SparseCore 0:
  9.4 69.4 all-gather.2

commit v7 on v6

--- a/solution.py
+++ b/solution.py
@@ -166,7 +166,7 @@
 
 
 def combine_kernel(*refs):
-    parts, keep_ref, send_ref, total_ref = refs[:-3], refs[-3], refs[-2], refs[-1]
+    parts, out_ref, total_ref = refs[:-2], refs[-2], refs[-1]
     head_size = parts[0].shape[1]
     groups = parts[0].shape[0] // (TILE + 4)
     rows = groups * TILE
@@ -196,25 +196,24 @@
             term = taken(part, group * TILE, (group + 1) * TILE).astype(F32) * column
             total = term if total is None else total + term
         total_ref[group * TILE : (group + 1) * TILE, :] = total
-    count = keep_ref.shape[0]
+    copies, count, _ = out_ref.shape
     heads = rows // (2 * count)
-    lead = lax.axis_index("y") == 0
     for head in range(heads):
-        first = total_ref[pl.ds(head, count, stride=heads), :].astype(BF16)
-        second = total_ref[pl.ds(heads * count + head, count, stride=heads), :].astype(BF16)
         columns = slice(head * head_size, (head + 1) * head_size)
-        keep_ref[:, columns] = jnp.where(lead, first, second)
-        send_ref[:, columns] = jnp.where(lead, second, first)
-
-
-def combine(parts, tokens, heads):
+        for half in range(2):
+            start = half * heads * count + head
+            piece = total_ref[pl.ds(start, count, stride=heads), :].astype(BF16)
+            for copy in range(half * copies // 2, (half + 1) * copies // 2):
+                out_ref[copy, :, columns] = piece
+
+
+def combine(parts, copies, tokens, heads):
     head_size = parts[0].shape[1]
-    half = jax.ShapeDtypeStruct((tokens // 2, heads * head_size), BF16)
     return pl.pallas_call(
         combine_kernel,
-        out_shape=(half, half),
+        out_shape=jax.ShapeDtypeStruct((2 * copies, tokens // 2, heads * head_size), BF16),
         in_specs=[VMEM] * len(parts),
-        out_specs=(VMEM, VMEM),
+        out_specs=VMEM,
         scratch_shapes=[pltpu.VMEM((heads * tokens, head_size), F32)],
         compiler_params=pltpu.CompilerParams(vmem_limit_bytes=8 << 20),
         cost_estimate=pl.CostEstimate(
@@ -224,59 +223,38 @@
     )(*parts)
 
 
-def widen_kernel(keep_ref, got_ref, out_ref):
-    width = keep_ref.shape[1]
-    for copy in range(out_ref.shape[0]):
-        out_ref[copy, :, :width] = keep_ref[...]
-        out_ref[copy, :, width:] = got_ref[...]
-
-
-def widen(keep, got, copies):
-    rows, width = keep.shape
-    return pl.pallas_call(
-        widen_kernel,
-        out_shape=jax.ShapeDtypeStruct((copies, rows, 2 * width), BF16),
-        in_specs=[VMEM] * 2,
-        out_specs=VMEM,
-        compiler_params=pltpu.CompilerParams(vmem_limit_bytes=8 << 20),
-        cost_estimate=pl.CostEstimate(
-            flops=1 << 18, bytes_accessed=1 << 20, transcendentals=0
-        ),
-        name="widen",
-    )(keep, got)
-
-
 def project_kernel(own_ref, other_ref, w_ref, out_ref):
-    groups, rows, width = own_ref.shape
-    depth = width // 2
-    pair = lax.axis_index("y")
-    w_own, w_other = w_ref[pair], w_ref[1 - pair]
+    groups, rows, depth = own_ref.shape
+    count = groups // 2
+    half = count * rows // 2
     for slot, ref in enumerate((own_ref, other_ref)):
-        lhs = ref[...].reshape(groups * rows, width)
-        part = jnp.dot(lhs[:, :depth], w_own, preferred_element_type=F32)
-        part += jnp.dot(lhs[:, depth:], w_other, preferred_element_type=F32)
+        part = None
+        for i in range(2):
+            lhs = ref[i * count : (i + 1) * count].reshape(count * rows, depth)
+            term = jnp.dot(lhs, w_ref[i], preferred_element_type=F32)
+            part = term if part is None else part + term
         part = part.astype(BF16)
-        half = groups * rows // 2
         for i in range(2):
             out_ref[0, i, 0, slot * half : (slot + 1) * half, :] = part[i * half : (i + 1) * half]
 
 
 def project(own, other, weights):
-    groups, rows, width = own.shape
-    depth, columns = weights.shape[1:]
+    groups, rows, depth = own.shape
+    columns = weights.shape[2]
     pieces = weights.shape[0] // 2
-    side = pl.BlockSpec((groups, rows, width), lambda i: (0, 0, 0))
+    held = groups * rows
+    side = pl.BlockSpec((groups, rows, depth), lambda i: (0, 0, 0))
     return pl.pallas_call(
         project_kernel,
         grid=(pieces,),
-        out_shape=pltpu.HBM((pieces // 2, 2, 2, groups * rows, columns), BF16),
+        out_shape=pltpu.HBM((pieces // 2, 2, 2, held // 2, columns), BF16),
         in_specs=[side, side, pl.BlockSpec((2, depth, columns), lambda i: (i, 0, 0))],
         out_specs=pl.BlockSpec(
-            (1, 2, 1, groups * rows, columns), lambda i: (i // 2, 0, i % 2, 0, 0)
+            (1, 2, 1, held // 2, columns), lambda i: (i // 2, 0, i % 2, 0, 0)
         ),
         compiler_params=pltpu.CompilerParams(vmem_limit_bytes=24 << 20),
         cost_estimate=pl.CostEstimate(
-            flops=4 * groups * rows * width * columns * pieces,
+            flops=4 * held * depth * columns * pieces,
             bytes_accessed=6 << 20,
             transcendentals=0,
         ),
@@ -370,10 +348,8 @@
         meta, q_own, q_far, k_other, v_other,
     )
     back_far = lax.ppermute(part_far, BLK, [(i, (i - 4) % shard_count) for i in odd])
-    keep, send = combine([part_own, back_near, part_far, back_far], tokens, heads)
-    got = passed_along(send, "y", 1)
-    wide = widen(keep, got, z_count)
-    own = lax.all_to_all(wide, "Z", split_axis=0, concat_axis=0, tiled=True)
+    halves = combine([part_own, back_near, part_far, back_far], z_count, tokens, heads)
+    own = lax.all_to_all(halves, ("y", "Z"), split_axis=0, concat_axis=0, tiled=True)
     other = passed_along(own, "K", 1)
     partial = project(own, other, weights)
     partial = partial.reshape(-1, *partial.shape[2:])

time: 153 us -> 144 us (0.941)
  waiting for transfers between devices: 43.6 us -> 37.8 us
  starting transfers between devices: 25 us -> 21.5 us
    ppermute x6 -> x5, waiting for transfers between devices: 26.4 us -> 21.2 us  [passed_along(): lax.ppermute(value, axis, [(i, (i + steps) % count) for i in range(count)])]
    ppermute x6 -> x5, starting transfers between devices: 18.2 us -> 14 us  [passed_along(): lax.ppermute(value, axis, [(i, (i + steps) % count) for i in range(count)])]
  transfers between devices with their start and end apart: 11 -> 10, of which waited for: 5 -> 4; matrix products, arithmetic and copies ran while one was open for 0% -> 0% of each run, Pallas kernels for 7% -> 8%
where the time goes in v7:
time: 144 us; the launch traced here: 143 us
  blocking collectives  52.8 us (37%)
  waiting for transfers between devices  37.8 us (26%)
  starting transfers between devices  21.5 us (15%)
  Pallas kernels  17.7 us (12%)
  between operations  13.5 us (9%)
    all_to_all x1, blocking collectives, on_device(): lax.all_to_all(halves, ('y', 'Z'), split_axis=0, concat_axis=0, tiled=True)  33 us
    ppermute x5, waiting for transfers between devices, passed_along(): lax.ppermute(value, axis, [(i, (i + steps) % count) for i in range(count)])  21.2 us
    all_to_all x1, blocking collectives, on_device(): lax.all_to_all(partial, 'x', split_axis=0, concat_axis=0, tiled=True)  19.9 us
    ppermute x2, waiting for transfers between devices, on_device(): placed.append(lax.ppermute(summed[k], ('y', 'x', 'Y'), pairs))  15.9 us
    ppermute x5, starting transfers between devices, passed_along(): lax.ppermute(value, axis, [(i, (i + steps) % count) for i in range(count)])  14 us
    pallas_call x2, Pallas kernels, later_part(): pl.pallas_call(functools.partial(kernel, tokens), out_shape=jax.ShapeDtyp...  7.19 us
    ppermute x2, starting transfers between devices, on_device(): placed.append(lax.ppermute(summed[k], ('y', 'x', 'Y'), pairs))  6.21 us
    pallas_call x1, Pallas kernels, project(): pl.pallas_call(project_kernel, grid=(pieces,), out_shape=pltpu.HBM((piece...  5.53 us
  transfers between devices with their start and end apart: 10, of which 4 were waited for; matrix products, arithmetic and copies ran while one was open for 0% of the time, Pallas kernels for 8%

profile of v7, /device:TPU:8, one launch (start us, length us, event | category | flops | bytes accessed | tf_op | source)
XLA Modules:
  0.0 143.4 jit_solution(5435382550170318231)
XLA Ops:
  6.5 0.0 copy-start
  6.5 0.0 all-gather.3.cloned.1.call-start
  6.5 0.7 all-gather.3.cloned.1.call-update
  7.3 1.9 %collective-permute-start.1 = (bf16[2048,128]{1,0:T(8,128)(2,1)}, bf16[2048,128]{1,0:T(8,128)(2,1)S(1)}, u32[]{:S(2)}, u32[]{:S(2)}) collective-permute-start(bf16[2048,128]{1,0:T(8,128)(2,1)} %bitcast.11), channel_id=1, source_target_pairs={{0,1},{1,0},{2,3},{3,2},{4,5},{5,4},{6,7},{7,6},{8,9},{9,8},{10,11... | collective-permute-start | bytes 1572872 | tf_op jit(solution)/shard_map/ppermute | solution.py:322
  9.2 2.4 %collective-permute-start.2 = (bf16[2048,128]{1,0:T(8,128)(2,1)}, bf16[2048,128]{1,0:T(8,128)(2,1)S(1)}, u32[]{:S(2)}, u32[]{:S(2)}) collective-permute-start(bf16[2048,128]{1,0:T(8,128)(2,1)} %bitcast.13), channel_id=1, source_target_pairs={{0,1},{1,0},{2,3},{3,2},{4,5},{5,4},{6,7},{7,6},{8,9},{9,8},{10,11... | collective-permute-start | bytes 1572872 | tf_op jit(solution)/shard_map/ppermute | solution.py:322
  11.6 4.3 %collective-permute-start = (bf16[512,128]{1,0:T(8,128)(2,1)}, bf16[512,128]{1,0:T(8,128)(2,1)S(1)}, u32[]{:S(2)}, u32[]{:S(2)}) collective-permute-start(bf16[512,128]{1,0:T(8,128)(2,1)} %bitcast.5), channel_id=1, source_target_pairs={{0,2},{1,3},{2,4},{3,5},{4,6},{5,7},{6,8},{7,9},{8,10},{9,11},{10,... | collective-permute-start | bytes 393224 | tf_op jit(solution)/shard_map/ppermute | solution.py:322
  15.9 0.7 collective-permute-start.4
  16.6 3.7 %first_part.1 = (bf16[528,128]{1,0:T(8,128)(2,1)S(1)}, bf16[2048,128]{1,0:T(8,128)(2,1)S(1)}, bf16[2048,128]{1,0:T(8,128)(2,1)S(1)}, s32[8,128]{1,0:T(8,128)S(1)}) custom-call(s32[64]{0:T(128)} %refs_0_.1, s32[64]{0:T(128)} %refs_1_.1, bf16[512,128]{1,0:T(8,128)(2,1)} %bitcast.7, bf16[2048,128]{1,0:T(8,128)(2,1)} %bitcast.12, bf16[2048,128]{1,0:T(8,128)(2,1)} %bitcast.14), custom_call_target="tpu_custom_call" | custom-call | flops 536870912 | bytes 1048576 | tf_op jit(solution)/shard_map/first_part/pallas_call | solution.py:132
  20.3 13.9 %collective-permute-done.q_ref = bf16[512,128]{1,0:T(8,128)(2,1)S(1)} collective-permute-done((bf16[512,128]{1,0:T(8,128)(2,1)}, bf16[512,128]{1,0:T(8,128)(2,1)S(1)}, u32[]{:S(2)}, u32[]{:S(2)}) %collective-permute-start) | collective-permute-done | bytes 131104 | tf_op jit(solution)/shard_map/ppermute | solution.py:322
  34.2 0.0 collective-permute-done.1.k_other
  34.2 0.0 collective-permute-done.2.v_other
  34.2 4.7 %shard_map.64 = bf16[528,128]{1,0:T(8,128)(2,1)S(1)} custom-call(s32[8,128]{1,0:T(8,128)S(1)} %get-tuple-element.12.meta_ref, bf16[512,128]{1,0:T(8,128)(2,1)S(1)} %collective-permute-done.q_ref, bf16[2048,128]{1,0:T(8,128)(2,1)S(1)} %get-tuple-element.13.k_ref, bf16[2048,128]{1,0:T(8,128)(2,1)S(1)} %get-tuple-element.14.v_ref, ...), custom_call_target="tpu_custom_call" | custom-call | flops 1073741824 | bytes 2097152 | tf_op jit(solution)/shard_map/pallas_call | solution.py:157
  38.9 1.9 %collective-permute-start.3 = (bf16[528,128]{1,0:T(8,128)(2,1)S(1)}, bf16[528,128]{1,0:T(8,128)(2,1)S(1)}, u32[]{:S(2)}, u32[]{:S(2)}) collective-permute-start(bf16[528,128]{1,0:T(8,128)(2,1)S(1)} %shard_map.64), channel_id=1, source_target_pairs={{0,62},{1,63},{2,0},{3,1},{4,2},{5,3},{6,4},{7,5},{8,6},{9,7},{10,... | collective-permute-start | bytes 405512 | tf_op jit(solution)/shard_map/ppermute | solution.py:322
  40.9 0.0 collective-permute-done.4.q_visit
  40.9 0.0 copy-done
  40.9 2.5 %shard_map.65.refs_2_ = bf16[528,128]{1,0:T(8,128)(2,1)S(1)} custom-call(s32[8,128]{1,0:T(8,128)S(1)} %get-tuple-element.12.meta_ref, bf16[512,128]{1,0:T(8,128)(2,1)S(1)} %bitcast.8, bf16[512,128]{1,0:T(8,128)(2,1)S(1)} %collective-permute-done.4.q_visit, bf16[2048,128]{1,0:T(8,128)(2,1)S(1)} %collective-permute-done.1.k_other, ...), custom_call_target="tpu_custom_call" | custom-call | flops 536870912 | bytes 1048576 | tf_op jit(solution)/shard_map/pallas_call | solution.py:157
  43.4 0.7 collective-permute-start.5
  44.0 5.0 %collective-permute-done.3.refs_1_ = bf16[528,128]{1,0:T(8,128)(2,1)S(1)} collective-permute-done((bf16[528,128]{1,0:T(8,128)(2,1)S(1)}, bf16[528,128]{1,0:T(8,128)(2,1)S(1)}, u32[]{:S(2)}, u32[]{:S(2)}) %collective-permute-start.3) | collective-permute-done | bytes 135200 | tf_op jit(solution)/shard_map/ppermute | solution.py:322
  49.1 0.0 collective-permute-done.5.refs_3_
  49.1 0.4 combine.1
  49.5 33.0 %all_to_all.10.own_ref = bf16[16,32,1024]{2,1,0:T(8,128)(2,1)S(1)} all-to-all(bf16[16,32,1024]{2,1,0:T(8,128)(2,1)S(1)} %combine.1), channel_id=1, replica_groups=mesh['y'=2,'x'=4,'Y'=4,'Z'=8,'K'=2] {'y','Z'}, dimensions={0} | all-to-all | bytes 2097152 | tf_op jit(solution)/shard_map/all_to_all | solution.py:352
  82.5 3.4 %collective-permute-start.6 = (bf16[16,32,1024]{2,1,0:T(8,128)(2,1)S(1)}, bf16[16,32,1024]{2,1,0:T(8,128)(2,1)S(1)}, u32[]{:S(2)}, u32[]{:S(2)}) collective-permute-start(bf16[16,32,1024]{2,1,0:T(8,128)(2,1)S(1)} %all_to_all.10.own_ref), channel_id=1, source_target_pairs={{0,1},{1,0},{2,3},{3,2},{4,5},{5,4},{6,7},{7,6},{8,9},{9,8},{10,11... | collective-permute-start | bytes 3145736 | tf_op jit(solution)/shard_map/ppermute | solution.py:322
  85.9 2.3 %collective-permute-done.6.other_ref = bf16[16,32,1024]{2,1,0:T(8,128)(2,1)S(1)} collective-permute-done((bf16[16,32,1024]{2,1,0:T(8,128)(2,1)S(1)}, bf16[16,32,1024]{2,1,0:T(8,128)(2,1)S(1)}, u32[]{:S(2)}, u32[]{:S(2)}) %collective-permute-start.6) | collective-permute-done | bytes 1048608 | tf_op jit(solution)/shard_map/ppermute | solution.py:322
  88.2 0.0 all-gather.3.cloned.1.call-done
  88.2 5.5 %project.1 = bf16[2,2,2,256,256]{4,3,2,1,0:T(8,128)(2,1)} custom-call(bf16[16,32,1024]{2,1,0:T(8,128)(2,1)S(1)} %all_to_all.10.own_ref, bf16[16,32,1024]{2,1,0:T(8,128)(2,1)S(1)} %collective-permute-done.6.other_ref, bf16[8,1024,256]{2,1,0:T(8,128)(2,1)} %bitcast.10), custom_call_target="tpu_custom_call" | custom-call | flops 2147483648 | bytes 6291456 | tf_op jit(solution)/shard_map/project/pallas_call | solution.py:247
  93.7 19.9 %all_to_all.11.in_ref = bf16[4,2,256,256]{3,2,1,0:T(8,128)(2,1)S(1)} all-to-all(bf16[4,2,256,256]{3,2,1,0:T(8,128)(2,1)} %bitcast.9), channel_id=1, replica_groups=mesh['y'=2,'x'=4,'Y'=4,'Z'=8,'K'=2] {'x'}, dimensions={0} | all-to-all | bytes 2097152 | tf_op jit(solution)/shard_map/all_to_all | solution.py:356
  113.6 0.1 totals.1
  113.7 4.3 %collective-permute-start.7 = (bf16[256,256]{1,0:T(8,128)(2,1)S(1)}, bf16[256,256]{1,0:T(8,128)(2,1)S(1)}, u32[]{:S(2)}, u32[]{:S(2)}) collective-permute-start(bf16[256,256]{1,0:T(8,128)(2,1)S(1)} %get-tuple-element.15), channel_id=1, source_target_pairs={{0,0},{16,128},{32,256},{48,384},{64,64},{80,192},{96,320},{112,44... | collective-permute-start | bytes 393224 | tf_op jit(solution)/shard_map/ppermute | solution.py:367
  118.0 1.9 %collective-permute-start.8 = (bf16[256,256]{1,0:T(8,128)(2,1)S(1)}, bf16[256,256]{1,0:T(8,128)(2,1)S(1)}, u32[]{:S(2)}, u32[]{:S(2)}) collective-permute-start(bf16[256,256]{1,0:T(8,128)(2,1)S(1)} %get-tuple-element.16), channel_id=1, source_target_pairs={{0,16},{16,144},{32,272},{48,400},{64,80},{80,208},{96,336},{112,4... | collective-permute-start | bytes 393224 | tf_op jit(solution)/shard_map/ppermute | solution.py:367
  119.9 15.9 %collective-permute-done.7.refs_0_ = bf16[256,256]{1,0:T(8,128)(2,1)S(1)} collective-permute-done((bf16[256,256]{1,0:T(8,128)(2,1)S(1)}, bf16[256,256]{1,0:T(8,128)(2,1)S(1)}, u32[]{:S(2)}, u32[]{:S(2)}) %collective-permute-start.7) | collective-permute-done | bytes 131104 | tf_op jit(solution)/shard_map/ppermute | solution.py:367
  135.9 0.0 collective-permute-done.8.refs_1_
  135.9 0.7 in_order.1
Async XLA Ops:
  6.5 34.3 %copy-start = (bf16[64,8,128]{2,1,0:T(8,128)(2,1)S(1)}, bf16[64,8,128]{2,1,0:T(8,128)(2,1)}, u32[]{:S(2)}) copy-start(bf16[64,8,128]{2,1,0:T(8,128)(2,1)} %param.6) | copy-start | bytes 393220
  6.5 81.6 %all-gather.3.cloned.1.call-start = ((), (), s32[]{:S(2)}) async-start(), calls=%async_computation.2 | async-start | bytes 4718592 | tf_op jit(solution)/shard_map/all_gather | solution.py:336
  7.3 26.9 %collective-permute-start.1 = (bf16[2048,128]{1,0:T(8,128)(2,1)}, bf16[2048,128]{1,0:T(8,128)(2,1)S(1)}, u32[]{:S(2)}, u32[]{:S(2)}) collective-permute-start(bf16[2048,128]{1,0:T(8,128)(2,1)} %bitcast.11), channel_id=1, source_target_pairs={{0,1},{1,0},{2,3},{3,2},{4,5},{5,4},{6,7},{7,6},{8,9},{9,8},{10,11... | collective-permute-start | bytes 1572872 | tf_op jit(solution)/shard_map/ppermute | solution.py:322
  9.2 25.0 %collective-permute-start.2 = (bf16[2048,128]{1,0:T(8,128)(2,1)}, bf16[2048,128]{1,0:T(8,128)(2,1)S(1)}, u32[]{:S(2)}, u32[]{:S(2)}) collective-permute-start(bf16[2048,128]{1,0:T(8,128)(2,1)} %bitcast.13), channel_id=1, source_target_pairs={{0,1},{1,0},{2,3},{3,2},{4,5},{5,4},{6,7},{7,6},{8,9},{9,8},{10,11... | collective-permute-start | bytes 1572872 | tf_op jit(solution)/shard_map/ppermute | solution.py:322
  11.6 22.6 %collective-permute-start = (bf16[512,128]{1,0:T(8,128)(2,1)}, bf16[512,128]{1,0:T(8,128)(2,1)S(1)}, u32[]{:S(2)}, u32[]{:S(2)}) collective-permute-start(bf16[512,128]{1,0:T(8,128)(2,1)} %bitcast.5), channel_id=1, source_target_pairs={{0,2},{1,3},{2,4},{3,5},{4,6},{5,7},{6,8},{7,9},{8,10},{9,11},{10,... | collective-permute-start | bytes 393224 | tf_op jit(solution)/shard_map/ppermute | solution.py:322
  15.9 25.0 %collective-permute-start.4 = (bf16[512,128]{1,0:T(8,128)(2,1)}, bf16[512,128]{1,0:T(8,128)(2,1)S(1)}, u32[]{:S(2)}, u32[]{:S(2)}) collective-permute-start(bf16[512,128]{1,0:T(8,128)(2,1)} %bitcast.6), channel_id=1, source_target_pairs={{1,5},{3,7},{5,9},{7,11},{9,13},{11,15},{13,17},{15,19},{17,21},{1... | collective-permute-start | bytes 393224 | tf_op jit(solution)/shard_map/ppermute | solution.py:333
  38.9 10.1 %collective-permute-start.3 = (bf16[528,128]{1,0:T(8,128)(2,1)S(1)}, bf16[528,128]{1,0:T(8,128)(2,1)S(1)}, u32[]{:S(2)}, u32[]{:S(2)}) collective-permute-start(bf16[528,128]{1,0:T(8,128)(2,1)S(1)} %shard_map.64), channel_id=1, source_target_pairs={{0,62},{1,63},{2,0},{3,1},{4,2},{5,3},{6,4},{7,5},{8,6},{9,7},{10,... | collective-permute-start | bytes 405512 | tf_op jit(solution)/shard_map/ppermute | solution.py:322
  43.4 5.7 %collective-permute-start.5 = (bf16[528,128]{1,0:T(8,128)(2,1)S(1)}, bf16[528,128]{1,0:T(8,128)(2,1)S(1)}, u32[]{:S(2)}, u32[]{:S(2)}) collective-permute-start(bf16[528,128]{1,0:T(8,128)(2,1)S(1)} %shard_map.65.refs_2_), channel_id=1, source_target_pairs={{1,61},{3,63},{5,1},{7,3},{9,5},{11,7},{13,9},{15,11},{17,13},{19,... | collective-permute-start | bytes 405512 | tf_op jit(solution)/shard_map/ppermute | solution.py:350
  82.5 5.7 %collective-permute-start.6 = (bf16[16,32,1024]{2,1,0:T(8,128)(2,1)S(1)}, bf16[16,32,1024]{2,1,0:T(8,128)(2,1)S(1)}, u32[]{:S(2)}, u32[]{:S(2)}) collective-permute-start(bf16[16,32,1024]{2,1,0:T(8,128)(2,1)S(1)} %all_to_all.10.own_ref), channel_id=1, source_target_pairs={{0,1},{1,0},{2,3},{3,2},{4,5},{5,4},{6,7},{7,6},{8,9},{9,8},{10,11... | collective-permute-start | bytes 3145736 | tf_op jit(solution)/shard_map/ppermute | solution.py:322
  113.7 22.2 %collective-permute-start.7 = (bf16[256,256]{1,0:T(8,128)(2,1)S(1)}, bf16[256,256]{1,0:T(8,128)(2,1)S(1)}, u32[]{:S(2)}, u32[]{:S(2)}) collective-permute-start(bf16[256,256]{1,0:T(8,128)(2,1)S(1)} %get-tuple-element.15), channel_id=1, source_target_pairs={{0,0},{16,128},{32,256},{48,384},{64,64},{80,192},{96,320},{112,44... | collective-permute-start | bytes 393224 | tf_op jit(solution)/shard_map/ppermute | solution.py:367
  118.0 17.9 %collective-permute-start.8 = (bf16[256,256]{1,0:T(8,128)(2,1)S(1)}, bf16[256,256]{1,0:T(8,128)(2,1)S(1)}, u32[]{:S(2)}, u32[]{:S(2)}) collective-permute-start(bf16[256,256]{1,0:T(8,128)(2,1)S(1)} %get-tuple-element.16), channel_id=1, source_target_pairs={{0,16},{16,144},{32,272},{48,400},{64,80},{80,208},{96,336},{112,4... | collective-permute-start | bytes 393224 | tf_op jit(solution)/shard_map/ppermute | solution.py:367
Sparse Core Ops, SparseCore 0:
  9.4 78.0 all-gather.2

commit v8 on v7

--- a/solution.py
+++ b/solution.py
@@ -226,16 +226,18 @@
 def project_kernel(own_ref, other_ref, w_ref, out_ref):
     groups, rows, depth = own_ref.shape
     count = groups // 2
+    part = None
+    for i in range(2):
+        sides = [ref[i * count : (i + 1) * count] for ref in (own_ref, other_ref)]
+        lhs = jnp.concatenate([side.reshape(count * rows, depth) for side in sides], axis=0)
+        term = jnp.dot(lhs, w_ref[i], preferred_element_type=F32)
+        part = term if part is None else part + term
+    part = part.astype(BF16)
     half = count * rows // 2
-    for slot, ref in enumerate((own_ref, other_ref)):
-        part = None
+    for slot in range(2):
         for i in range(2):
-            lhs = ref[i * count : (i + 1) * count].reshape(count * rows, depth)
-            term = jnp.dot(lhs, w_ref[i], preferred_element_type=F32)
-            part = term if part is None else part + term
-        part = part.astype(BF16)
-        for i in range(2):
-            out_ref[0, i, 0, slot * half : (slot + 1) * half, :] = part[i * half : (i + 1) * half]
+            start = (2 * slot + i) * half
+            out_ref[0, i, slot * half : (slot + 1) * half, :] = part[start : start + half]
 
 
 def project(own, other, weights):
@@ -247,11 +249,9 @@
     return pl.pallas_call(
         project_kernel,
         grid=(pieces,),
-        out_shape=pltpu.HBM((pieces // 2, 2, 2, held // 2, columns), BF16),
+        out_shape=pltpu.HBM((pieces, 2, held // 2, columns), BF16),
         in_specs=[side, side, pl.BlockSpec((2, depth, columns), lambda i: (i, 0, 0))],
-        out_specs=pl.BlockSpec(
-            (1, 2, 1, held // 2, columns), lambda i: (i // 2, 0, i % 2, 0, 0)
-        ),
+        out_specs=pl.BlockSpec((1, 2, held // 2, columns), lambda i: (i, 0, 0, 0)),
         compiler_params=pltpu.CompilerParams(vmem_limit_bytes=24 << 20),
         cost_estimate=pl.CostEstimate(
             flops=4 * held * depth * columns * pieces,
@@ -262,59 +262,34 @@
     )(own, other, pltpu.with_memory_space_constraint(weights, pltpu.HBM))
 
 
-def total_kernel(in_ref, *out_refs):
-    rows = in_ref.shape[2]
-    step = 64
-    for k, out_ref in enumerate(out_refs):
-        piece = lax.rem(lax.axis_index("y") + k, 2)
-        for start in range(0, rows, step):
-            total = in_ref[0, piece, start : start + step, :].astype(F32)
-            for i in range(1, in_ref.shape[0]):
-                total += in_ref[i, piece, start : start + step, :].astype(F32)
-            out_ref[start : start + step, :] = total.astype(BF16)
-
-
-def totals(received):
-    sources, count, rows, columns = received.shape
-    return pl.pallas_call(
-        total_kernel,
-        out_shape=[jax.ShapeDtypeStruct((rows, columns), BF16)] * count,
+def total_kernel(runs, in_ref, out_ref):
+    sources = in_ref.shape[0] // 2
+    rows = in_ref.shape[1] // (2 * runs)
+    core = lax.axis_index("K")
+    for half in range(2):
+        for slot, held in enumerate((core, 1 - core)):
+            for i in range(runs):
+                lines = slice((slot * runs + i) * rows, (slot * runs + i + 1) * rows)
+                total = in_ref[half * sources, lines, :].astype(F32)
+                for source in range(half * sources + 1, (half + 1) * sources):
+                    total += in_ref[source, lines, :].astype(F32)
+                start = pl.multiple_of(((2 * i + held) * 2 + half) * rows, rows)
+                out_ref[pl.ds(start, rows), :] = total.astype(BF16)
+
+
+def totals(received, runs):
+    sources, rows, columns = received.shape
+    return pl.pallas_call(
+        functools.partial(total_kernel, runs),
+        out_shape=jax.ShapeDtypeStruct((2 * rows, columns), BF16),
         in_specs=[VMEM],
-        out_specs=[VMEM] * count,
+        out_specs=VMEM,
         compiler_params=pltpu.CompilerParams(vmem_limit_bytes=16 << 20),
         cost_estimate=pl.CostEstimate(
-            flops=sources * count * rows * columns, bytes_accessed=2 << 20, transcendentals=0
+            flops=sources * rows * columns, bytes_accessed=2 << 20, transcendentals=0
         ),
         name="totals",
     )(received)
-
-
-def order_kernel(runs, *refs):
-    pieces, out_ref = refs[:-1], refs[-1]
-    rows = pieces[0].shape[0] // (2 * runs)
-    core, big = lax.axis_index("K"), lax.axis_index("Y")
-    for k, ref in enumerate(pieces):
-        half = lax.rem(big + k, 2)
-        for slot, held in enumerate((core, 1 - core)):
-            for i in range(runs):
-                start = pl.multiple_of(((2 * i + held) * 2 + half) * rows, rows)
-                source = (slot * runs + i) * rows
-                out_ref[pl.ds(start, rows), :] = ref[source : source + rows, :]
-
-
-def in_order(runs, pieces):
-    rows, columns = pieces[0].shape
-    return pl.pallas_call(
-        functools.partial(order_kernel, runs),
-        out_shape=jax.ShapeDtypeStruct((2 * rows, columns), BF16),
-        in_specs=[VMEM] * 2,
-        out_specs=VMEM,
-        compiler_params=pltpu.CompilerParams(vmem_limit_bytes=4 << 20),
-        cost_estimate=pl.CostEstimate(
-            flops=1 << 18, bytes_accessed=1 << 19, transcendentals=0
-        ),
-        name="in_order",
-    )(*pieces)
 
 
 def passed_along(value, axis, steps):
@@ -353,19 +328,16 @@
     other = passed_along(own, "K", 1)
     partial = project(own, other, weights)
     partial = partial.reshape(-1, *partial.shape[2:])
-    received = lax.all_to_all(partial, "x", split_axis=0, concat_axis=0, tiled=True)
-    summed = totals(received)
-    placed = []
-    for k in range(2):
-        pairs = []
-        for y in range(2):
-            for x in range(lax.axis_size("x")):
-                for big in range(y_count):
-                    head = (big // 2) * 4 + (big % 2) * 2 + x % 2
-                    target = head * y_count + (x // 2) * 2 + (y + k) % 2
-                    pairs.append(((y * 4 + x) * y_count + big, target))
-        placed.append(lax.ppermute(summed[k], ("y", "x", "Y"), pairs))
-    return in_order(z_count // 2, placed)
+    received = lax.all_to_all(partial, HEADS, split_axis=0, concat_axis=0, tiled=True)
+    summed = totals(received, z_count // 2)
+    pairs = []
+    for y in range(2):
+        for x in range(lax.axis_size("x")):
+            for big in range(y_count):
+                head = (big // 2) * 4 + (big % 2) * 2 + x % 2
+                target = head * y_count + y * 2 + x // 2
+                pairs.append(((y * 4 + x) * y_count + big, target))
+    return lax.ppermute(summed, ("y", "x", "Y"), pairs)
 
 
 def solution(mesh):

time: 144 us -> 142 us (0.986)
  the two profiles are of different devices: /device:TPU:8 before, /device:TPU:90 now
where the time goes in v8:
time: 142 us; the launch traced here: 141 us
  blocking collectives  60.1 us (42%)
  starting transfers between devices  31.1 us (22%)
  waiting for transfers between devices  18.8 us (13%)
  Pallas kernels  16.9 us (12%)
  between operations  13.5 us (10%)
    all_to_all x1, blocking collectives, on_device(): lax.all_to_all(halves, ('y', 'Z'), split_axis=0, concat_axis=0, tiled=True)  40.2 us
    ppermute x5, starting transfers between devices, passed_along(): lax.ppermute(value, axis, [(i, (i + steps) % count) for i in range(count)])  26.3 us
    all_to_all x1, blocking collectives, on_device(): lax.all_to_all(partial, HEADS, split_axis=0, concat_axis=0, tiled=True)  19.9 us
    ppermute x1, waiting for transfers between devices, on_device(): return lax.ppermute(summed, ('y', 'x', 'Y'), pairs)  15.8 us
    pallas_call x2, Pallas kernels, later_part(): pl.pallas_call(functools.partial(kernel, tokens), out_shape=jax.ShapeDtyp...  7.18 us
    pallas_call x1, Pallas kernels, project(): pl.pallas_call(project_kernel, grid=(pieces,), out_shape=pltpu.HBM((piece...  5.48 us
    pallas_call x1, Pallas kernels, first_part(): pl.pallas_call(functools.partial(first_kernel, tokens), out_shape=(jax.Sh...  3.74 us
    ppermute x1, starting transfers between devices, on_device(): return lax.ppermute(summed, ('y', 'x', 'Y'), pairs)  3.5 us
  transfers between devices with their start and end apart: 9, of which 2 were waited for; matrix products, arithmetic and copies ran while one was open for 0% of the time, Pallas kernels for 8%

profile of v8, /device:TPU:90, one launch (start us, length us, event | category | flops | bytes accessed | tf_op | source)
XLA Modules:
  0.0 141.2 jit_solution(18229946125518374686)
XLA Ops:
  6.5 0.0 copy-start
  6.5 0.0 all-gather.3.cloned.1.call-start
  6.5 0.7 all-gather.3.cloned.1.call-update
  7.3 1.9 %collective-permute-start.1 = (bf16[2048,128]{1,0:T(8,128)(2,1)}, bf16[2048,128]{1,0:T(8,128)(2,1)S(1)}, u32[]{:S(2)}, u32[]{:S(2)}) collective-permute-start(bf16[2048,128]{1,0:T(8,128)(2,1)} %bitcast.11), channel_id=1, source_target_pairs={{0,1},{1,0},{2,3},{3,2},{4,5},{5,4},{6,7},{7,6},{8,9},{9,8},{10,11... | collective-permute-start | bytes 1572872 | tf_op jit(solution)/shard_map/ppermute | solution.py:297
  9.2 2.4 %collective-permute-start.2 = (bf16[2048,128]{1,0:T(8,128)(2,1)}, bf16[2048,128]{1,0:T(8,128)(2,1)S(1)}, u32[]{:S(2)}, u32[]{:S(2)}) collective-permute-start(bf16[2048,128]{1,0:T(8,128)(2,1)} %bitcast.13), channel_id=1, source_target_pairs={{0,1},{1,0},{2,3},{3,2},{4,5},{5,4},{6,7},{7,6},{8,9},{9,8},{10,11... | collective-permute-start | bytes 1572872 | tf_op jit(solution)/shard_map/ppermute | solution.py:297
  11.6 4.3 %collective-permute-start = (bf16[512,128]{1,0:T(8,128)(2,1)}, bf16[512,128]{1,0:T(8,128)(2,1)S(1)}, u32[]{:S(2)}, u32[]{:S(2)}) collective-permute-start(bf16[512,128]{1,0:T(8,128)(2,1)} %bitcast.5), channel_id=1, source_target_pairs={{0,2},{1,3},{2,4},{3,5},{4,6},{5,7},{6,8},{7,9},{8,10},{9,11},{10,... | collective-permute-start | bytes 393224 | tf_op jit(solution)/shard_map/ppermute | solution.py:297
  15.9 0.7 collective-permute-start.4
  16.6 3.7 %first_part.1 = (bf16[528,128]{1,0:T(8,128)(2,1)S(1)}, bf16[2048,128]{1,0:T(8,128)(2,1)S(1)}, bf16[2048,128]{1,0:T(8,128)(2,1)S(1)}, s32[8,128]{1,0:T(8,128)S(1)}) custom-call(s32[64]{0:T(128)} %refs_0_.1, s32[64]{0:T(128)} %refs_1_.1, bf16[512,128]{1,0:T(8,128)(2,1)} %bitcast.7, bf16[2048,128]{1,0:T(8,128)(2,1)} %bitcast.12, bf16[2048,128]{1,0:T(8,128)(2,1)} %bitcast.14), custom_call_target="tpu_custom_call" | custom-call | flops 536870912 | bytes 1048576 | tf_op jit(solution)/shard_map/first_part/pallas_call | solution.py:132
  20.3 0.0 collective-permute-done.q_ref
  20.3 0.0 collective-permute-done.1.k_other
  20.3 0.0 collective-permute-done.2.v_other
  20.3 4.7 %shard_map.64 = bf16[528,128]{1,0:T(8,128)(2,1)S(1)} custom-call(s32[8,128]{1,0:T(8,128)S(1)} %get-tuple-element.10.meta_ref, bf16[512,128]{1,0:T(8,128)(2,1)S(1)} %collective-permute-done.q_ref, bf16[2048,128]{1,0:T(8,128)(2,1)S(1)} %get-tuple-element.11.k_ref, bf16[2048,128]{1,0:T(8,128)(2,1)S(1)} %get-tuple-element.12.v_ref, ...), custom_call_target="tpu_custom_call" | custom-call | flops 1073741824 | bytes 2097152 | tf_op jit(solution)/shard_map/pallas_call | solution.py:157
  25.1 12.5 %collective-permute-start.3 = (bf16[528,128]{1,0:T(8,128)(2,1)S(1)}, bf16[528,128]{1,0:T(8,128)(2,1)S(1)}, u32[]{:S(2)}, u32[]{:S(2)}) collective-permute-start(bf16[528,128]{1,0:T(8,128)(2,1)S(1)} %shard_map.64), channel_id=1, source_target_pairs={{0,62},{1,63},{2,0},{3,1},{4,2},{5,3},{6,4},{7,5},{8,6},{9,7},{10,... | collective-permute-start | bytes 405512 | tf_op jit(solution)/shard_map/ppermute | solution.py:297
  37.6 0.0 collective-permute-done.4.q_visit
  37.6 0.0 copy-done
  37.6 2.5 %shard_map.65.refs_2_ = bf16[528,128]{1,0:T(8,128)(2,1)S(1)} custom-call(s32[8,128]{1,0:T(8,128)S(1)} %get-tuple-element.10.meta_ref, bf16[512,128]{1,0:T(8,128)(2,1)S(1)} %bitcast.8, bf16[512,128]{1,0:T(8,128)(2,1)S(1)} %collective-permute-done.4.q_visit, bf16[2048,128]{1,0:T(8,128)(2,1)S(1)} %collective-permute-done.1.k_other, ...), custom_call_target="tpu_custom_call" | custom-call | flops 536870912 | bytes 1048576 | tf_op jit(solution)/shard_map/pallas_call | solution.py:157
  40.1 0.7 collective-permute-start.5
  40.7 0.0 collective-permute-done.3.refs_1_
  40.7 0.0 collective-permute-done.5.refs_3_
  40.8 0.4 combine.1
  41.2 40.2 %all_to_all.10.own_ref = bf16[16,32,1024]{2,1,0:T(8,128)(2,1)S(1)} all-to-all(bf16[16,32,1024]{2,1,0:T(8,128)(2,1)S(1)} %combine.1), channel_id=1, replica_groups=mesh['y'=2,'x'=4,'Y'=4,'Z'=8,'K'=2] {'y','Z'}, dimensions={0} | all-to-all | bytes 2097152 | tf_op jit(solution)/shard_map/all_to_all | solution.py:327
  81.4 5.2 %collective-permute-start.6 = (bf16[16,32,1024]{2,1,0:T(8,128)(2,1)S(1)}, bf16[16,32,1024]{2,1,0:T(8,128)(2,1)S(1)}, u32[]{:S(2)}, u32[]{:S(2)}) collective-permute-start(bf16[16,32,1024]{2,1,0:T(8,128)(2,1)S(1)} %all_to_all.10.own_ref), channel_id=1, source_target_pairs={{0,1},{1,0},{2,3},{3,2},{4,5},{5,4},{6,7},{7,6},{8,9},{9,8},{10,11... | collective-permute-start | bytes 3145736 | tf_op jit(solution)/shard_map/ppermute | solution.py:297
  86.6 2.3 %collective-permute-done.6.other_ref = bf16[16,32,1024]{2,1,0:T(8,128)(2,1)S(1)} collective-permute-done((bf16[16,32,1024]{2,1,0:T(8,128)(2,1)S(1)}, bf16[16,32,1024]{2,1,0:T(8,128)(2,1)S(1)}, u32[]{:S(2)}, u32[]{:S(2)}) %collective-permute-start.6) | collective-permute-done | bytes 1048608 | tf_op jit(solution)/shard_map/ppermute | solution.py:297
  88.8 0.0 all-gather.3.cloned.1.call-done
  88.8 5.5 %project.1 = bf16[4,2,256,256]{3,2,1,0:T(8,128)(2,1)} custom-call(bf16[16,32,1024]{2,1,0:T(8,128)(2,1)S(1)} %all_to_all.10.own_ref, bf16[16,32,1024]{2,1,0:T(8,128)(2,1)S(1)} %collective-permute-done.6.other_ref, bf16[8,1024,256]{2,1,0:T(8,128)(2,1)} %bitcast.10), custom_call_target="tpu_custom_call" | custom-call | flops 2147483648 | bytes 6291456 | tf_op jit(solution)/shard_map/project/pallas_call | solution.py:249
  94.3 19.9 %all_to_all.11.in_ref = bf16[8,256,256]{2,1,0:T(8,128)(2,1)S(1)} all-to-all(bf16[8,256,256]{2,1,0:T(8,128)(2,1)} %bitcast.9), channel_id=1, replica_groups=mesh['y'=2,'x'=4,'Y'=4,'Z'=8,'K'=2] {'y','x'}, dimensions={0} | all-to-all | bytes 2097152 | tf_op jit(solution)/shard_map/all_to_all | solution.py:331
  114.2 0.1 totals.1
  114.4 3.5 %collective-permute-start.7 = (bf16[512,256]{1,0:T(8,128)(2,1)S(1)}, bf16[512,256]{1,0:T(8,128)(2,1)S(1)}, u32[]{:S(2)}, u32[]{:S(2)}) collective-permute-start(bf16[512,256]{1,0:T(8,128)(2,1)S(1)} %totals.1), channel_id=1, source_target_pairs={{0,0},{16,128},{32,256},{48,384},{64,64},{80,192},{96,320},{112,44... | collective-permute-start | bytes 786440 | tf_op jit(solution)/shard_map/ppermute | solution.py:340
  117.9 15.8 %collective-permute-done.7 = bf16[512,256]{1,0:T(8,128)(2,1)S(1)} collective-permute-done((bf16[512,256]{1,0:T(8,128)(2,1)S(1)}, bf16[512,256]{1,0:T(8,128)(2,1)S(1)}, u32[]{:S(2)}, u32[]{:S(2)}) %collective-permute-start.7) | collective-permute-done | bytes 262176 | tf_op jit(solution)/shard_map/ppermute | solution.py:340
  133.6 0.7 copy.8
Async XLA Ops:
  6.5 31.0 %copy-start = (bf16[64,8,128]{2,1,0:T(8,128)(2,1)S(1)}, bf16[64,8,128]{2,1,0:T(8,128)(2,1)}, u32[]{:S(2)}) copy-start(bf16[64,8,128]{2,1,0:T(8,128)(2,1)} %param.6) | copy-start | bytes 393220
  6.5 82.3 %all-gather.3.cloned.1.call-start = ((), (), s32[]{:S(2)}) async-start(), calls=%async_computation.2 | async-start | bytes 4718592 | tf_op jit(solution)/shard_map/all_gather | solution.py:311
  7.3 13.1 %collective-permute-start.1 = (bf16[2048,128]{1,0:T(8,128)(2,1)}, bf16[2048,128]{1,0:T(8,128)(2,1)S(1)}, u32[]{:S(2)}, u32[]{:S(2)}) collective-permute-start(bf16[2048,128]{1,0:T(8,128)(2,1)} %bitcast.11), channel_id=1, source_target_pairs={{0,1},{1,0},{2,3},{3,2},{4,5},{5,4},{6,7},{7,6},{8,9},{9,8},{10,11... | collective-permute-start | bytes 1572872 | tf_op jit(solution)/shard_map/ppermute | solution.py:297
  9.2 11.2 %collective-permute-start.2 = (bf16[2048,128]{1,0:T(8,128)(2,1)}, bf16[2048,128]{1,0:T(8,128)(2,1)S(1)}, u32[]{:S(2)}, u32[]{:S(2)}) collective-permute-start(bf16[2048,128]{1,0:T(8,128)(2,1)} %bitcast.13), channel_id=1, source_target_pairs={{0,1},{1,0},{2,3},{3,2},{4,5},{5,4},{6,7},{7,6},{8,9},{9,8},{10,11... | collective-permute-start | bytes 1572872 | tf_op jit(solution)/shard_map/ppermute | solution.py:297
  11.6 8.7 %collective-permute-start = (bf16[512,128]{1,0:T(8,128)(2,1)}, bf16[512,128]{1,0:T(8,128)(2,1)S(1)}, u32[]{:S(2)}, u32[]{:S(2)}) collective-permute-start(bf16[512,128]{1,0:T(8,128)(2,1)} %bitcast.5), channel_id=1, source_target_pairs={{0,2},{1,3},{2,4},{3,5},{4,6},{5,7},{6,8},{7,9},{8,10},{9,11},{10,... | collective-permute-start | bytes 393224 | tf_op jit(solution)/shard_map/ppermute | solution.py:297
  15.9 21.7 %collective-permute-start.4 = (bf16[512,128]{1,0:T(8,128)(2,1)}, bf16[512,128]{1,0:T(8,128)(2,1)S(1)}, u32[]{:S(2)}, u32[]{:S(2)}) collective-permute-start(bf16[512,128]{1,0:T(8,128)(2,1)} %bitcast.6), channel_id=1, source_target_pairs={{1,5},{3,7},{5,9},{7,11},{9,13},{11,15},{13,17},{15,19},{17,21},{1... | collective-permute-start | bytes 393224 | tf_op jit(solution)/shard_map/ppermute | solution.py:308
  25.1 15.7 %collective-permute-start.3 = (bf16[528,128]{1,0:T(8,128)(2,1)S(1)}, bf16[528,128]{1,0:T(8,128)(2,1)S(1)}, u32[]{:S(2)}, u32[]{:S(2)}) collective-permute-start(bf16[528,128]{1,0:T(8,128)(2,1)S(1)} %shard_map.64), channel_id=1, source_target_pairs={{0,62},{1,63},{2,0},{3,1},{4,2},{5,3},{6,4},{7,5},{8,6},{9,7},{10,... | collective-permute-start | bytes 405512 | tf_op jit(solution)/shard_map/ppermute | solution.py:297
  40.1 0.7 collective-permute-start.5
  81.4 7.4 %collective-permute-start.6 = (bf16[16,32,1024]{2,1,0:T(8,128)(2,1)S(1)}, bf16[16,32,1024]{2,1,0:T(8,128)(2,1)S(1)}, u32[]{:S(2)}, u32[]{:S(2)}) collective-permute-start(bf16[16,32,1024]{2,1,0:T(8,128)(2,1)S(1)} %all_to_all.10.own_ref), channel_id=1, source_target_pairs={{0,1},{1,0},{2,3},{3,2},{4,5},{5,4},{6,7},{7,6},{8,9},{9,8},{10,11... | collective-permute-start | bytes 3145736 | tf_op jit(solution)/shard_map/ppermute | solution.py:297
  114.4 19.3 %collective-permute-start.7 = (bf16[512,256]{1,0:T(8,128)(2,1)S(1)}, bf16[512,256]{1,0:T(8,128)(2,1)S(1)}, u32[]{:S(2)}, u32[]{:S(2)}) collective-permute-start(bf16[512,256]{1,0:T(8,128)(2,1)S(1)} %totals.1), channel_id=1, source_target_pairs={{0,0},{16,128},{32,256},{48,384},{64,64},{80,192},{96,320},{112,44... | collective-permute-start | bytes 786440 | tf_op jit(solution)/shard_map/ppermute | solution.py:340
Sparse Core Ops, SparseCore 0:
  9.4 70.0 all-gather.2
